TPU v7x, 256 devices: a whole 4x4x8 slice. The times are simulated.
256 devices in a mesh: gx: 16 (over z, core), gy: 4 (over x), gz: 4 (over y).
Axes of the slice: x: 4, y: 4, z: 8, core: 2. Of those that a mesh axis runs over, the one named last changes fastest.
Arguments:
- edge_state: bfloat16 [524288, 512], P(('gx', 'gy', 'gz')), may hold values from -6 to 6
- angle_weight: float32 [524288, 32], P(('gx', 'gy', 'gz')), may hold values from -6 to 6
- angle_bins: int32 [524288, 32], P(('gx', 'gy', 'gz')), may hold values from 0 to 15
- send_slots: int32 [16, 4, 4, 27, 32], P('gx', 'gy', 'gz'), may hold values from -1 to 2047, as said below
- fetch_index: int32 [524288], P(('gx', 'gy', 'gz')), may hold values from -1 to 2911, as said below
- down_weight: bfloat16 [2, 512, 64], replicated, may hold values from -0.25 to 0.25
- bilinear: bfloat16 [2, 1024, 64], replicated, may hold values from -0.1875 to 0.1875
- up_weight: bfloat16 [2, 64, 512], replicated, may hold values from -0.75 to 0.75
- first_dense: bfloat16 [2, 512, 512], replicated, may hold values from -0.25 to 0.25
- second_dense: bfloat16 [2, 512, 512], replicated, may hold values from -0.25 to 0.25
Outputs:
- edge_out: bfloat16 [524288, 512], P(('gx', 'gy', 'gz'))
Inputs may be any that keep to these rules, and one draw needn't show every extreme that they name: `send_slots`: direction t = 9a + 3b + c stands for the neighbouring brick at offset (a - 1, b - 1, c - 1), periodic. Row t of a brick lists, in its first slots, local edges whose reverses lie in the brick at direction t; the rest hold -1; row 13 holds only -1. Every edge is listed at most once. Some direction of every brick is full. `fetch_index`: -1 marks an empty neighbour slot. A value below 2048 is the local edge that is the reverse; 2048 + t * 32 + r says that the reverse is listed in slot r of row 26 - t of send_slots of the brick at direction t, and that this brick's own edge is listed in slot r of row t of its own send_slots. Reverses are mutual, live edges have live reverses, and rev of an edge is another edge.
All inputs are finite; a program needn't handle non-finite values.
Results may differ from a plain program's by a relative error of at most 0.014.
Values may be sent and summed in bfloat16 or wider, within the bound.
No kernel may reach another device: no remote copies, remote signals or barrier semaphores. Data moves between devices by JAX's collectives and lax.ppermute only.
A program may use at most 128 MiB of HBM per device.

v0:
```python
import jax
import jax.numpy as jnp
from jax import lax
from jax.experimental import pallas as pl
from jax.experimental.pallas import tpu as pltpu
from jax.sharding import PartitionSpec as P

HALF_ROOT = 0.7071067811865476
F32 = jnp.float32
BF16 = jnp.bfloat16
VMEM_LIMIT = 56 * 1024 * 1024


def silu(x):
    half = 0.5 * x
    return half + half * jnp.tanh(half)


def dot(a, b):
    return jnp.dot(a, b, preferred_element_type=F32)


def dot_t(a, b):
    return lax.dot_general(a, b, (((1,), (1,)), ((), ())), preferred_element_type=F32)


def from_behind(array, axis, by):
    length = lax.axis_size(axis)
    return lax.ppermute(array, axis, [(i, (i + by) % length) for i in range(length)])


def exchange(buffer):
    for dim, axis in ((0, "gx"), (1, "gy"), (2, "gz")):
        from_low = from_behind(lax.slice_in_dim(buffer, 2, 3, axis=dim), axis, 1)
        from_high = from_behind(lax.slice_in_dim(buffer, 0, 1, axis=dim), axis, -1)
        middle = lax.slice_in_dim(buffer, 1, 2, axis=dim)
        buffer = jnp.concatenate([from_low, middle, from_high], axis=dim)
    return buffer


def residual(rows, lifted, first, second):
    mixed = ((rows.astype(F32) + lifted) * HALF_ROOT).astype(BF16)
    inner = silu(dot(mixed, first)).astype(BF16)
    return (mixed.astype(F32) + silu(dot(inner, second))) * HALF_ROOT


def spread_rows(rows_ref, wide_ref):
    count = rows_ref.shape[0]
    step = 256
    for start in range(0, count, step):
        for c in range(4):
            wide_ref[pl.ds(4 * start + c, step, stride=4), :] = rows_ref[
                start : start + step, 128 * c : 128 * (c + 1)
            ].astype(F32)


def move_rows(count, unroll, step):
    def body(i, carry):
        base = i * unroll
        for k in range(unroll):
            step(base + k)
        return carry

    lax.fori_loop(0, count // unroll, body, 0)


def pack_kernel(send_ref, rows_ref, out_ref, wide_ref, packed_ref):
    slots = send_ref.shape[0]
    spread_rows(rows_ref, wide_ref)

    def step(s):
        source = pl.multiple_of(send_ref[s] * 4, 4)
        target = pl.multiple_of(s * 4, 4)
        packed_ref[pl.ds(target, 4), :] = wide_ref[pl.ds(source, 4), :]

    move_rows(slots, 16, step)
    out_ref[...] = packed_ref[...].astype(BF16)


def local_kernel(fetch_ref, rows_ref, out_ref, wide_ref):
    count = rows_ref.shape[0]
    quarter = count // 4
    spread_rows(rows_ref, wide_ref)

    def atom(i, carry):
        target = (i % 4) * quarter + (i // 4) * 32
        for k in range(32):
            source = pl.multiple_of(fetch_ref[i * 32 + k] * 4, 4)
            out_ref[pl.ds(pl.multiple_of((target + k) * 4, 4), 4), :] = wide_ref[
                pl.ds(source, 4), :
            ]
        return carry

    lax.fori_loop(0, count // 32, atom, 0)


def blocks_kernel(
    target_ref,
    arrived_ref,
    reverse_ref,
    weight_ref,
    bins_ref,
    down_ref,
    mixer_ref,
    up_ref,
    first_ref,
    second_ref,
    trip_ref,
    send_ref,
    arrived32_ref,
    rows_ref,
    wide_ref,
    summed_ref,
    packed_ref,
):
    slots = target_ref.shape[0]
    count = rows_ref.shape[0]
    quarter = count // 4
    groups = quarter // 32
    trip = up_ref.shape[1]
    angular = summed_ref.shape[1] // 256
    arrived32_ref[...] = arrived_ref[...].astype(F32)

    def place(s):
        target = pl.multiple_of(target_ref[s] * 4, 4)
        reverse_ref[pl.ds(target, 4), :] = arrived32_ref[
            pl.ds(pl.multiple_of(s * 4, 4), 4), :
        ]

    move_rows(slots, 16, place)
    for start in range(0, count, 256):
        for c in range(4):
            rows_ref[start : start + 256, 128 * c : 128 * (c + 1)] = reverse_ref[
                pl.ds(4 * start + c, 256, stride=4), :
            ].astype(BF16)
    trip_ref[count : count + 8, :] = jnp.zeros((8, 128), F32)
    lane_block = lax.broadcasted_iota(jnp.int32, (quarter, 4 * trip), 1) // trip
    for block in range(2):
        down = down_ref[block]
        down = jnp.concatenate([down, down, down, down], axis=0)
        for a in range(4):
            projected = silu(dot_t(rows_ref[a * quarter : (a + 1) * quarter, :], down))
            projected = jnp.where(lane_block == a, projected, 0.0).astype(BF16)
            for g in range(groups):
                wide_ref[g, 32 * a : 32 * (a + 1), :] = projected[32 * g : 32 * (g + 1), :]

        def group(g, carry):
            start = pl.multiple_of(g * 32, 32)
            weight = weight_ref[pl.ds(start, 32), :]
            bins = bins_ref[pl.ds(start, 32), :]
            chosen = [jnp.where(bins == b, weight, 0.0).astype(BF16) for b in range(angular)]
            sums = dot(jnp.concatenate(chosen, axis=0), wide_ref[g]).astype(BF16)
            for b in range(angular):
                summed_ref[pl.ds(start, 32), 256 * b : 256 * (b + 1)] = sums[
                    32 * b : 32 * (b + 1), :
                ]
            return carry

        lax.fori_loop(0, groups, group, 0)
        triplet = dot(summed_ref[...], mixer_ref[block]).astype(BF16)
        for a in range(4):
            part = triplet[:, trip * a : trip * (a + 1)]
            trip_ref[a * quarter : (a + 1) * quarter, trip * block : trip * (block + 1)] = (
                part.astype(F32)
            )
            if block == 0:
                lifted = silu(dot(part, up_ref[0])).astype(BF16).astype(F32)
                rows = rows_ref[a * quarter : (a + 1) * quarter, :]
                rows_ref[a * quarter : (a + 1) * quarter, :] = residual(
                    rows, lifted, first_ref[0], second_ref[0]
                ).astype(BF16)

    def pick(s):
        packed_ref[pl.ds(s, 1), :] = trip_ref[pl.ds(target_ref[s], 1), :]

    move_rows(slots, 16, pick)
    send_ref[...] = packed_ref[...].astype(BF16)


def trip_kernel(fetch_ref, trip_ref, out_ref):
    count = fetch_ref.shape[0]

    def step(e):
        out_ref[pl.ds(e, 1), :] = trip_ref[pl.ds(fetch_ref[e], 1), :]

    move_rows(count, 16, step)


def final_kernel(
    send_ref,
    arrived_ref,
    trip_ref,
    rows_ref,
    live_ref,
    up_ref,
    first_ref,
    second_ref,
    out_ref,
    arrived32_ref,
):
    slots = send_ref.shape[0]
    count = rows_ref.shape[0]
    trip = up_ref.shape[1]
    arrived32_ref[...] = arrived_ref[...].astype(F32)

    def place(s):
        trip_ref[pl.ds(send_ref[s], 1), :] = arrived32_ref[pl.ds(s, 1), :]

    move_rows(slots, 16, place)
    step = 256
    for start in range(0, count, step):
        rows = rows_ref[start : start + step, :]
        both = trip_ref[start : start + step, :].astype(BF16)
        for block in range(2):
            part = both[:, trip * block : trip * (block + 1)]
            lifted = silu(dot(part, up_ref[block])).astype(BF16).astype(F32)
            updated = residual(rows, lifted, first_ref[block], second_ref[block])
            rows = updated.astype(BF16)
        out_ref[start : start + step, :] = jnp.where(
            live_ref[start : start + step, :] > 0.0, updated, 0.0
        ).astype(BF16)


def prepare_kernel(
    weight_ref, bins_ref, live_ref, bilinear_ref, weight_out_ref, bins_out_ref, mixer_ref
):
    neigh = weight_ref.shape[0]
    groups = weight_ref.shape[1] // (4 * neigh)
    trip = bilinear_ref.shape[1]
    angular = bilinear_ref.shape[2] // trip
    row = lax.broadcasted_iota(jnp.int32, (neigh, 4 * neigh), 0)
    lane = lax.broadcasted_iota(jnp.int32, (neigh, 4 * neigh), 1)
    distinct = row != lane % neigh

    def turn(block):
        return jnp.concatenate(
            [block[:, neigh * a : neigh * (a + 1)].T for a in range(4)], axis=1
        )

    for g in range(groups):
        lanes = slice(4 * neigh * g, 4 * neigh * (g + 1))
        rows = slice(neigh * g, neigh * (g + 1))
        weight_out_ref[rows, :] = turn(weight_ref[:, lanes])
        kept = distinct & (live_ref[g : g + 1, :] >= 0)
        bins_out_ref[rows, :] = jnp.where(kept, turn(bins_ref[:, lanes]), -1)
    lane_block = lax.broadcasted_iota(jnp.int32, (trip, 4 * trip), 1) // trip
    for block in range(2):
        for b in range(angular):
            part = bilinear_ref[block, :, trip * b : trip * (b + 1)].astype(F32).T
            wide = jnp.concatenate([part] * 4, axis=1)
            for a in range(4):
                start = 4 * trip * b + trip * a
                mixer_ref[block, start : start + trip, :] = jnp.where(
                    lane_block == a, wide, 0.0
                ).astype(BF16)


def local(
    edge_state,
    angle_weight,
    angle_bins,
    send_slots,
    fetch_index,
    down_weight,
    bilinear,
    up_weight,
    first_dense,
    second_dense,
):
    count, width = edge_state.shape
    neigh = angle_weight.shape[1]
    trip = down_weight.shape[2]
    angular = bilinear.shape[1] // trip
    slots = 27 * send_slots.shape[-1]
    quarter = count // 4
    groups = count // (4 * neigh)
    spare = count + 8

    def turned(edges):
        return (edges // neigh % 4) * quarter + edges // (4 * neigh) * neigh + edges % neigh

    senders = send_slots.reshape(slots)
    send_rows = jnp.maximum(senders, 0)
    own_target = jnp.where(senders >= 0, senders, count)
    turned_target = jnp.where(senders >= 0, turned(send_rows), count)
    live = fetch_index >= 0
    is_local = live & (fetch_index < count)
    fetch_rows = jnp.where(is_local, fetch_index, 0)
    turned_fetch = jnp.where(is_local, turned(fetch_rows), count)
    live_column = live.astype(F32).reshape(count, 1)

    down_turned = jnp.swapaxes(down_weight, 1, 2)

    smem = pl.BlockSpec(memory_space=pltpu.SMEM)
    vmem = pl.BlockSpec(memory_space=pltpu.VMEM)
    params = pltpu.CompilerParams(vmem_limit_bytes=VMEM_LIMIT)

    packed = pl.pallas_call(
        pack_kernel,
        out_shape=jax.ShapeDtypeStruct((slots * 4, 128), BF16),
        in_specs=[smem, vmem],
        out_specs=vmem,
        scratch_shapes=[pltpu.VMEM((count * 4, 128), F32), pltpu.VMEM((slots * 4, 128), F32)],
        compiler_params=params,
        name="pack",
    )(send_rows, edge_state)
    weights, bins, mixer = pl.pallas_call(
        prepare_kernel,
        out_shape=(
            jax.ShapeDtypeStruct((quarter, 4 * neigh), F32),
            jax.ShapeDtypeStruct((quarter, 4 * neigh), jnp.int32),
            jax.ShapeDtypeStruct((2, angular * 4 * trip, 4 * trip), BF16),
        ),
        in_specs=[vmem] * 4,
        out_specs=(vmem, vmem, vmem),
        compiler_params=params,
        name="prepare",
    )(
        angle_weight.T,
        angle_bins.T,
        fetch_index.reshape(groups, 4 * neigh),
        jnp.swapaxes(bilinear, 1, 2),
    )
    arrived = exchange(packed.reshape(3, 3, 3, -1, 128)).reshape(slots * 4, 128)

    reverse = pl.pallas_call(
        local_kernel,
        out_shape=jax.ShapeDtypeStruct((spare * 4, 128), F32),
        in_specs=[smem, vmem],
        out_specs=vmem,
        scratch_shapes=[pltpu.VMEM((count * 4, 128), F32)],
        compiler_params=params,
        name="reverse_local",
    )(fetch_rows, edge_state)

    triplet, sending = pl.pallas_call(
        blocks_kernel,
        out_shape=(
            jax.ShapeDtypeStruct((spare, 2 * trip), F32),
            jax.ShapeDtypeStruct((slots, 2 * trip), BF16),
        ),
        in_specs=[smem] + [vmem] * 9,
        out_specs=(vmem, vmem),
        scratch_shapes=[
            pltpu.VMEM((slots * 4, 128), F32),
            pltpu.VMEM((count, width), BF16),
            pltpu.VMEM((groups, 4 * neigh, 4 * trip), BF16),
            pltpu.VMEM((quarter, angular * 4 * trip), BF16),
            pltpu.VMEM((slots, 2 * trip), F32),
        ],
        compiler_params=params,
        name="blocks",
    )(
        turned_target,
        arrived,
        reverse,
        weights,
        bins,
        down_turned,
        mixer,
        up_weight,
        first_dense,
        second_dense,
    )
    carried = exchange(sending.reshape(3, 3, 3, -1, 128)).reshape(slots, 2 * trip)

    own_trip = pl.pallas_call(
        trip_kernel,
        out_shape=jax.ShapeDtypeStruct((spare, 2 * trip), F32),
        in_specs=[smem, vmem],
        out_specs=vmem,
        compiler_params=params,
        name="trip_local",
    )(turned_fetch, triplet)

    out = pl.pallas_call(
        final_kernel,
        out_shape=jax.ShapeDtypeStruct((count, width), BF16),
        in_specs=[smem] + [vmem] * 7,
        out_specs=vmem,
        scratch_shapes=[pltpu.VMEM((slots, 2 * trip), F32)],
        compiler_params=params,
        name="final",
    )(
        own_target,
        carried,
        own_trip,
        edge_state,
        live_column,
        up_weight,
        first_dense,
        second_dense,
    )
    return out


def solution(mesh):
    spread = P(("gx", "gy", "gz"), None)
    in_specs = (
        spread,
        spread,
        spread,
        P("gx", "gy", "gz", None, None),
        P(("gx", "gy", "gz")),
        P(),
        P(),
        P(),
        P(),
        P(),
    )
    return jax.shard_map(local, mesh=mesh, in_specs=in_specs, out_specs=spread, check_vma=False)
```

profile of v0, /device:TPU:24, one launch (start us, length us, event | category | flops | bytes accessed | tf_op | source)
XLA Modules:
  0.0 117.2 jit_solution(14227455998697701954)
XLA Ops:
  0.0 0.8 reduce
  0.8 0.6 broadcast_maximum_fusion
  1.4 4.3 %pack.1 = bf16[3456,128]{1,0:T(8,128)(2,1)} custom-call(s32[864]{0:T(1024)} %get-tuple-element.35.send_ref, bf16[2048,512]{1,0:T(8,128)(2,1)} %rows_ref.5), custom_call_target="tpu_custom_call" | custom-call | tf_op jit(solution)/shard_map/pack/pallas_call | solution.py:298
  5.7 1.2 %fusion.21 = (bf16[1152,128]{1,0:T(8,128)(2,1)S(1)}, bf16[1152,128]{1,0:T(8,128)(2,1)S(1)}, bf16[1152,128]{1,0:T(8,128)(2,1)S(1)}) fusion(bf16[3456,128]{1,0:T(8,128)(2,1)} %pack.1), kind=kLoop, calls=%fused_computation.53 | loop fusion | bytes 1769472 | tf_op jit(solution)/shard_map/slice | solution.py:34
  6.9 5.3 %collective-permute-start.1 = (bf16[1,3,3,128,128]{4,3,2,1,0:T(8,128)(2,1)S(1)}, bf16[1,3,3,128,128]{4,3,2,1,0:T(8,128)(2,1)S(1)}, u32[]{:S(2)}, u32[]{:S(2)}) collective-permute-start(bf16[1,3,3,128,128]{4,3,2,1,0:T(8,128)(2,1)S(1)} %bitcast.18), channel_id=1, source_target_pairs={{0,240},{16,0},{32,16},{48,32},{64,48},{80,64},{96,80},{112,96},{1... | collective-permute-start | bytes 884744 | tf_op jit(solution)/shard_map/ppermute | solution.py:29
  12.2 4.2 %collective-permute-done.1 = bf16[1,3,3,128,128]{4,3,2,1,0:T(8,128)(2,1)S(1)} collective-permute-done((bf16[1,3,3,128,128]{4,3,2,1,0:T(8,128)(2,1)S(1)}, bf16[1,3,3,128,128]{4,3,2,1,0:T(8,128)(2,1)S(1)}, u32[]{:S(2)}, u32[]{:S(2)}) %collective-permute-start.1) | collective-permute-done | bytes 294944 | tf_op jit(solution)/shard_map/ppermute | solution.py:29
  16.5 3.1 %collective-permute-done = bf16[1,3,3,128,128]{4,3,2,1,0:T(8,128)(2,1)S(1)} collective-permute-done((bf16[1,3,3,128,128]{4,3,2,1,0:T(8,128)(2,1)S(1)}, bf16[1,3,3,128,128]{4,3,2,1,0:T(8,128)(2,1)S(1)}, u32[]{:S(2)}, u32[]{:S(2)}) %collective-permute-start) | collective-permute-done | bytes 294944 | tf_op jit(solution)/shard_map/ppermute | solution.py:29
  19.6 0.1 pad_maximum_fusion
  19.8 2.8 %collective-permute-start.3 = (bf16[3,1,3,128,128]{4,3,2,1,0:T(8,128)(2,1)S(1)}, bf16[3,1,3,128,128]{4,3,2,1,0:T(8,128)(2,1)S(1)}, u32[]{:S(2)}, u32[]{:S(2)}) collective-permute-start(bf16[3,1,3,128,128]{4,3,2,1,0:T(8,128)(2,1)S(1)} %get-tuple-element.19), channel_id=1, source_target_pairs={{0,12},{4,0},{8,4},{12,8},{1,13},{5,1},{9,5},{13,9},{2,14},{6,2},{... | collective-permute-start | bytes 884744 | tf_op jit(solution)/shard_map/ppermute | solution.py:29
  22.6 4.2 %collective-permute-done.3 = bf16[3,1,3,128,128]{4,3,2,1,0:T(8,128)(2,1)S(1)} collective-permute-done((bf16[3,1,3,128,128]{4,3,2,1,0:T(8,128)(2,1)S(1)}, bf16[3,1,3,128,128]{4,3,2,1,0:T(8,128)(2,1)S(1)}, u32[]{:S(2)}, u32[]{:S(2)}) %collective-permute-start.3) | collective-permute-done | bytes 294944 | tf_op jit(solution)/shard_map/ppermute | solution.py:29
  26.9 3.7 %collective-permute-done.2 = bf16[3,1,3,128,128]{4,3,2,1,0:T(8,128)(2,1)S(1)} collective-permute-done((bf16[3,1,3,128,128]{4,3,2,1,0:T(8,128)(2,1)S(1)}, bf16[3,1,3,128,128]{4,3,2,1,0:T(8,128)(2,1)S(1)}, u32[]{:S(2)}, u32[]{:S(2)}) %collective-permute-start.2) | collective-permute-done | bytes 294944 | tf_op jit(solution)/shard_map/ppermute | solution.py:29
  30.6 0.1 pad_maximum_fusion.1
  30.7 0.8 collective-permute-start.5
  31.5 2.5 %collective-permute-start.4 = (bf16[3,3,1,128,128]{4,3,2,1,0:T(8,128)(2,1)S(1)}, bf16[3,3,1,128,128]{4,3,2,1,0:T(8,128)(2,1)S(1)}, u32[]{:S(2)}, u32[]{:S(2)}) collective-permute-start(bf16[3,3,1,128,128]{4,3,2,1,0:T(8,128)(2,1)S(1)} %get-tuple-element.15), channel_id=1, source_target_pairs={{0,1},{1,2},{2,3},{3,0},{4,5},{5,6},{6,7},{7,4},{8,9},{9,10},{10,1... | collective-permute-start | bytes 884744 | tf_op jit(solution)/shard_map/ppermute | solution.py:29
  34.0 0.6 fusion.4
  34.7 6.9 %reverse_local.1.reverse_ref = f32[8224,128]{1,0:T(8,128)} custom-call(s32[2048]{0:T(1024)} %get-tuple-element.34.fetch_ref, bf16[2048,512]{1,0:T(8,128)(2,1)} %rows_ref.5), custom_call_target="tpu_custom_call" | custom-call | tf_op jit(solution)/shard_map/reverse_local/pallas_call | solution.py:326
  41.6 10.8 %prepare.1 = (f32[512,128]{1,0:T(8,128)}, s32[512,128]{1,0:T(8,128)}, bf16[2,4096,256]{2,1,0:T(8,128)(2,1)}) custom-call(f32[32,2048]{1,0:T(8,128)} %bitcast.20, s32[32,2048]{1,0:T(8,128)} %bitcast.21, s32[16,128]{1,0:T(8,128)} %bitcast.24, bf16[2,64,1024]{2,1,0:T(8,128)(2,1)} %bitcast.22), custom_call_target="tpu_custom_call" | custom-call | tf_op jit(solution)/shard_map/prepare/pallas_call | solution.py:307
  52.4 1.1 pad_maximum_fusion.2
  53.5 24.3 %blocks.1 = (f32[2056,128]{1,0:T(8,128)}, bf16[864,128]{1,0:T(8,128)(2,1)}) custom-call(s32[864]{0:T(1024)} %get-tuple-element.37.target_ref, bf16[3456,128]{1,0:T(8,128)(2,1)} %bitcast.14, f32[8224,128]{1,0:T(8,128)} %reverse_local.1.reverse_ref, f32[512,128]{1,0:T(8,128)} %get-tuple-element.10.weight_ref, s32[512,128]{1,0:T(8,128)} %get-tuple-element.11.bins_ref, ...), custom_call_target="tpu_custom_call" | custom-call | tf_op jit(solution)/shard_map/blocks/pallas_call | solution.py:336
  77.8 1.0 fusion.24
  78.7 1.0 collective-permute-start.7
  79.7 2.0 %collective-permute-done.7 = bf16[1,3,3,32,128]{4,3,2,1,0:T(8,128)(2,1)S(1)} collective-permute-done((bf16[1,3,3,32,128]{4,3,2,1,0:T(8,128)(2,1)S(1)}, bf16[1,3,3,32,128]{4,3,2,1,0:T(8,128)(2,1)S(1)}, u32[]{:S(2)}, u32[]{:S(2)}) %collective-permute-start.7) | collective-permute-done | bytes 73760 | tf_op jit(solution)/shard_map/ppermute | solution.py:29
  81.7 3.0 %collective-permute-done.6 = bf16[1,3,3,32,128]{4,3,2,1,0:T(8,128)(2,1)S(1)} collective-permute-done((bf16[1,3,3,32,128]{4,3,2,1,0:T(8,128)(2,1)S(1)}, bf16[1,3,3,32,128]{4,3,2,1,0:T(8,128)(2,1)S(1)}, u32[]{:S(2)}, u32[]{:S(2)}) %collective-permute-start.6) | collective-permute-done | bytes 73760 | tf_op jit(solution)/shard_map/ppermute | solution.py:29
  84.8 0.6 collective-permute-start.9
  85.4 1.5 %collective-permute-start.8 = (bf16[3,1,3,32,128]{4,3,2,1,0:T(8,128)(2,1)S(1)}, bf16[3,1,3,32,128]{4,3,2,1,0:T(8,128)(2,1)S(1)}, u32[]{:S(2)}, u32[]{:S(2)}) collective-permute-start(bf16[3,1,3,32,128]{4,3,2,1,0:T(8,128)(2,1)S(1)} %get-tuple-element.27), channel_id=1, source_target_pairs={{0,4},{4,8},{8,12},{12,0},{1,5},{5,9},{9,13},{13,1},{2,6},{6,10},{... | collective-permute-start | bytes 221192 | tf_op jit(solution)/shard_map/ppermute | solution.py:29
  86.9 2.3 %collective-permute-done.9 = bf16[3,1,3,32,128]{4,3,2,1,0:T(8,128)(2,1)S(1)} collective-permute-done((bf16[3,1,3,32,128]{4,3,2,1,0:T(8,128)(2,1)S(1)}, bf16[3,1,3,32,128]{4,3,2,1,0:T(8,128)(2,1)S(1)}, u32[]{:S(2)}, u32[]{:S(2)}) %collective-permute-start.9) | collective-permute-done | bytes 73760 | tf_op jit(solution)/shard_map/ppermute | solution.py:29
  89.2 1.8 %collective-permute-done.8 = bf16[3,1,3,32,128]{4,3,2,1,0:T(8,128)(2,1)S(1)} collective-permute-done((bf16[3,1,3,32,128]{4,3,2,1,0:T(8,128)(2,1)S(1)}, bf16[3,1,3,32,128]{4,3,2,1,0:T(8,128)(2,1)S(1)}, u32[]{:S(2)}, u32[]{:S(2)}) %collective-permute-start.8) | collective-permute-done | bytes 73760 | tf_op jit(solution)/shard_map/ppermute | solution.py:29
  91.1 3.2 %collective-permute-start.10 = (bf16[3,3,1,32,128]{4,3,2,1,0:T(8,128)(2,1)S(1)}, bf16[3,3,1,32,128]{4,3,2,1,0:T(8,128)(2,1)S(1)}, u32[]{:S(2)}, u32[]{:S(2)}) collective-permute-start(bf16[3,3,1,32,128]{4,3,2,1,0:T(8,128)(2,1)S(1)} %get-tuple-element.24), channel_id=1, source_target_pairs={{0,1},{1,2},{2,3},{3,0},{4,5},{5,6},{6,7},{7,4},{8,9},{9,10},{10,1... | collective-permute-start | bytes 221192 | tf_op jit(solution)/shard_map/ppermute | solution.py:29
  94.3 1.3 %copy.11.live_ref = f32[2048,1]{1,0:T(8,128)} copy(f32[2048,1]{0,1:T(1,128)S(1)} %bitcast.27) | data formatting | bytes 16384 | tf_op jit(solution)/shard_map/reshape | solution.py:290
  95.7 4.4 %trip_local.1.trip_ref = f32[2056,128]{1,0:T(8,128)} custom-call(s32[2048]{0:T(1024)} %get-tuple-element.33.fetch_ref, f32[2056,128]{1,0:T(8,128)} %get-tuple-element.14.trip_ref), custom_call_target="tpu_custom_call" | custom-call | tf_op jit(solution)/shard_map/trip_local/pallas_call | solution.py:367
  100.1 0.7 pad_maximum_fusion.5
  100.8 16.4 %final.1 = bf16[2048,512]{1,0:T(8,128)(2,1)} custom-call(s32[864]{0:T(1024)} %get-tuple-element.36.send_ref, bf16[864,128]{1,0:T(8,128)(2,1)} %bitcast.16, f32[2056,128]{1,0:T(8,128)} %trip_local.1.trip_ref, bf16[2048,512]{1,0:T(8,128)(2,1)} %rows_ref.5, f32[2048,1]{1,0:T(8,128)} %copy.11.live_ref, bf16[2,64,512]{2,1,0:T(8,128)(2,1)} %up_ref.3, ...), custom_call_target="tpu_custom_call" | custom-call | tf_op jit(solution)/shard_map/final/pallas_call | solution.py:376
  (20 shorter events, 0.4 us)
Async XLA Ops:
  6.9 9.6 %collective-permute-start.1 = (bf16[1,3,3,128,128]{4,3,2,1,0:T(8,128)(2,1)S(1)}, bf16[1,3,3,128,128]{4,3,2,1,0:T(8,128)(2,1)S(1)}, u32[]{:S(2)}, u32[]{:S(2)}) collective-permute-start(bf16[1,3,3,128,128]{4,3,2,1,0:T(8,128)(2,1)S(1)} %bitcast.18), channel_id=1, source_target_pairs={{0,240},{16,0},{32,16},{48,32},{64,48},{80,64},{96,80},{112,96},{1... | collective-permute-start | bytes 884744 | tf_op jit(solution)/shard_map/ppermute | solution.py:29
  12.2 7.4 %collective-permute-start = (bf16[1,3,3,128,128]{4,3,2,1,0:T(8,128)(2,1)S(1)}, bf16[1,3,3,128,128]{4,3,2,1,0:T(8,128)(2,1)S(1)}, u32[]{:S(2)}, u32[]{:S(2)}) collective-permute-start(bf16[1,3,3,128,128]{4,3,2,1,0:T(8,128)(2,1)S(1)} %bitcast.17), channel_id=1, source_target_pairs={{0,16},{16,32},{32,48},{48,64},{64,80},{80,96},{96,112},{112,128},... | collective-permute-start | bytes 884744 | tf_op jit(solution)/shard_map/ppermute | solution.py:29
  19.8 14.3 %copy-start = (s32[2048]{0:T(1024)S(1)}, s32[2048]{0:T(1024)}, u32[]{:S(2)}) copy-start(s32[2048]{0:T(1024)} %param.14) | copy-start | bytes 24580
  19.8 7.1 %collective-permute-start.3 = (bf16[3,1,3,128,128]{4,3,2,1,0:T(8,128)(2,1)S(1)}, bf16[3,1,3,128,128]{4,3,2,1,0:T(8,128)(2,1)S(1)}, u32[]{:S(2)}, u32[]{:S(2)}) collective-permute-start(bf16[3,1,3,128,128]{4,3,2,1,0:T(8,128)(2,1)S(1)} %get-tuple-element.19), channel_id=1, source_target_pairs={{0,12},{4,0},{8,4},{12,8},{1,13},{5,1},{9,5},{13,9},{2,14},{6,2},{... | collective-permute-start | bytes 884744 | tf_op jit(solution)/shard_map/ppermute | solution.py:29
  22.6 7.9 %collective-permute-start.2 = (bf16[3,1,3,128,128]{4,3,2,1,0:T(8,128)(2,1)S(1)}, bf16[3,1,3,128,128]{4,3,2,1,0:T(8,128)(2,1)S(1)}, u32[]{:S(2)}, u32[]{:S(2)}) collective-permute-start(bf16[3,1,3,128,128]{4,3,2,1,0:T(8,128)(2,1)S(1)} %get-tuple-element.18), channel_id=1, source_target_pairs={{0,4},{4,8},{8,12},{12,0},{1,5},{5,9},{9,13},{13,1},{2,6},{6,10},{... | collective-permute-start | bytes 884744 | tf_op jit(solution)/shard_map/ppermute | solution.py:29
  30.7 21.7 %collective-permute-start.5 = (bf16[3,3,1,128,128]{4,3,2,1,0:T(8,128)(2,1)S(1)}, bf16[3,3,1,128,128]{4,3,2,1,0:T(8,128)(2,1)S(1)}, u32[]{:S(2)}, u32[]{:S(2)}) collective-permute-start(bf16[3,3,1,128,128]{4,3,2,1,0:T(8,128)(2,1)S(1)} %get-tuple-element.16), channel_id=1, source_target_pairs={{0,3},{1,0},{2,1},{3,2},{4,7},{5,4},{6,5},{7,6},{8,11},{9,8},{10,9... | collective-permute-start | bytes 884744 | tf_op jit(solution)/shard_map/ppermute | solution.py:29
  31.5 20.8 %collective-permute-start.4 = (bf16[3,3,1,128,128]{4,3,2,1,0:T(8,128)(2,1)S(1)}, bf16[3,3,1,128,128]{4,3,2,1,0:T(8,128)(2,1)S(1)}, u32[]{:S(2)}, u32[]{:S(2)}) collective-permute-start(bf16[3,3,1,128,128]{4,3,2,1,0:T(8,128)(2,1)S(1)} %get-tuple-element.15), channel_id=1, source_target_pairs={{0,1},{1,2},{2,3},{3,0},{4,5},{5,6},{6,7},{7,4},{8,9},{9,10},{10,1... | collective-permute-start | bytes 884744 | tf_op jit(solution)/shard_map/ppermute | solution.py:29
  77.8 16.6 %copy-start.1 = (s32[2048]{0:T(1024)S(1)}, s32[2048]{0:T(1024)}, u32[]{:S(2)}) copy-start(s32[2048]{0:T(1024)} %param.14) | copy-start | bytes 24580
  78.7 2.9 %collective-permute-start.7 = (bf16[1,3,3,32,128]{4,3,2,1,0:T(8,128)(2,1)S(1)}, bf16[1,3,3,32,128]{4,3,2,1,0:T(8,128)(2,1)S(1)}, u32[]{:S(2)}, u32[]{:S(2)}) collective-permute-start(bf16[1,3,3,32,128]{4,3,2,1,0:T(8,128)(2,1)S(1)} %bitcast.26), channel_id=1, source_target_pairs={{0,240},{16,0},{32,16},{48,32},{64,48},{80,64},{96,80},{112,96},{1... | collective-permute-start | bytes 221192 | tf_op jit(solution)/shard_map/ppermute | solution.py:29
  79.7 5.0 %collective-permute-start.6 = (bf16[1,3,3,32,128]{4,3,2,1,0:T(8,128)(2,1)S(1)}, bf16[1,3,3,32,128]{4,3,2,1,0:T(8,128)(2,1)S(1)}, u32[]{:S(2)}, u32[]{:S(2)}) collective-permute-start(bf16[1,3,3,32,128]{4,3,2,1,0:T(8,128)(2,1)S(1)} %bitcast.25), channel_id=1, source_target_pairs={{0,16},{16,32},{32,48},{48,64},{64,80},{80,96},{96,112},{112,128},... | collective-permute-start | bytes 221192 | tf_op jit(solution)/shard_map/ppermute | solution.py:29
  84.8 4.4 %collective-permute-start.9 = (bf16[3,1,3,32,128]{4,3,2,1,0:T(8,128)(2,1)S(1)}, bf16[3,1,3,32,128]{4,3,2,1,0:T(8,128)(2,1)S(1)}, u32[]{:S(2)}, u32[]{:S(2)}) collective-permute-start(bf16[3,1,3,32,128]{4,3,2,1,0:T(8,128)(2,1)S(1)} %get-tuple-element.28), channel_id=1, source_target_pairs={{0,12},{4,0},{8,4},{12,8},{1,13},{5,1},{9,5},{13,9},{2,14},{6,2},{... | collective-permute-start | bytes 221192 | tf_op jit(solution)/shard_map/ppermute | solution.py:29
  85.4 5.6 %collective-permute-start.8 = (bf16[3,1,3,32,128]{4,3,2,1,0:T(8,128)(2,1)S(1)}, bf16[3,1,3,32,128]{4,3,2,1,0:T(8,128)(2,1)S(1)}, u32[]{:S(2)}, u32[]{:S(2)}) collective-permute-start(bf16[3,1,3,32,128]{4,3,2,1,0:T(8,128)(2,1)S(1)} %get-tuple-element.27), channel_id=1, source_target_pairs={{0,4},{4,8},{8,12},{12,0},{1,5},{5,9},{9,13},{13,1},{2,6},{6,10},{... | collective-permute-start | bytes 221192 | tf_op jit(solution)/shard_map/ppermute | solution.py:29
  91.0 9.1 %collective-permute-start.11 = (bf16[3,3,1,32,128]{4,3,2,1,0:T(8,128)(2,1)S(1)}, bf16[3,3,1,32,128]{4,3,2,1,0:T(8,128)(2,1)S(1)}, u32[]{:S(2)}, u32[]{:S(2)}) collective-permute-start(bf16[3,3,1,32,128]{4,3,2,1,0:T(8,128)(2,1)S(1)} %get-tuple-element.25), channel_id=1, source_target_pairs={{0,3},{1,0},{2,1},{3,2},{4,7},{5,4},{6,5},{7,6},{8,11},{9,8},{10,9... | collective-permute-start | bytes 221192 | tf_op jit(solution)/shard_map/ppermute | solution.py:29
  91.1 9.0 %collective-permute-start.10 = (bf16[3,3,1,32,128]{4,3,2,1,0:T(8,128)(2,1)S(1)}, bf16[3,3,1,32,128]{4,3,2,1,0:T(8,128)(2,1)S(1)}, u32[]{:S(2)}, u32[]{:S(2)}) collective-permute-start(bf16[3,3,1,32,128]{4,3,2,1,0:T(8,128)(2,1)S(1)} %get-tuple-element.24), channel_id=1, source_target_pairs={{0,1},{1,2},{2,3},{3,0},{4,5},{5,6},{6,7},{7,4},{8,9},{9,10},{10,1... | collective-permute-start | bytes 221192 | tf_op jit(solution)/shard_map/ppermute | solution.py:29
where the time goes:
time: 118 us; the launch traced here: 117 us
  Pallas kernels  67.1 us (57%)
  waiting for transfers between devices  24.4 us (21%)
  starting transfers between devices  17.8 us (15%)
  other arithmetic  4.04 us (3%)
  local copies, waits for them, and re-layouts  3.77 us (3%)
    ppermute x12, waiting for transfers between devices, from_behind(): lax.ppermute(array, axis, [(i, (i + by) % length) for i in range(length)])  24.4 us
    pallas_call x1, Pallas kernels, local(): pl.pallas_call(blocks_kernel, out_shape=(jax.ShapeDtypeStruct((spare, 2 *...  24.3 us
    ppermute x12, starting transfers between devices, from_behind(): lax.ppermute(array, axis, [(i, (i + by) % length) for i in range(length)])  17.8 us
    pallas_call x1, Pallas kernels, local(): pl.pallas_call(final_kernel, out_shape=jax.ShapeDtypeStruct((count, width...  16.4 us
    pallas_call x1, Pallas kernels, local(): pl.pallas_call(prepare_kernel, out_shape=(jax.ShapeDtypeStruct((quarter,...  10.8 us
    pallas_call x1, Pallas kernels, local(): pl.pallas_call(local_kernel, out_shape=jax.ShapeDtypeStruct((spare * 4, 1...  6.94 us
    pallas_call x1, Pallas kernels, local(): pl.pallas_call(trip_kernel, out_shape=jax.ShapeDtypeStruct((spare, 2 * tr...  4.44 us
    pallas_call x1, Pallas kernels, local(): pl.pallas_call(pack_kernel, out_shape=jax.ShapeDtypeStruct((slots * 4, 12...  4.29 us
  transfers between devices with their start and end apart: 12, of which 8 were waited for; matrix products, arithmetic and copies ran while one was open for 2% of the time, Pallas kernels for 19%

commit v1 on v0

v1 whole, which is shorter than its diff:
```python
import jax
import jax.numpy as jnp
from jax import lax
from jax.experimental import pallas as pl
from jax.experimental.pallas import tpu as pltpu
from jax.sharding import PartitionSpec as P


HALF_ROOT = 0.7071067811865476
F32 = jnp.float32
BF16 = jnp.bfloat16
MIB = 1024 * 1024


def silu_of_half(half):
    return half + half * jnp.tanh(half)


def dot(a, b):
    return jnp.dot(a, b, preferred_element_type=F32)


def dot_t(a, b):
    return lax.dot_general(a, b, (((1,), (1,)), ((), ())), preferred_element_type=F32)


def from_behind(array, axis, by):
    length = lax.axis_size(axis)
    return lax.ppermute(array, axis, [(i, (i + by) % length) for i in range(length)])


def second_kernel(low_ref, middle_ref, high_ref, *out_refs):
    third = low_ref.shape[0] // 3
    for a, slab_ref in enumerate((low_ref, middle_ref, high_ref)):
        for b, out_ref in enumerate(out_refs):
            out_ref[third * a : third * (a + 1), :] = slab_ref[third * b : third * (b + 1), :]


def third_kernel(low_ref, middle_ref, high_ref, *out_refs):
    rows = low_ref.shape[0] // 9
    for b, slab_ref in enumerate((low_ref, middle_ref, high_ref)):
        for a in range(3):
            for c, out_ref in enumerate(out_refs):
                source, target = rows * (3 * a + c), rows * (3 * b + a)
                out_ref[target : target + rows, :] = slab_ref[source : source + rows, :]


def exchange(slabs):
    vmem = pl.BlockSpec(memory_space=pltpu.VMEM)

    def regroup(kernel, pieces):
        return pl.pallas_call(
            kernel,
            out_shape=[jax.ShapeDtypeStruct(piece.shape, piece.dtype) for piece in pieces],
            in_specs=[vmem] * 3,
            out_specs=[vmem] * 3,
            compiler_params=pltpu.CompilerParams(vmem_limit_bytes=4 * MIB),
            name="regroup",
        )(*pieces)

    def hop(sent, axis):
        low, middle, high = sent
        return [from_behind(high, axis, 1), middle, from_behind(low, axis, -1)]

    slabs = hop(slabs, "gx")
    slabs = hop(regroup(second_kernel, slabs), "gy")
    return hop(regroup(third_kernel, slabs), "gz")


def pipelined(blocks, stages):
    for step in range(blocks + len(stages) - 1):
        for depth in reversed(range(len(stages))):
            if 0 <= step - depth < blocks:
                stages[depth](step - depth)


def spread_rows(rows_ref, wide_ref, start, count):
    for c in range(4):
        wide_ref[pl.ds(4 * start + c, count, stride=4), :] = rows_ref[
            start : start + count, 128 * c : 128 * (c + 1)
        ].astype(F32)


def move_rows(count, unroll, step):
    def body(i, carry):
        base = i * unroll
        for k in range(unroll):
            step(base + k)
        return carry

    lax.fori_loop(0, count // unroll, body, 0)


def pack_kernel(
    send_hbm_ref,
    rows_hbm_ref,
    low_ref,
    middle_ref,
    high_ref,
    send_ref,
    rows_ref,
    wide_ref,
    packed_ref,
    copied,
    listed,
):
    count = rows_ref.shape[0]
    directions, _, each = send_ref.shape
    chunk = count // 8
    copies = [
        pltpu.make_async_copy(
            rows_hbm_ref.at[pl.ds(chunk * i, chunk), :],
            rows_ref.at[pl.ds(chunk * i, chunk), :],
            copied.at[i],
        )
        for i in range(8)
    ]
    slots = pltpu.make_async_copy(send_hbm_ref, send_ref, listed)
    slots.start()
    for copy in copies:
        copy.start()
    for i, copy in enumerate(copies):
        copy.wait()
        spread_rows(rows_ref, wide_ref, chunk * i, chunk)
    slots.wait()

    def direction(t, carry):
        for r in range(each):
            source = pl.multiple_of(jnp.maximum(send_ref[t, 0, r], 0) * 4, 4)
            target = pl.multiple_of(t * (4 * each) + 4 * r, 4)
            packed_ref[pl.ds(target, 4), :] = wide_ref[pl.ds(source, 4), :]
        return carry

    lax.fori_loop(0, directions, direction, 0)
    slab = 9 * 4 * each
    for i, out_ref in enumerate((low_ref, middle_ref, high_ref)):
        out_ref[...] = packed_ref[slab * i : slab * (i + 1), :].astype(BF16)


def local_kernel(fetch_ref, rows_ref, out_ref, wide_ref):
    count = rows_ref.shape[0]
    quarter = count // 4
    for start in range(0, count, 256):
        spread_rows(rows_ref, wide_ref, start, 256)

    def atom(i, carry):
        target = (i % 4) * quarter + (i // 4) * 32
        for k in range(32):
            source = pl.multiple_of(fetch_ref[i * 32 + k] * 4, 4)
            out_ref[pl.ds(pl.multiple_of((target + k) * 4, 4), 4), :] = wide_ref[
                pl.ds(source, 4), :
            ]
        return carry

    lax.fori_loop(0, count // 32, atom, 0)


def widen_arrived(pieces, wide_ref):
    for c, piece in enumerate(pieces):
        rows = piece.shape[0] // 9
        for i in range(9):
            start = rows * (9 * (i % 3) + 3 * (i // 3) + c)
            wide_ref[start : start + rows, :] = piece[rows * i : rows * (i + 1), :].astype(F32)


def blocks_kernel(
    target_ref,
    low_ref,
    middle_ref,
    high_ref,
    reverse_ref,
    weight_ref,
    bins_ref,
    down_ref,
    mixer_ref,
    up_ref,
    first_ref,
    second_ref,
    trip_ref,
    send_low_ref,
    send_middle_ref,
    send_high_ref,
    arrived32_ref,
    rows_ref,
    wide_ref,
    summed_ref,
    packed_ref,
    mixed_ref,
    inner_ref,
):
    slots = target_ref.shape[0]
    count = rows_ref.shape[0]
    quarter = count // 4
    groups = quarter // 32
    trip = up_ref.shape[1]
    angular = summed_ref.shape[1] // 256
    widen_arrived((low_ref, middle_ref, high_ref), arrived32_ref)

    def place(s):
        target = pl.multiple_of(target_ref[s] * 4, 4)
        reverse_ref[pl.ds(target, 4), :] = arrived32_ref[pl.ds(pl.multiple_of(s * 4, 4), 4), :]

    move_rows(slots, 16, place)
    for start in range(0, count, 256):
        for c in range(4):
            rows_ref[start : start + 256, 128 * c : 128 * (c + 1)] = reverse_ref[
                pl.ds(4 * start + c, 256, stride=4), :
            ].astype(BF16)
    trip_ref[count : count + 8, :] = jnp.zeros((8, 128), F32)
    lane_block = lax.broadcasted_iota(jnp.int32, (256, 4 * trip), 1) // trip
    step = 256
    for block in range(2):
        down = down_ref[block]
        down = jnp.concatenate([down, down, down, down], axis=0)

        def project(i):
            start = step * i
            a = start // quarter
            half = dot_t(rows_ref[start : start + step, :], down)
            projected = jnp.where(lane_block == a, silu_of_half(half), 0.0).astype(BF16)
            for k in range(step // 32):
                g = (start % quarter) // 32 + k
                wide_ref[g, 32 * a : 32 * (a + 1), :] = projected[32 * k : 32 * (k + 1), :]

        if block == 0:
            for i in range(count // step):
                project(i)

        def group(g, carry):
            start = pl.multiple_of(g * 32, 32)
            weight = weight_ref[pl.ds(start, 32), :]
            bins = bins_ref[pl.ds(start, 32), :]
            zero = jnp.zeros_like(weight)
            chosen = [jnp.where(bins == b, weight, zero) for b in range(angular)]
            sums = dot(jnp.concatenate(chosen, axis=0), wide_ref[g]).astype(BF16)
            for b in range(angular):
                summed_ref[pl.ds(start, 32), 256 * b : 256 * (b + 1)] = sums[
                    32 * b : 32 * (b + 1), :
                ]
            return carry

        lax.fori_loop(0, groups, group, 0, unroll=4)
        triplet = dot(summed_ref[...], mixer_ref[block]).astype(BF16)
        for a in range(4):
            part = triplet[:, trip * a : trip * (a + 1)]
            trip_ref[a * quarter : (a + 1) * quarter, trip * block : trip * (block + 1)] = (
                part.astype(F32)
            )
        if block == 0:

            def lift(i):
                start = step * i
                a, low = start // quarter, start % quarter
                lifted = silu_of_half(
                    dot(triplet[low : low + step, trip * a : trip * (a + 1)], up_ref[0])
                )
                rows = rows_ref[start : start + step, :].astype(F32)
                mixed_ref[start : start + step, :] = ((rows + lifted) * HALF_ROOT).astype(BF16)

            def first(i):
                at = slice(step * i, step * (i + 1))
                inner_ref[at, :] = silu_of_half(dot(mixed_ref[at, :], first_ref[0])).astype(BF16)

            def second(i):
                at = slice(step * i, step * (i + 1))
                change = silu_of_half(dot(inner_ref[at, :], second_ref[0]))
                rows_ref[at, :] = ((mixed_ref[at, :].astype(F32) + change) * HALF_ROOT).astype(
                    BF16
                )

            next_down = jnp.concatenate([down_ref[1]] * 4, axis=0)

            def project_next(i):
                start = step * i
                a = start // quarter
                half = dot_t(rows_ref[start : start + step, :], next_down)
                projected = jnp.where(lane_block == a, silu_of_half(half), 0.0).astype(BF16)
                for k in range(step // 32):
                    g = (start % quarter) // 32 + k
                    wide_ref[g, 32 * a : 32 * (a + 1), :] = projected[32 * k : 32 * (k + 1), :]

            pipelined(count // step, (lift, first, second, project_next))

    def pick(s):
        packed_ref[pl.ds(s, 1), :] = trip_ref[pl.ds(target_ref[s], 1), :]

    move_rows(slots, 16, pick)
    slab = slots // 3
    for i, send_ref in enumerate((send_low_ref, send_middle_ref, send_high_ref)):
        send_ref[...] = packed_ref[slab * i : slab * (i + 1), :].astype(BF16)


def trip_kernel(fetch_ref, trip_ref, out_ref):
    count = fetch_ref.shape[0]

    def step(e):
        out_ref[pl.ds(e, 1), :] = trip_ref[pl.ds(fetch_ref[e], 1), :]

    move_rows(count, 16, step)


def final_kernel(
    send_ref,
    low_ref,
    middle_ref,
    high_ref,
    trip_ref,
    rows_ref,
    live_ref,
    up_ref,
    first_ref,
    second_ref,
    out_ref,
    arrived32_ref,
    mixed_ref,
    inner_ref,
    mixed_next_ref,
    inner_next_ref,
    rows_out_ref,
    mask_ref,
    copied,
):
    slots = send_ref.shape[0]
    count = rows_ref.shape[0]
    trip = up_ref.shape[1]
    widen_arrived((low_ref, middle_ref, high_ref), arrived32_ref)

    def place(s):
        trip_ref[pl.ds(send_ref[s], 1), :] = arrived32_ref[pl.ds(s, 1), :]

    move_rows(slots, 16, place)
    step = 256

    def lifted(at, block):
        both = trip_ref[at, :].astype(BF16)
        return silu_of_half(dot(both[:, trip * block : trip * (block + 1)], up_ref[block]))

    def lift(i):
        at = slice(step * i, step * (i + 1))
        for g in range(step * i // 128, step * (i + 1) // 128):
            line = live_ref[g : g + 1, :].astype(F32)
            mask_ref[128 * g : 128 * (g + 1), :] = jnp.broadcast_to(line, (128, 128)).T
        rows = rows_ref[at, :].astype(F32)
        mixed_ref[at, :] = ((rows + lifted(at, 0)) * HALF_ROOT).astype(BF16)

    def first(i):
        at = slice(step * i, step * (i + 1))
        inner_ref[at, :] = silu_of_half(dot(mixed_ref[at, :], first_ref[0])).astype(BF16)

    def second(i):
        at = slice(step * i, step * (i + 1))
        change = silu_of_half(dot(inner_ref[at, :], second_ref[0]))
        rows = (mixed_ref[at, :].astype(F32) + change) * HALF_ROOT
        mixed_next_ref[at, :] = ((rows + lifted(at, 1)) * HALF_ROOT).astype(BF16)

    def first_next(i):
        at = slice(step * i, step * (i + 1))
        inner_next_ref[at, :] = silu_of_half(dot(mixed_next_ref[at, :], first_ref[1])).astype(BF16)

    def second_next(i):
        at = slice(step * i, step * (i + 1))
        change = silu_of_half(dot(inner_next_ref[at, :], second_ref[1]))
        rows = (mixed_next_ref[at, :].astype(F32) + change) * HALF_ROOT
        for c in range(4):
            lanes = slice(128 * c, 128 * (c + 1))
            rows_out_ref[at, lanes] = jnp.where(mask_ref[at, :] >= 0.0, rows[:, lanes], 0.0).astype(
                BF16
            )
        copies[i].start()

    copies = [
        pltpu.make_async_copy(
            rows_out_ref.at[pl.ds(step * i, step), :],
            out_ref.at[pl.ds(step * i, step), :],
            copied.at[i],
        )
        for i in range(count // step)
    ]
    pipelined(count // step, (lift, first, second, first_next, second_next))
    for copy in copies:
        copy.wait()


def prepare_kernel(
    weight_ref,
    bins_ref,
    live_ref,
    bilinear_ref,
    up_ref,
    first_ref,
    second_ref,
    down_ref,
    weight_out_ref,
    bins_out_ref,
    mixer_ref,
    up_out_ref,
    first_out_ref,
    second_out_ref,
    down_out_ref,
):
    neigh = weight_ref.shape[0]
    side = 4 * neigh
    groups = weight_ref.shape[1] // side
    trip = bilinear_ref.shape[1]
    angular = bilinear_ref.shape[2] // trip
    row = lax.broadcasted_iota(jnp.int32, (side, side), 0)
    lane = lax.broadcasted_iota(jnp.int32, (side, side), 1)
    distinct = row % neigh != lane % neigh
    piece = lax.broadcasted_iota(jnp.int32, (neigh, side), 1) // neigh

    def turn(blocks):
        stacked = []
        for a in range(4):
            rows = jnp.zeros((neigh, side), F32)
            for h in range(4):
                shift = (h - a) * neigh % side
                moved = pltpu.roll(blocks[h], shift, 1) if shift else blocks[h]
                rows = jnp.where(piece == h, moved, rows)
            stacked.append(rows)
        return jnp.concatenate(stacked, axis=0).T

    for start in range(0, groups, 4):
        spans = [slice(side * (start + h), side * (start + h + 1)) for h in range(4)]
        rows = slice(neigh * start, neigh * start + side)
        weight_out_ref[rows, :] = turn([weight_ref[:, span] for span in spans]).astype(BF16)
        live = jnp.concatenate(
            [
                jnp.broadcast_to(live_ref[start + h : start + h + 1, :], (neigh, side))
                for h in range(4)
            ],
            axis=0,
        )
        bins = turn([bins_ref[:, span].astype(F32) for span in spans])
        bins_out_ref[rows, :] = jnp.where(distinct & (live >= 0), bins, -1.0).astype(BF16)
    lane_block = lax.broadcasted_iota(jnp.int32, (trip, 4 * trip), 1) // trip
    for block in range(2):
        turned = bilinear_ref[block].astype(F32).T
        wide = jnp.concatenate([turned] * 4, axis=1)
        for b in range(angular):
            part = wide[trip * b : trip * (b + 1), :]
            for a in range(4):
                start = 4 * trip * b + trip * a
                mixer_ref[block, start : start + trip, :] = jnp.where(
                    lane_block == a, part, 0.0
                ).astype(BF16)
    for source, target in (
        (up_ref, up_out_ref),
        (first_ref, first_out_ref),
        (second_ref, second_out_ref),
        (down_ref, down_out_ref),
    ):
        target[...] = (source[...].astype(F32) * 0.5).astype(BF16)


def local(
    edge_state,
    angle_weight,
    angle_bins,
    send_slots,
    fetch_index,
    down_weight,
    bilinear,
    up_weight,
    first_dense,
    second_dense,
):
    count, width = edge_state.shape
    neigh = angle_weight.shape[1]
    trip = down_weight.shape[2]
    angular = bilinear.shape[1] // trip
    slots = 27 * send_slots.shape[-1]
    quarter = count // 4
    groups = count // (4 * neigh)
    spare = count + 8

    def turned(edges):
        return (edges // neigh % 4) * quarter + edges // (4 * neigh) * neigh + edges % neigh

    senders = send_slots.reshape(slots)
    send_rows = jnp.maximum(senders, 0)
    own_target = jnp.where(senders >= 0, senders, count)
    turned_target = jnp.where(senders >= 0, turned(send_rows), count)
    live = fetch_index >= 0
    is_local = live & (fetch_index < count)
    fetch_rows = jnp.where(is_local, fetch_index, 0)
    turned_fetch = jnp.where(is_local, turned(fetch_rows), count)
    live_lines = fetch_index.reshape(groups, 4 * neigh)

    down_turned = jnp.swapaxes(down_weight, 1, 2)

    smem = pl.BlockSpec(memory_space=pltpu.SMEM)
    vmem = pl.BlockSpec(memory_space=pltpu.VMEM)

    def params(mib):
        return pltpu.CompilerParams(vmem_limit_bytes=mib * MIB)

    outside = pl.BlockSpec(memory_space=pltpu.HBM)
    slab = slots // 3
    each = send_slots.shape[-1]
    packed = pl.pallas_call(
        pack_kernel,
        out_shape=(jax.ShapeDtypeStruct((slab * 4, 128), BF16),) * 3,
        in_specs=[outside, outside],
        out_specs=(vmem,) * 3,
        scratch_shapes=[
            pltpu.SMEM((27, 1, each), jnp.int32),
            pltpu.VMEM((count, width), BF16),
            pltpu.VMEM((count * 4, 128), F32),
            pltpu.VMEM((slots * 4, 128), F32),
            pltpu.SemaphoreType.DMA((8,)),
            pltpu.SemaphoreType.DMA,
        ],
        compiler_params=params(14),
        name="pack",
    )(send_slots.reshape(27, 1, each), edge_state)
    weights, bins, mixer, up_half, first_half, second_half, down_half = pl.pallas_call(
        prepare_kernel,
        out_shape=(
            jax.ShapeDtypeStruct((quarter, 4 * neigh), BF16),
            jax.ShapeDtypeStruct((quarter, 4 * neigh), BF16),
            jax.ShapeDtypeStruct((2, angular * 4 * trip, 4 * trip), BF16),
            jax.ShapeDtypeStruct(up_weight.shape, BF16),
            jax.ShapeDtypeStruct(first_dense.shape, BF16),
            jax.ShapeDtypeStruct(second_dense.shape, BF16),
            jax.ShapeDtypeStruct(down_turned.shape, BF16),
        ),
        in_specs=[vmem] * 8,
        out_specs=(vmem,) * 7,
        compiler_params=params(16),
        name="prepare",
    )(
        angle_weight.T,
        angle_bins.T,
        live_lines,
        jnp.swapaxes(bilinear, 1, 2),
        up_weight,
        first_dense,
        second_dense,
        down_turned,
    )
    arrived = exchange(packed)

    reverse = pl.pallas_call(
        local_kernel,
        out_shape=jax.ShapeDtypeStruct((spare * 4, 128), F32),
        in_specs=[smem, vmem],
        out_specs=vmem,
        scratch_shapes=[pltpu.VMEM((count * 4, 128), F32)],
        compiler_params=params(14),
        name="reverse_local",
    )(fetch_rows, edge_state)

    triplet, *sending = pl.pallas_call(
        blocks_kernel,
        out_shape=(
            jax.ShapeDtypeStruct((spare, 2 * trip), F32),
        )
        + (jax.ShapeDtypeStruct((slab, 2 * trip), BF16),) * 3,
        in_specs=[smem] + [vmem] * 11,
        out_specs=(vmem,) * 4,
        scratch_shapes=[
            pltpu.VMEM((slots * 4, 128), F32),
            pltpu.VMEM((count, width), BF16),
            pltpu.VMEM((groups, 4 * neigh, 4 * trip), BF16),
            pltpu.VMEM((quarter, angular * 4 * trip), BF16),
            pltpu.VMEM((slots, 2 * trip), F32),
            pltpu.VMEM((count, width), BF16),
            pltpu.VMEM((count, width), BF16),
        ],
        compiler_params=params(32),
        name="blocks",
    )(
        turned_target,
        *arrived,
        reverse,
        weights,
        bins,
        down_half,
        mixer,
        up_half,
        first_half,
        second_half,
    )
    own_trip = pl.pallas_call(
        trip_kernel,
        out_shape=jax.ShapeDtypeStruct((spare, 2 * trip), F32),
        in_specs=[smem, vmem],
        out_specs=vmem,
        compiler_params=params(5),
        name="trip_local",
    )(turned_fetch, triplet)
    carried = exchange(sending)

    out = pl.pallas_call(
        final_kernel,
        out_shape=jax.ShapeDtypeStruct((count, width), BF16),
        in_specs=[smem] + [vmem] * 9,
        out_specs=outside,
        scratch_shapes=[pltpu.VMEM((slots, 2 * trip), F32)]
        + [pltpu.VMEM((count, width), BF16)] * 5
        + [pltpu.VMEM((count, 128), F32)]
        + [pltpu.SemaphoreType.DMA((8,))],
        compiler_params=params(24),
        name="final",
    )(
        own_target,
        *carried,
        own_trip,
        edge_state,
        live_lines,
        up_half,
        first_half,
        second_half,
    )
    return out


def solution(mesh):
    spread = P(("gx", "gy", "gz"), None)
    in_specs = (
        spread,
        spread,
        spread,
        P("gx", "gy", "gz", None, None),
        P(("gx", "gy", "gz")),
        P(),
        P(),
        P(),
        P(),
        P(),
    )

    return jax.shard_map(local, mesh=mesh, in_specs=in_specs, out_specs=spread, check_vma=False)
```

time: 118 us -> 77.8 us (0.66)
  Pallas kernels: 67.1 us -> 36.9 us
  waiting for transfers between devices: 24.4 us -> 16.1 us
  other arithmetic: 4.04 us -> 0.08 us
  starting transfers between devices: 17.8 us -> 21.1 us
  local copies, waits for them, and re-layouts: 3.77 us -> 2.42 us
    pallas_call x1, Pallas kernels: 10.8 us -> 1.88 us  [local(): pl.pallas_call(prepare_kernel, out_shape=(jax.ShapeDtypeStruct((quarter,...]
    pallas_call x1, Pallas kernels: 24.3 us -> 15.5 us  [local(): pl.pallas_call(blocks_kernel, out_shape=(jax.ShapeDtypeStruct((spare, 2 *...]
    ppermute x12, waiting for transfers between devices: 24.4 us -> 16.1 us  [from_behind(): lax.ppermute(array, axis, [(i, (i + by) % length) for i in range(length)])]
    pallas_call x1, Pallas kernels: 16.4 us -> 9.42 us  [local(): pl.pallas_call(final_kernel, out_shape=jax.ShapeDtypeStruct((count, width...]
    ppermute x12, starting transfers between devices: 17.8 us -> 21.1 us  [from_behind(): lax.ppermute(array, axis, [(i, (i + by) % length) for i in range(length)])]
    pallas_call x1, Pallas kernels: 6.94 us -> 4.04 us  [local(): pl.pallas_call(local_kernel, out_shape=jax.ShapeDtypeStruct((spare * 4, 1...]
    unnamed x4 -> x24, local copies, waits for them, and re-layouts: 0.01 us -> 2.35 us
    slice x6 -> x0, local copies, waits for them, and re-layouts: 2.34 us -> none  [exchange(): from_low = from_behind(lax.slice_in_dim(buffer, 2, 3, axis=dim), axis, 1)]
  transfers between devices with their start and end apart: 12 -> 12, of which waited for: 8 -> 6; matrix products, arithmetic and copies ran while one was open for 2% -> 0% of each run, Pallas kernels for 19% -> 11%
where the time goes in v1:
time: 77.8 us; the launch traced here: 77.1 us
  Pallas kernels  36.9 us (47%)
  starting transfers between devices  21.1 us (27%)
  waiting for transfers between devices  16.1 us (21%)
  local copies, waits for them, and re-layouts  2.42 us (3%)
    ppermute x12, starting transfers between devices, from_behind(): lax.ppermute(array, axis, [(i, (i + by) % length) for i in range(length)])  21.1 us
    ppermute x12, waiting for transfers between devices, from_behind(): lax.ppermute(array, axis, [(i, (i + by) % length) for i in range(length)])  16.1 us
    pallas_call x1, Pallas kernels, local(): pl.pallas_call(blocks_kernel, out_shape=(jax.ShapeDtypeStruct((spare, 2 *...  15.5 us
    pallas_call x1, Pallas kernels, local(): pl.pallas_call(final_kernel, out_shape=jax.ShapeDtypeStruct((count, width...  9.42 us
    pallas_call x1, Pallas kernels, local(): pl.pallas_call(local_kernel, out_shape=jax.ShapeDtypeStruct((spare * 4, 1...  4.04 us
    pallas_call x1, Pallas kernels, local(): pl.pallas_call(trip_kernel, out_shape=jax.ShapeDtypeStruct((spare, 2 * tr...  2.82 us
    pallas_call x1, Pallas kernels, local(): pl.pallas_call(pack_kernel, out_shape=(jax.ShapeDtypeStruct((slab * 4, 12...  2.43 us
    unnamed x24, local copies, waits for them, and re-layouts  2.35 us
  transfers between devices with their start and end apart: 12, of which 6 were waited for; matrix products, arithmetic and copies ran while one was open for 0% of the time, Pallas kernels for 11%

profile of v1, /device:TPU:24, one launch (start us, length us, event | category | flops | bytes accessed | tf_op | source)
XLA Modules:
  0.0 77.1 jit_solution(6161728356001329348)
XLA Ops:
  0.0 1.6 %copy-done = bf16[2048,512]{1,0:T(8,128)(2,1)S(1)} copy-done((bf16[2048,512]{1,0:T(8,128)(2,1)S(1)}, bf16[2048,512]{1,0:T(8,128)(2,1)}, u32[]{:S(2)}) %copy-start) | copy-done | bytes 2097176
  1.6 0.7 copy-done.10
  2.3 2.4 %pack.1 = (bf16[1152,128]{1,0:T(8,128)(2,1)S(1)}, bf16[1152,128]{1,0:T(8,128)(2,1)S(1)}, bf16[1152,128]{1,0:T(8,128)(2,1)S(1)}) custom-call(s32[27,1,32]{2,1,0:T(1,128)S(1)} %bitcast.12, bf16[2048,512]{1,0:T(8,128)(2,1)S(1)} %copy-done), custom_call_target="tpu_custom_call" | custom-call | tf_op jit(solution)/shard_map/pack/pallas_call | solution.py:500
  4.8 0.0 collective-permute-start
  4.8 5.3 %collective-permute-start.1 = (bf16[1152,128]{1,0:T(8,128)(2,1)S(1)}, bf16[1152,128]{1,0:T(8,128)(2,1)S(1)}, u32[]{:S(2)}, u32[]{:S(2)}) collective-permute-start(bf16[1152,128]{1,0:T(8,128)(2,1)S(1)} %get-tuple-element.33), channel_id=1, source_target_pairs={{0,240},{16,0},{32,16},{48,32},{64,48},{80,64},{96,80},{112,96},{1... | collective-permute-start | bytes 884744 | tf_op jit(solution)/shard_map/ppermute | solution.py:29
  10.1 4.4 %collective-permute-done.low_ref = bf16[1152,128]{1,0:T(8,128)(2,1)S(1)} collective-permute-done((bf16[1152,128]{1,0:T(8,128)(2,1)S(1)}, bf16[1152,128]{1,0:T(8,128)(2,1)S(1)}, u32[]{:S(2)}, u32[]{:S(2)}) %collective-permute-start) | collective-permute-done | bytes 294944 | tf_op jit(solution)/shard_map/ppermute | solution.py:29
  14.5 0.1 regroup.4
  14.5 1.6 %collective-permute-start.2 = (bf16[1152,128]{1,0:T(8,128)(2,1)S(1)}, bf16[1152,128]{1,0:T(8,128)(2,1)S(1)}, u32[]{:S(2)}, u32[]{:S(2)}) collective-permute-start(bf16[1152,128]{1,0:T(8,128)(2,1)S(1)} %get-tuple-element.34), channel_id=1, source_target_pairs={{0,4},{4,8},{8,12},{12,0},{1,5},{5,9},{9,13},{13,1},{2,6},{6,10},{... | collective-permute-start | bytes 884744 | tf_op jit(solution)/shard_map/ppermute | solution.py:29
  16.1 1.7 %collective-permute-start.3 = (bf16[1152,128]{1,0:T(8,128)(2,1)S(1)}, bf16[1152,128]{1,0:T(8,128)(2,1)S(1)}, u32[]{:S(2)}, u32[]{:S(2)}) collective-permute-start(bf16[1152,128]{1,0:T(8,128)(2,1)S(1)} %get-tuple-element.36), channel_id=1, source_target_pairs={{0,12},{4,0},{8,4},{12,8},{1,13},{5,1},{9,5},{13,9},{2,14},{6,2},{... | collective-permute-start | bytes 884744 | tf_op jit(solution)/shard_map/ppermute | solution.py:29
  17.8 5.7 %collective-permute-done.2.low_ref = bf16[1152,128]{1,0:T(8,128)(2,1)S(1)} collective-permute-done((bf16[1152,128]{1,0:T(8,128)(2,1)S(1)}, bf16[1152,128]{1,0:T(8,128)(2,1)S(1)}, u32[]{:S(2)}, u32[]{:S(2)}) %collective-permute-start.2) | collective-permute-done | bytes 294944 | tf_op jit(solution)/shard_map/ppermute | solution.py:29
  23.5 0.8 %regroup.5 = (bf16[1152,128]{1,0:T(8,128)(2,1)S(1)}, bf16[1152,128]{1,0:T(8,128)(2,1)S(1)}, bf16[1152,128]{1,0:T(8,128)(2,1)}) custom-call(bf16[1152,128]{1,0:T(8,128)(2,1)S(1)} %collective-permute-done.2.low_ref, bf16[1152,128]{1,0:T(8,128)(2,1)S(1)} %get-tuple-element.35.middle_ref, bf16[1152,128]{1,0:T(8,128)(2,1)S(1)} %collective-permute-done.3.high_ref), custom_call_target="tpu_custom_call" | custom-call | tf_op jit(solution)/shard_map/regroup/pallas_call | solution.py:52
  24.3 0.2 collective-permute-start.4
  24.5 1.8 %collective-permute-start.5 = (bf16[1152,128]{1,0:T(8,128)(2,1)S(1)}, bf16[1152,128]{1,0:T(8,128)(2,1)S(1)}, u32[]{:S(2)}, u32[]{:S(2)}) collective-permute-start(bf16[1152,128]{1,0:T(8,128)(2,1)S(1)} %get-tuple-element.39), channel_id=1, source_target_pairs={{0,3},{1,0},{2,1},{3,2},{4,7},{5,4},{6,5},{7,6},{8,11},{9,8},{10,9... | collective-permute-start | bytes 884744 | tf_op jit(solution)/shard_map/ppermute | solution.py:29
  26.4 0.1 reshape.9
  26.5 0.0 copy-start.5
  26.5 0.0 copy-start.6
  26.5 0.0 copy-start.7
  26.5 4.0 %reverse_local.1.reverse_ref = f32[8224,128]{1,0:T(8,128)S(1)} custom-call(s32[2048]{0:T(1024)S(1)} %get-tuple-element.58.fetch_ref, bf16[2048,512]{1,0:T(8,128)(2,1)S(1)} %copy-done.1), custom_call_target="tpu_custom_call" | custom-call | tf_op jit(solution)/shard_map/reverse_local/pallas_call | solution.py:543
  30.6 1.9 %prepare.1 = (bf16[512,128]{1,0:T(8,128)(2,1)S(1)}, bf16[512,128]{1,0:T(8,128)(2,1)S(1)}, bf16[2,4096,256]{2,1,0:T(8,128)(2,1)S(1)}, bf16[2,64,512]{2,1,0:T(8,12...) custom-call(f32[32,2048]{1,0:T(8,128)S(1)} %bitcast.6, ...), custom_call_target="tpu_custom_call" | custom-call | tf_op jit(solution)/shard_map/prepare/pallas_call | solution.py:516
  32.6 15.5 %blocks.1 = (f32[2056,128]{1,0:T(8,128)S(1)}, bf16[288,128]{1,0:T(8,128)(2,1)S(1)}, bf16[288,128]{1,0:T(8,128)(2,1)S(1)}, bf16[288,128]{1,0:T(8,128)(2,1)S(1)}) custom-call(s32[864]{0:T(1024)S(1)} %get-tuple-element.59.target_ref, bf16[1152,128]{1,0:T(8,128)(2,1)S(1)} %collective-permute-done.4.low_ref, bf16[1152,128]{1,0:T(8,128)(2,1)S(1)} %get-tuple-element.38.middle_ref, ...), custom_call_target="tpu_custom_call" | custom-call | tf_op jit(solution)/shard_map/blocks/pallas_call | solution.py:553
  48.1 0.0 collective-permute-start.6
  48.1 4.8 %collective-permute-start.7 = (bf16[288,128]{1,0:T(8,128)(2,1)S(1)}, bf16[288,128]{1,0:T(8,128)(2,1)S(1)}, u32[]{:S(2)}, u32[]{:S(2)}) collective-permute-start(bf16[288,128]{1,0:T(8,128)(2,1)S(1)} %get-tuple-element.49), channel_id=1, source_target_pairs={{0,240},{16,0},{32,16},{48,32},{64,48},{80,64},{96,80},{112,96},{1... | collective-permute-start | bytes 221192 | tf_op jit(solution)/shard_map/ppermute | solution.py:29
  52.9 2.0 %collective-permute-done.6.low_ref = bf16[288,128]{1,0:T(8,128)(2,1)S(1)} collective-permute-done((bf16[288,128]{1,0:T(8,128)(2,1)S(1)}, bf16[288,128]{1,0:T(8,128)(2,1)S(1)}, u32[]{:S(2)}, u32[]{:S(2)}) %collective-permute-start.6) | collective-permute-done | bytes 73760 | tf_op jit(solution)/shard_map/ppermute | solution.py:29
  54.9 1.6 %collective-permute-start.8 = (bf16[288,128]{1,0:T(8,128)(2,1)S(1)}, bf16[288,128]{1,0:T(8,128)(2,1)S(1)}, u32[]{:S(2)}, u32[]{:S(2)}) collective-permute-start(bf16[288,128]{1,0:T(8,128)(2,1)S(1)} %get-tuple-element.50), channel_id=1, source_target_pairs={{0,4},{4,8},{8,12},{12,0},{1,5},{5,9},{9,13},{13,1},{2,6},{6,10},{... | collective-permute-start | bytes 221192 | tf_op jit(solution)/shard_map/ppermute | solution.py:29
  56.5 1.7 %collective-permute-start.9 = (bf16[288,128]{1,0:T(8,128)(2,1)S(1)}, bf16[288,128]{1,0:T(8,128)(2,1)S(1)}, u32[]{:S(2)}, u32[]{:S(2)}) collective-permute-start(bf16[288,128]{1,0:T(8,128)(2,1)S(1)} %get-tuple-element.52), channel_id=1, source_target_pairs={{0,12},{4,0},{8,4},{12,8},{1,13},{5,1},{9,5},{13,9},{2,14},{6,2},{... | collective-permute-start | bytes 221192 | tf_op jit(solution)/shard_map/ppermute | solution.py:29
  58.3 2.3 %collective-permute-done.8.low_ref = bf16[288,128]{1,0:T(8,128)(2,1)S(1)} collective-permute-done((bf16[288,128]{1,0:T(8,128)(2,1)S(1)}, bf16[288,128]{1,0:T(8,128)(2,1)S(1)}, u32[]{:S(2)}, u32[]{:S(2)}) %collective-permute-start.8) | collective-permute-done | bytes 73760 | tf_op jit(solution)/shard_map/ppermute | solution.py:29
  60.6 0.3 collective-permute-done.9.high_ref
  60.9 1.1 %collective-permute-start.10 = (bf16[288,128]{1,0:T(8,128)(2,1)S(1)}, bf16[288,128]{1,0:T(8,128)(2,1)S(1)}, u32[]{:S(2)}, u32[]{:S(2)}) collective-permute-start(bf16[288,128]{1,0:T(8,128)(2,1)S(1)} %get-tuple-element.53), channel_id=1, source_target_pairs={{0,1},{1,2},{2,3},{3,0},{4,5},{5,6},{6,7},{7,4},{8,9},{9,10},{10,1... | collective-permute-start | bytes 221192 | tf_op jit(solution)/shard_map/ppermute | solution.py:29
  62.0 1.3 %collective-permute-start.11 = (bf16[288,128]{1,0:T(8,128)(2,1)S(1)}, bf16[288,128]{1,0:T(8,128)(2,1)S(1)}, u32[]{:S(2)}, u32[]{:S(2)}) collective-permute-start(bf16[288,128]{1,0:T(8,128)(2,1)S(1)} %get-tuple-element.55), channel_id=1, source_target_pairs={{0,3},{1,0},{2,1},{3,2},{4,7},{5,4},{6,5},{7,6},{8,11},{9,8},{10,9... | collective-permute-start | bytes 221192 | tf_op jit(solution)/shard_map/ppermute | solution.py:29
  63.2 2.8 %trip_local.1.trip_ref = f32[2056,128]{1,0:T(8,128)S(1)} custom-call(s32[2048]{0:T(1024)S(1)} %get-tuple-element.57.fetch_ref, f32[2056,128]{1,0:T(8,128)S(1)} %get-tuple-element.56.trip_ref), custom_call_target="tpu_custom_call" | custom-call | tf_op jit(solution)/shard_map/trip_local/pallas_call | solution.py:584
  66.1 1.5 %collective-permute-done.11.high_ref = bf16[288,128]{1,0:T(8,128)(2,1)S(1)} collective-permute-done((bf16[288,128]{1,0:T(8,128)(2,1)S(1)}, bf16[288,128]{1,0:T(8,128)(2,1)S(1)}, u32[]{:S(2)}, u32[]{:S(2)}) %collective-permute-start.11) | collective-permute-done | bytes 73760 | tf_op jit(solution)/shard_map/ppermute | solution.py:29
  67.5 9.4 %final.1 = bf16[2048,512]{1,0:T(8,128)(2,1)} custom-call(s32[864]{0:T(1024)S(1)} %get-tuple-element.60.send_ref, bf16[288,128]{1,0:T(8,128)(2,1)S(1)} %collective-permute-done.10.low_ref, bf16[288,128]{1,0:T(8,128)(2,1)S(1)} %get-tuple-element.54.middle_ref, bf16[288,128]{1,0:T(8,128)(2,1)S(1)} %collective-permute-done.11.high_ref, ...), custom_call_target="tpu_custom_call" | custom-call | tf_op jit(solution)/shard_map/final/pallas_call | solution.py:594
  (30 shorter events, 0.2 us)
Async XLA Ops:
  0.0 1.6 %copy-start = (bf16[2048,512]{1,0:T(8,128)(2,1)S(1)}, bf16[2048,512]{1,0:T(8,128)(2,1)}, u32[]{:S(2)}) copy-start(bf16[2048,512]{1,0:T(8,128)(2,1)} %rows_ref.3) | copy-start | bytes 6291460
  1.6 0.7 copy-start.10
  2.3 24.0 %copy-start.9 = (s32[2048]{0:T(1024)S(1)}, s32[2048]{0:T(1024)}, u32[]{:S(2)}) copy-start(s32[2048]{0:T(1024)} %param.14) | copy-start | bytes 24580
  2.3 24.0 %copy-start.11 = (s32[1,1,1,27,32]{4,2,3,1,0:T(1,128)S(1)}, s32[1,1,1,27,32]{4,2,3,1,0:T(1,128)}, u32[]{:S(2)}) copy-start(s32[1,1,1,27,32]{4,2,3,1,0:T(1,128)} %param.13) | copy-start | bytes 10372
  2.3 24.2 %copy-start.1 = (bf16[2048,512]{1,0:T(8,128)(2,1)S(1)}, bf16[2048,512]{1,0:T(8,128)(2,1)}, u32[]{:S(2)}) copy-start(bf16[2048,512]{1,0:T(8,128)(2,1)} %rows_ref.3) | copy-start | bytes 6291460
  4.8 9.7 %collective-permute-start = (bf16[1152,128]{1,0:T(8,128)(2,1)S(1)}, bf16[1152,128]{1,0:T(8,128)(2,1)S(1)}, u32[]{:S(2)}, u32[]{:S(2)}) collective-permute-start(bf16[1152,128]{1,0:T(8,128)(2,1)S(1)} %get-tuple-element.31), channel_id=1, source_target_pairs={{0,16},{16,32},{32,48},{48,64},{64,80},{80,96},{96,112},{112,128},... | collective-permute-start | bytes 884744 | tf_op jit(solution)/shard_map/ppermute | solution.py:29
  4.8 9.7 %collective-permute-start.1 = (bf16[1152,128]{1,0:T(8,128)(2,1)S(1)}, bf16[1152,128]{1,0:T(8,128)(2,1)S(1)}, u32[]{:S(2)}, u32[]{:S(2)}) collective-permute-start(bf16[1152,128]{1,0:T(8,128)(2,1)S(1)} %get-tuple-element.33), channel_id=1, source_target_pairs={{0,240},{16,0},{32,16},{48,32},{64,48},{80,64},{96,80},{112,96},{1... | collective-permute-start | bytes 884744 | tf_op jit(solution)/shard_map/ppermute | solution.py:29
  14.5 9.0 %collective-permute-start.2 = (bf16[1152,128]{1,0:T(8,128)(2,1)S(1)}, bf16[1152,128]{1,0:T(8,128)(2,1)S(1)}, u32[]{:S(2)}, u32[]{:S(2)}) collective-permute-start(bf16[1152,128]{1,0:T(8,128)(2,1)S(1)} %get-tuple-element.34), channel_id=1, source_target_pairs={{0,4},{4,8},{8,12},{12,0},{1,5},{5,9},{9,13},{13,1},{2,6},{6,10},{... | collective-permute-start | bytes 884744 | tf_op jit(solution)/shard_map/ppermute | solution.py:29
  16.1 7.4 %collective-permute-start.3 = (bf16[1152,128]{1,0:T(8,128)(2,1)S(1)}, bf16[1152,128]{1,0:T(8,128)(2,1)S(1)}, u32[]{:S(2)}, u32[]{:S(2)}) collective-permute-start(bf16[1152,128]{1,0:T(8,128)(2,1)S(1)} %get-tuple-element.36), channel_id=1, source_target_pairs={{0,12},{4,0},{8,4},{12,8},{1,13},{5,1},{9,5},{13,9},{2,14},{6,2},{... | collective-permute-start | bytes 884744 | tf_op jit(solution)/shard_map/ppermute | solution.py:29
  24.3 8.3 %collective-permute-start.4 = (bf16[1152,128]{1,0:T(8,128)(2,1)}, bf16[1152,128]{1,0:T(8,128)(2,1)S(1)}, u32[]{:S(2)}, u32[]{:S(2)}) collective-permute-start(bf16[1152,128]{1,0:T(8,128)(2,1)} %get-tuple-element.37), channel_id=1, source_target_pairs={{0,1},{1,2},{2,3},{3,0},{4,5},{5,6},{6,7},{7,4},{8,9},{9,10},{10,1... | collective-permute-start | bytes 884744 | tf_op jit(solution)/shard_map/ppermute | solution.py:29
  24.5 8.1 %collective-permute-start.5 = (bf16[1152,128]{1,0:T(8,128)(2,1)S(1)}, bf16[1152,128]{1,0:T(8,128)(2,1)S(1)}, u32[]{:S(2)}, u32[]{:S(2)}) collective-permute-start(bf16[1152,128]{1,0:T(8,128)(2,1)S(1)} %get-tuple-element.39), channel_id=1, source_target_pairs={{0,3},{1,0},{2,1},{3,2},{4,7},{5,4},{6,5},{7,6},{8,11},{9,8},{10,9... | collective-permute-start | bytes 884744 | tf_op jit(solution)/shard_map/ppermute | solution.py:29
  26.5 4.1 %copy-start.2 = (bf16[2,512,512]{2,1,0:T(8,128)(2,1)S(1)}, bf16[2,512,512]{2,1,0:T(8,128)(2,1)}, u32[]{:S(2)}) copy-start(bf16[2,512,512]{2,1,0:T(8,128)(2,1)} %first_ref.1) | copy-start | bytes 3145732
  26.5 4.1 %copy-start.3 = (bf16[2,512,512]{2,1,0:T(8,128)(2,1)S(1)}, bf16[2,512,512]{2,1,0:T(8,128)(2,1)}, u32[]{:S(2)}) copy-start(bf16[2,512,512]{2,1,0:T(8,128)(2,1)} %second_ref.1) | copy-start | bytes 3145732
  26.5 4.1 %copy-start.4 = (f32[2048,32]{0,1:T(8,128)S(1)}, f32[2048,32]{0,1:T(8,128)}, u32[]{:S(2)}) copy-start(f32[2048,32]{0,1:T(8,128)} %param.11) | copy-start | bytes 786436
  26.5 4.1 %copy-start.5 = (s32[2048,32]{0,1:T(8,128)S(1)}, s32[2048,32]{0,1:T(8,128)}, u32[]{:S(2)}) copy-start(s32[2048,32]{0,1:T(8,128)} %param.12) | copy-start | bytes 786436
  26.5 4.1 %copy-start.6 = (bf16[2,1024,64]{1,2,0:T(8,128)(2,1)S(1)}, bf16[2,1024,64]{1,2,0:T(8,128)(2,1)}, u32[]{:S(2)}) copy-start(bf16[2,1024,64]{1,2,0:T(8,128)(2,1)} %param.16) | copy-start | bytes 786436
  26.5 4.1 %copy-start.7 = (bf16[2,64,512]{2,1,0:T(8,128)(2,1)S(1)}, bf16[2,64,512]{2,1,0:T(8,128)(2,1)}, u32[]{:S(2)}) copy-start(bf16[2,64,512]{2,1,0:T(8,128)(2,1)} %up_ref.1) | copy-start | bytes 393220
  26.5 4.1 %copy-start.8 = (bf16[2,512,64]{1,2,0:T(8,128)(2,1)S(1)}, bf16[2,512,64]{1,2,0:T(8,128)(2,1)}, u32[]{:S(2)}) copy-start(bf16[2,512,64]{1,2,0:T(8,128)(2,1)} %param.15) | copy-start | bytes 393220
  48.1 6.9 %collective-permute-start.6 = (bf16[288,128]{1,0:T(8,128)(2,1)S(1)}, bf16[288,128]{1,0:T(8,128)(2,1)S(1)}, u32[]{:S(2)}, u32[]{:S(2)}) collective-permute-start(bf16[288,128]{1,0:T(8,128)(2,1)S(1)} %get-tuple-element.47), channel_id=1, source_target_pairs={{0,16},{16,32},{32,48},{48,64},{64,80},{80,96},{96,112},{112,128},... | collective-permute-start | bytes 221192 | tf_op jit(solution)/shard_map/ppermute | solution.py:29
  48.1 6.8 %collective-permute-start.7 = (bf16[288,128]{1,0:T(8,128)(2,1)S(1)}, bf16[288,128]{1,0:T(8,128)(2,1)S(1)}, u32[]{:S(2)}, u32[]{:S(2)}) collective-permute-start(bf16[288,128]{1,0:T(8,128)(2,1)S(1)} %get-tuple-element.49), channel_id=1, source_target_pairs={{0,240},{16,0},{32,16},{48,32},{64,48},{80,64},{96,80},{112,96},{1... | collective-permute-start | bytes 221192 | tf_op jit(solution)/shard_map/ppermute | solution.py:29
  54.9 5.6 %collective-permute-start.8 = (bf16[288,128]{1,0:T(8,128)(2,1)S(1)}, bf16[288,128]{1,0:T(8,128)(2,1)S(1)}, u32[]{:S(2)}, u32[]{:S(2)}) collective-permute-start(bf16[288,128]{1,0:T(8,128)(2,1)S(1)} %get-tuple-element.50), channel_id=1, source_target_pairs={{0,4},{4,8},{8,12},{12,0},{1,5},{5,9},{9,13},{13,1},{2,6},{6,10},{... | collective-permute-start | bytes 221192 | tf_op jit(solution)/shard_map/ppermute | solution.py:29
  56.5 4.4 %collective-permute-start.9 = (bf16[288,128]{1,0:T(8,128)(2,1)S(1)}, bf16[288,128]{1,0:T(8,128)(2,1)S(1)}, u32[]{:S(2)}, u32[]{:S(2)}) collective-permute-start(bf16[288,128]{1,0:T(8,128)(2,1)S(1)} %get-tuple-element.52), channel_id=1, source_target_pairs={{0,12},{4,0},{8,4},{12,8},{1,13},{5,1},{9,5},{13,9},{2,14},{6,2},{... | collective-permute-start | bytes 221192 | tf_op jit(solution)/shard_map/ppermute | solution.py:29
  60.9 5.2 %collective-permute-start.10 = (bf16[288,128]{1,0:T(8,128)(2,1)S(1)}, bf16[288,128]{1,0:T(8,128)(2,1)S(1)}, u32[]{:S(2)}, u32[]{:S(2)}) collective-permute-start(bf16[288,128]{1,0:T(8,128)(2,1)S(1)} %get-tuple-element.53), channel_id=1, source_target_pairs={{0,1},{1,2},{2,3},{3,0},{4,5},{5,6},{6,7},{7,4},{8,9},{9,10},{10,1... | collective-permute-start | bytes 221192 | tf_op jit(solution)/shard_map/ppermute | solution.py:29
  62.0 5.6 %collective-permute-start.11 = (bf16[288,128]{1,0:T(8,128)(2,1)S(1)}, bf16[288,128]{1,0:T(8,128)(2,1)S(1)}, u32[]{:S(2)}, u32[]{:S(2)}) collective-permute-start(bf16[288,128]{1,0:T(8,128)(2,1)S(1)} %get-tuple-element.55), channel_id=1, source_target_pairs={{0,3},{1,0},{2,1},{3,2},{4,7},{5,4},{6,5},{7,6},{8,11},{9,8},{10,9... | collective-permute-start | bytes 221192 | tf_op jit(solution)/shard_map/ppermute | solution.py:29

commit v2 on v1

v2 whole, which is shorter than its diff:
```python
import jax
import jax.numpy as jnp
from jax import lax
from jax.experimental import pallas as pl
from jax.experimental.pallas import tpu as pltpu
from jax.sharding import PartitionSpec as P


HALF_ROOT = 0.7071067811865476
F32 = jnp.float32
BF16 = jnp.bfloat16
MIB = 1024 * 1024
BLOCK_TRIPS = 2
FINAL_TRIPS = 1


def silu_of_half(half):
    return half + half * jnp.tanh(half)


def dot(a, b):
    return jnp.dot(a, b, preferred_element_type=F32)


def dot_t(a, b):
    return lax.dot_general(a, b, (((1,), (1,)), ((), ())), preferred_element_type=F32)


def from_behind(array, axis, by):
    length = lax.axis_size(axis)
    return lax.ppermute(array, axis, [(i, (i + by) % length) for i in range(length)])


def second_kernel(low_ref, middle_ref, high_ref, *out_refs):
    third = low_ref.shape[0] // 3
    for a, slab_ref in enumerate((low_ref, middle_ref, high_ref)):
        for b, out_ref in enumerate(out_refs):
            out_ref[third * a : third * (a + 1), :] = slab_ref[third * b : third * (b + 1), :]


def third_kernel(low_ref, middle_ref, high_ref, *out_refs):
    rows = low_ref.shape[0] // 9
    for b, slab_ref in enumerate((low_ref, middle_ref, high_ref)):
        for a in range(3):
            for c, out_ref in enumerate(out_refs):
                source, target = rows * (3 * a + c), rows * (3 * b + a)
                out_ref[target : target + rows, :] = slab_ref[source : source + rows, :]


def exchange(slabs):
    vmem = pl.BlockSpec(memory_space=pltpu.VMEM)

    def regroup(kernel, pieces):
        return pl.pallas_call(
            kernel,
            out_shape=[jax.ShapeDtypeStruct(piece.shape, piece.dtype) for piece in pieces],
            in_specs=[vmem] * 3,
            out_specs=[vmem] * 3,
            compiler_params=pltpu.CompilerParams(vmem_limit_bytes=4 * MIB),
            name="regroup",
        )(*pieces)

    def hop(sent, axis):
        low, middle, high = sent
        return [from_behind(high, axis, 1), middle, from_behind(low, axis, -1)]

    slabs = hop(slabs, "gx")
    slabs = hop(regroup(second_kernel, slabs), "gy")
    return hop(regroup(third_kernel, slabs), "gz")


def pipelined(blocks, stages, trips):
    share = blocks // trips

    def trip(t, carry):
        for step in range(share + len(stages) - 1):
            for depth in reversed(range(len(stages))):
                if 0 <= step - depth < share:
                    stages[depth](t * share + step - depth)
        return carry

    if trips == 1:
        trip(0, 0)
    else:
        lax.fori_loop(0, trips, trip, 0)


def span(i, size):
    if isinstance(i, int):
        return slice(size * i, size * (i + 1))
    return pl.ds(pl.multiple_of(size * i, size), size)


def spread_rows(rows_ref, wide_ref, start, count, shift=0):
    for c in range(4):
        wide_ref[pl.ds(4 * (start + shift) + c, count, stride=4), :] = rows_ref[
            start : start + count, 128 * c : 128 * (c + 1)
        ].astype(F32)


def local_edge(fetch_ref, edge, spare):
    return jnp.minimum(fetch_ref[edge].astype(jnp.uint32), jnp.uint32(spare)).astype(jnp.int32)


def for_slots(send_ref, step):
    directions, _, each = send_ref.shape

    def body(t, carry):
        for r in range(each):
            step(t, r, t * each + r)
        return carry

    lax.fori_loop(0, directions, body, 0)


def pack_kernel(
    send_hbm_ref,
    rows_hbm_ref,
    low_ref,
    middle_ref,
    high_ref,
    send_ref,
    rows_ref,
    wide_ref,
    packed_ref,
    copied,
    listed,
):
    count = rows_ref.shape[0]
    each = send_ref.shape[2]
    chunk = count // 8
    copies = [
        pltpu.make_async_copy(
            rows_hbm_ref.at[pl.ds(chunk * i, chunk), :],
            rows_ref.at[pl.ds(chunk * i, chunk), :],
            copied.at[i],
        )
        for i in range(8)
    ]
    slots = pltpu.make_async_copy(send_hbm_ref, send_ref, listed)
    slots.start()
    wide_ref[0:32, :] = jnp.zeros((32, 128), F32)
    for copy in copies:
        copy.start()
    for i, copy in enumerate(copies):
        copy.wait()
        spread_rows(rows_ref, wide_ref, chunk * i, chunk, 8)
    slots.wait()

    def pick(t, r, s):
        source = pl.multiple_of(send_ref[t, 0, r] * 4 + 32, 4)
        packed_ref[pl.ds(pl.multiple_of(s * 4, 4), 4), :] = wide_ref[pl.ds(source, 4), :]

    for_slots(send_ref, pick)
    slab = 9 * 4 * each
    for i, out_ref in enumerate((low_ref, middle_ref, high_ref)):
        out_ref[...] = packed_ref[slab * i : slab * (i + 1), :].astype(BF16)


def local_kernel(fetch_ref, rows_ref, out_ref, wide_ref):
    count = rows_ref.shape[0]
    for start in range(0, count, 256):
        spread_rows(rows_ref, wide_ref, start, 256)
    wide_ref[4 * count : 4 * count + 8, :] = jnp.zeros((8, 128), F32)
    unroll = 32

    def body(i, carry):
        for k in range(unroll):
            source = pl.multiple_of(local_edge(fetch_ref, i * unroll + k, count) * 4, 4)
            target = pl.multiple_of((i * unroll + k) * 4, 4)
            out_ref[pl.ds(target, 4), :] = wide_ref[pl.ds(source, 4), :]
        return carry

    lax.fori_loop(0, count // unroll, body, 0)


def widen_arrived(pieces, wide_ref):
    for c, piece in enumerate(pieces):
        rows = piece.shape[0] // 9
        for i in range(9):
            start = rows * (9 * (i % 3) + 3 * (i // 3) + c)
            wide_ref[start : start + rows, :] = piece[rows * i : rows * (i + 1), :].astype(F32)


def blocks_kernel(
    send_ref,
    low_ref,
    middle_ref,
    high_ref,
    reverse_ref,
    weight_ref,
    bins_ref,
    down_ref,
    mixer_ref,
    up_ref,
    first_ref,
    second_ref,
    trip_ref,
    send_low_ref,
    send_middle_ref,
    send_high_ref,
    arrived32_ref,
    rows_ref,
    wide_ref,
    summed_ref,
    packed_ref,
    mixed_ref,
    inner_ref,
):
    count = rows_ref.shape[0]
    groups = summed_ref.shape[0] // 32
    trip = up_ref.shape[1]
    angular = summed_ref.shape[1] // 256
    widen_arrived((low_ref, middle_ref, high_ref), arrived32_ref)

    def place(t, r, s):
        target = pl.multiple_of(send_ref[t, 0, r] * 4, 4)
        reverse_ref[pl.ds(target, 4), :] = arrived32_ref[pl.ds(pl.multiple_of(s * 4, 4), 4), :]

    for_slots(send_ref, place)
    for start in range(0, count, 256):
        for c in range(4):
            rows_ref[start : start + 256, 128 * c : 128 * (c + 1)] = reverse_ref[
                pl.ds(4 * start + c, 256, stride=4), :
            ].astype(BF16)
    trip_ref[count : count + 8, :] = jnp.zeros((8, 128), F32)
    step = 256
    shape = (step, 4 * trip)
    own_lanes = (
        lax.broadcasted_iota(jnp.int32, shape, 0) // 32 % 4
        == lax.broadcasted_iota(jnp.int32, shape, 1) // trip
    )
    downs = [jnp.concatenate([down_ref[block]] * 4, axis=0) for block in range(2)]

    def project(i, block):
        at = span(i, step)
        projected = silu_of_half(dot_t(rows_ref[at, :], downs[block]))
        wide_ref[at, :] = jnp.where(own_lanes, projected, 0.0).astype(BF16)

    def lift(i):
        at = span(i, step)
        lifted = silu_of_half(dot(trip_ref[at, :trip].astype(BF16), up_ref[0]))
        rows = rows_ref[at, :].astype(F32)
        mixed_ref[at, :] = ((rows + lifted) * HALF_ROOT).astype(BF16)

    def first(i):
        at = span(i, step)
        inner_ref[at, :] = silu_of_half(dot(mixed_ref[at, :], first_ref[0])).astype(BF16)

    def second(i):
        at = span(i, step)
        change = silu_of_half(dot(inner_ref[at, :], second_ref[0]))
        rows_ref[at, :] = ((mixed_ref[at, :].astype(F32) + change) * HALF_ROOT).astype(BF16)

    def group(g, carry):
        start = pl.multiple_of(g * 32, 32)
        weight = weight_ref[pl.ds(start, 32), :]
        bins = bins_ref[pl.ds(start, 32), :]
        zero = jnp.zeros_like(weight)
        chosen = [jnp.where(bins == b, weight, zero) for b in range(angular)]
        own = wide_ref[pl.ds(pl.multiple_of(g * 128, 128), 128), :]
        sums = dot(jnp.concatenate(chosen, axis=0), own).astype(BF16)
        for b in range(angular):
            summed_ref[pl.ds(start, 32), 256 * b : 256 * (b + 1)] = sums[32 * b : 32 * (b + 1), :]
        return carry

    for i in range(count // step):
        project(i, 0)
    for block in range(2):
        lax.fori_loop(0, groups, group, 0, unroll=8)
        triplet = dot(summed_ref[...], mixer_ref[block]).astype(BF16).astype(F32)
        for g in range(groups):
            for a in range(4):
                start = 128 * g + 32 * a
                trip_ref[start : start + 32, trip * block : trip * (block + 1)] = triplet[
                    32 * g : 32 * (g + 1), trip * a : trip * (a + 1)
                ]
        if block == 0:
            pipelined(count // step, (lift, first, second, lambda i: project(i, 1)), BLOCK_TRIPS)

    def pick(t, r, s):
        packed_ref[pl.ds(s, 1), :] = trip_ref[pl.ds(send_ref[t, 0, r], 1), :]

    for_slots(send_ref, pick)
    slab = packed_ref.shape[0] // 3
    for i, out_ref in enumerate((send_low_ref, send_middle_ref, send_high_ref)):
        out_ref[...] = packed_ref[slab * i : slab * (i + 1), :].astype(BF16)


def trip_kernel(fetch_ref, trip_ref, out_ref):
    count = fetch_ref.shape[0]
    unroll = 32

    def body(i, carry):
        for k in range(unroll):
            edge = i * unroll + k
            out_ref[pl.ds(edge, 1), :] = trip_ref[pl.ds(local_edge(fetch_ref, edge, count), 1), :]
        return carry

    lax.fori_loop(0, count // unroll, body, 0)


def final_kernel(
    send_ref,
    low_ref,
    middle_ref,
    high_ref,
    trip_ref,
    rows_ref,
    live_ref,
    up_ref,
    first_ref,
    second_ref,
    out_ref,
    arrived32_ref,
    mixed_ref,
    inner_ref,
    mixed_next_ref,
    inner_next_ref,
    rows_out_ref,
    mask_ref,
    copied,
):
    count = rows_ref.shape[0]
    trip = up_ref.shape[1]
    widen_arrived((low_ref, middle_ref, high_ref), arrived32_ref)

    def place(t, r, s):
        trip_ref[pl.ds(send_ref[t, 0, r], 1), :] = arrived32_ref[pl.ds(s, 1), :]

    for_slots(send_ref, place)
    step = 256

    def lifted(at, block):
        both = trip_ref[at, :].astype(BF16)
        return silu_of_half(dot(both[:, trip * block : trip * (block + 1)], up_ref[block]))

    def lift(i):
        at = span(i, step)
        for h in range(step // 128):
            g = i * (step // 128) + h
            line = live_ref[pl.ds(g, 1), :].astype(F32)
            mask_ref[span(g, 128), :] = jnp.broadcast_to(line, (128, 128)).T
        rows = rows_ref[at, :].astype(F32)
        mixed_ref[at, :] = ((rows + lifted(at, 0)) * HALF_ROOT).astype(BF16)

    def first(i):
        at = span(i, step)
        inner_ref[at, :] = silu_of_half(dot(mixed_ref[at, :], first_ref[0])).astype(BF16)

    def second(i):
        at = span(i, step)
        change = silu_of_half(dot(inner_ref[at, :], second_ref[0]))
        rows = (mixed_ref[at, :].astype(F32) + change) * HALF_ROOT
        mixed_next_ref[at, :] = ((rows + lifted(at, 1)) * HALF_ROOT).astype(BF16)

    def first_next(i):
        at = span(i, step)
        inner_next_ref[at, :] = silu_of_half(dot(mixed_next_ref[at, :], first_ref[1])).astype(BF16)

    def second_next(i):
        at = span(i, step)
        change = silu_of_half(dot(inner_next_ref[at, :], second_ref[1]))
        rows = (mixed_next_ref[at, :].astype(F32) + change) * HALF_ROOT
        for c in range(4):
            lanes = slice(128 * c, 128 * (c + 1))
            rows_out_ref[at, lanes] = jnp.where(mask_ref[at, :] >= 0.0, rows[:, lanes], 0.0).astype(
                BF16
            )
        copy_out(i).start()

    def copy_out(i):
        at = span(i, step)
        return pltpu.make_async_copy(rows_out_ref.at[at, :], out_ref.at[at, :], copied.at[i])

    pipelined(count // step, (lift, first, second, first_next, second_next), FINAL_TRIPS)
    for i in range(count // step):
        copy_out(i).wait()


def prepare_kernel(
    weight_ref,
    bins_ref,
    live_ref,
    bilinear_ref,
    up_ref,
    first_ref,
    second_ref,
    down_ref,
    senders_ref,
    weight_out_ref,
    bins_out_ref,
    mixer_ref,
    up_out_ref,
    first_out_ref,
    second_out_ref,
    down_out_ref,
    slots_ref,
):
    count = weight_ref.shape[1]
    slots_ref[...] = jnp.where(senders_ref[...] < 0, count, senders_ref[...])
    neigh = weight_ref.shape[0]
    side = 4 * neigh
    groups = weight_ref.shape[1] // side
    trip = bilinear_ref.shape[1]
    angular = bilinear_ref.shape[2] // trip
    row = lax.broadcasted_iota(jnp.int32, (side, side), 0)
    lane = lax.broadcasted_iota(jnp.int32, (side, side), 1)
    distinct = row % neigh != lane % neigh
    piece = lax.broadcasted_iota(jnp.int32, (neigh, side), 1) // neigh

    def turn(blocks):
        stacked = []
        for a in range(4):
            rows = jnp.zeros((neigh, side), F32)
            for h in range(4):
                shift = (h - a) * neigh % side
                moved = pltpu.roll(blocks[h], shift, 1) if shift else blocks[h]
                rows = jnp.where(piece == h, moved, rows)
            stacked.append(rows)
        return jnp.concatenate(stacked, axis=0).T

    for start in range(0, groups, 4):
        spans = [slice(side * (start + h), side * (start + h + 1)) for h in range(4)]
        rows = slice(neigh * start, neigh * start + side)
        weight_out_ref[rows, :] = turn([weight_ref[:, span] for span in spans]).astype(BF16)
        live = jnp.concatenate(
            [
                jnp.broadcast_to(live_ref[start + h : start + h + 1, :], (neigh, side))
                for h in range(4)
            ],
            axis=0,
        )
        bins = turn([bins_ref[:, span].astype(F32) for span in spans])
        bins_out_ref[rows, :] = jnp.where(distinct & (live >= 0), bins, -1.0).astype(BF16)
    lane_block = lax.broadcasted_iota(jnp.int32, (trip, 4 * trip), 1) // trip
    for block in range(2):
        turned = bilinear_ref[block].astype(F32).T
        wide = jnp.concatenate([turned] * 4, axis=1)
        for b in range(angular):
            part = wide[trip * b : trip * (b + 1), :]
            for a in range(4):
                start = 4 * trip * b + trip * a
                mixer_ref[block, start : start + trip, :] = jnp.where(
                    lane_block == a, part, 0.0
                ).astype(BF16)
    for source, target in (
        (up_ref, up_out_ref),
        (first_ref, first_out_ref),
        (second_ref, second_out_ref),
        (down_ref, down_out_ref),
    ):
        target[...] = (source[...].astype(F32) * 0.5).astype(BF16)


def local(
    edge_state,
    angle_weight,
    angle_bins,
    send_slots,
    fetch_index,
    down_weight,
    bilinear,
    up_weight,
    first_dense,
    second_dense,
):
    count, width = edge_state.shape
    neigh = angle_weight.shape[1]
    trip = down_weight.shape[2]
    angular = bilinear.shape[1] // trip
    slots = 27 * send_slots.shape[-1]
    quarter = count // 4
    groups = count // (4 * neigh)
    spare = count + 8
    live_lines = fetch_index.reshape(groups, 4 * neigh)
    each = send_slots.shape[-1]
    senders = send_slots.reshape(27, 1, each)
    down_turned = jnp.swapaxes(down_weight, 1, 2)

    smem = pl.BlockSpec(memory_space=pltpu.SMEM)
    vmem = pl.BlockSpec(memory_space=pltpu.VMEM)

    def params(mib):
        return pltpu.CompilerParams(vmem_limit_bytes=mib * MIB)

    outside = pl.BlockSpec(memory_space=pltpu.HBM)
    slab = slots // 3
    packed = pl.pallas_call(
        pack_kernel,
        out_shape=(jax.ShapeDtypeStruct((slab * 4, 128), BF16),) * 3,
        in_specs=[outside, outside],
        out_specs=(vmem,) * 3,
        scratch_shapes=[
            pltpu.SMEM((27, 1, each), jnp.int32),
            pltpu.VMEM((count, width), BF16),
            pltpu.VMEM((spare * 4, 128), F32),
            pltpu.VMEM((slots * 4, 128), F32),
            pltpu.SemaphoreType.DMA((8,)),
            pltpu.SemaphoreType.DMA,
        ],
        compiler_params=params(14),
        name="pack",
    )(
        pltpu.with_memory_space_constraint(senders, pltpu.HBM),
        pltpu.with_memory_space_constraint(edge_state, pltpu.HBM),
    )
    weights, bins, mixer, up_half, first_half, second_half, down_half, own_slots = pl.pallas_call(
        prepare_kernel,
        out_shape=(
            jax.ShapeDtypeStruct((quarter, 4 * neigh), BF16),
            jax.ShapeDtypeStruct((quarter, 4 * neigh), BF16),
            jax.ShapeDtypeStruct((2, angular * 4 * trip, 4 * trip), BF16),
            jax.ShapeDtypeStruct(up_weight.shape, BF16),
            jax.ShapeDtypeStruct(first_dense.shape, BF16),
            jax.ShapeDtypeStruct(second_dense.shape, BF16),
            jax.ShapeDtypeStruct(down_turned.shape, BF16),
            jax.ShapeDtypeStruct(senders.shape, jnp.int32),
        ),
        in_specs=[vmem] * 9,
        out_specs=(vmem,) * 8,
        compiler_params=params(16),
        name="prepare",
    )(
        angle_weight.T,
        angle_bins.T,
        live_lines,
        jnp.swapaxes(bilinear, 1, 2),
        up_weight,
        first_dense,
        second_dense,
        down_turned,
        senders,
    )
    arrived = exchange(packed)

    reverse = pl.pallas_call(
        local_kernel,
        out_shape=jax.ShapeDtypeStruct((spare * 4, 128), F32),
        in_specs=[smem, vmem],
        out_specs=vmem,
        scratch_shapes=[pltpu.VMEM((spare * 4, 128), F32)],
        compiler_params=params(14),
        name="reverse_local",
    )(fetch_index, edge_state)

    triplet, *sending = pl.pallas_call(
        blocks_kernel,
        out_shape=(
            jax.ShapeDtypeStruct((spare, 2 * trip), F32),
        )
        + (jax.ShapeDtypeStruct((slab, 2 * trip), BF16),) * 3,
        in_specs=[smem] + [vmem] * 11,
        out_specs=(vmem,) * 4,
        scratch_shapes=[
            pltpu.VMEM((slots * 4, 128), F32),
            pltpu.VMEM((count, width), BF16),
            pltpu.VMEM((count, 4 * trip), BF16),
            pltpu.VMEM((quarter, angular * 4 * trip), BF16),
            pltpu.VMEM((slots, 2 * trip), F32),
            pltpu.VMEM((count, width), BF16),
            pltpu.VMEM((count, width), BF16),
        ],
        compiler_params=params(32),
        name="blocks",
    )(
        own_slots,
        *arrived,
        reverse,
        weights,
        bins,
        down_half,
        mixer,
        up_half,
        first_half,
        second_half,
    )
    own_trip = pl.pallas_call(
        trip_kernel,
        out_shape=jax.ShapeDtypeStruct((spare, 2 * trip), F32),
        in_specs=[smem, vmem],
        out_specs=vmem,
        compiler_params=params(5),
        name="trip_local",
    )(fetch_index, triplet)
    carried = exchange(sending)

    out = pl.pallas_call(
        final_kernel,
        out_shape=jax.ShapeDtypeStruct((count, width), BF16),
        in_specs=[smem] + [vmem] * 9,
        out_specs=outside,
        scratch_shapes=[pltpu.VMEM((slots, 2 * trip), F32)]
        + [pltpu.VMEM((count, width), BF16)] * 5
        + [pltpu.VMEM((count, 128), F32)]
        + [pltpu.SemaphoreType.DMA((8,))],
        compiler_params=params(24),
        name="final",
    )(
        own_slots,
        *carried,
        own_trip,
        edge_state,
        live_lines,
        up_half,
        first_half,
        second_half,
    )
    return out


def solution(mesh):
    spread = P(("gx", "gy", "gz"), None)
    in_specs = (
        spread,
        spread,
        spread,
        P("gx", "gy", "gz", None, None),
        P(("gx", "gy", "gz")),
        P(),
        P(),
        P(),
        P(),
        P(),
    )

    return jax.shard_map(local, mesh=mesh, in_specs=in_specs, out_specs=spread, check_vma=False)
```

time: 77.8 us -> 73.3 us (0.942)
  local copies, waits for them, and re-layouts: 2.42 us -> 0.05 us
  Pallas kernels: 36.9 us -> 35.2 us
    unnamed x24 -> x20, local copies, waits for them, and re-layouts: 2.35 us -> 0.05 us
    pallas_call x1, Pallas kernels: 15.5 us -> 13.4 us  [local(): pl.pallas_call(blocks_kernel, out_shape=(jax.ShapeDtypeStruct((spare, 2 *...]
  transfers between devices with their start and end apart: 12 -> 12, of which waited for: 6 -> 6; matrix products, arithmetic and copies ran while one was open for 0% -> 0% of each run, Pallas kernels for 11% -> 13%
where the time goes in v2:
time: 73.3 us; the launch traced here: 72.4 us
  Pallas kernels  35.2 us (48%)
  starting transfers between devices  21.4 us (29%)
  waiting for transfers between devices  15.4 us (21%)
    ppermute x12, starting transfers between devices, from_behind(): lax.ppermute(array, axis, [(i, (i + by) % length) for i in range(length)])  21.4 us
    ppermute x12, waiting for transfers between devices, from_behind(): lax.ppermute(array, axis, [(i, (i + by) % length) for i in range(length)])  15.4 us
    pallas_call x1, Pallas kernels, local(): pl.pallas_call(blocks_kernel, out_shape=(jax.ShapeDtypeStruct((spare, 2 *...  13.4 us
    pallas_call x1, Pallas kernels, local(): pl.pallas_call(final_kernel, out_shape=jax.ShapeDtypeStruct((count, width...  9.54 us
    pallas_call x1, Pallas kernels, local(): pl.pallas_call(local_kernel, out_shape=jax.ShapeDtypeStruct((spare * 4, 1...  4.21 us
    pallas_call x1, Pallas kernels, local(): pl.pallas_call(trip_kernel, out_shape=jax.ShapeDtypeStruct((spare, 2 * tr...  3.06 us
    pallas_call x1, Pallas kernels, local(): pl.pallas_call(pack_kernel, out_shape=(jax.ShapeDtypeStruct((slab * 4, 12...  2.89 us
    pallas_call x1, Pallas kernels, local(): pl.pallas_call(prepare_kernel, out_shape=(jax.ShapeDtypeStruct((quarter,...  1.89 us
  transfers between devices with their start and end apart: 12, of which 6 were waited for; matrix products, arithmetic and copies ran while one was open for 0% of the time, Pallas kernels for 13%

profile of v2, /device:TPU:24, one launch (start us, length us, event | category | flops | bytes accessed | tf_op | source)
XLA Modules:
  0.0 72.4 jit_solution(9566724904655211826)
XLA Ops:
  0.0 2.9 %pack.1 = (bf16[1152,128]{1,0:T(8,128)(2,1)S(1)}, bf16[1152,128]{1,0:T(8,128)(2,1)S(1)}, bf16[1152,128]{1,0:T(8,128)(2,1)S(1)}) custom-call(s32[27,1,32]{2,1,0:T(1,128)} %bitcast.12, bf16[2048,512]{1,0:T(8,128)(2,1)} %rows_ref.3), custom_call_target="tpu_custom_call" | custom-call | tf_op jit(solution)/shard_map/pack/pallas_call | solution.py:489
  2.9 0.0 collective-permute-start
  2.9 5.3 %collective-permute-start.1 = (bf16[1152,128]{1,0:T(8,128)(2,1)S(1)}, bf16[1152,128]{1,0:T(8,128)(2,1)S(1)}, u32[]{:S(2)}, u32[]{:S(2)}) collective-permute-start(bf16[1152,128]{1,0:T(8,128)(2,1)S(1)} %get-tuple-element.35), channel_id=1, source_target_pairs={{0,240},{16,0},{32,16},{48,32},{64,48},{80,64},{96,80},{112,96},{1... | collective-permute-start | bytes 884744 | tf_op jit(solution)/shard_map/ppermute | solution.py:31
  8.2 4.4 %collective-permute-done.low_ref = bf16[1152,128]{1,0:T(8,128)(2,1)S(1)} collective-permute-done((bf16[1152,128]{1,0:T(8,128)(2,1)S(1)}, bf16[1152,128]{1,0:T(8,128)(2,1)S(1)}, u32[]{:S(2)}, u32[]{:S(2)}) %collective-permute-start) | collective-permute-done | bytes 294944 | tf_op jit(solution)/shard_map/ppermute | solution.py:31
  12.6 0.0 collective-permute-done.1.high_ref
  12.6 0.1 regroup.4
  12.7 1.6 %collective-permute-start.2 = (bf16[1152,128]{1,0:T(8,128)(2,1)S(1)}, bf16[1152,128]{1,0:T(8,128)(2,1)S(1)}, u32[]{:S(2)}, u32[]{:S(2)}) collective-permute-start(bf16[1152,128]{1,0:T(8,128)(2,1)S(1)} %get-tuple-element.36), channel_id=1, source_target_pairs={{0,4},{4,8},{8,12},{12,0},{1,5},{5,9},{9,13},{13,1},{2,6},{6,10},{... | collective-permute-start | bytes 884744 | tf_op jit(solution)/shard_map/ppermute | solution.py:31
  14.3 1.7 %collective-permute-start.3 = (bf16[1152,128]{1,0:T(8,128)(2,1)S(1)}, bf16[1152,128]{1,0:T(8,128)(2,1)S(1)}, u32[]{:S(2)}, u32[]{:S(2)}) collective-permute-start(bf16[1152,128]{1,0:T(8,128)(2,1)S(1)} %get-tuple-element.38), channel_id=1, source_target_pairs={{0,12},{4,0},{8,4},{12,8},{1,13},{5,1},{9,5},{13,9},{2,14},{6,2},{... | collective-permute-start | bytes 884744 | tf_op jit(solution)/shard_map/ppermute | solution.py:31
  16.0 5.7 %collective-permute-done.2.low_ref = bf16[1152,128]{1,0:T(8,128)(2,1)S(1)} collective-permute-done((bf16[1152,128]{1,0:T(8,128)(2,1)S(1)}, bf16[1152,128]{1,0:T(8,128)(2,1)S(1)}, u32[]{:S(2)}, u32[]{:S(2)}) %collective-permute-start.2) | collective-permute-done | bytes 294944 | tf_op jit(solution)/shard_map/ppermute | solution.py:31
  21.7 0.1 regroup.5
  21.7 0.3 collective-permute-start.4
  22.0 0.0 copy-start.5
  22.0 0.0 copy-start.6
  22.1 0.0 copy-start.7
  22.1 0.0 copy-start.9
  22.1 2.1 %collective-permute-start.5 = (bf16[1152,128]{1,0:T(8,128)(2,1)S(1)}, bf16[1152,128]{1,0:T(8,128)(2,1)S(1)}, u32[]{:S(2)}, u32[]{:S(2)}) collective-permute-start(bf16[1152,128]{1,0:T(8,128)(2,1)S(1)} %get-tuple-element.41), channel_id=1, source_target_pairs={{0,3},{1,0},{2,1},{3,2},{4,7},{5,4},{6,5},{7,6},{8,11},{9,8},{10,9... | collective-permute-start | bytes 884744 | tf_op jit(solution)/shard_map/ppermute | solution.py:31
  24.2 4.2 %reverse_local.1.reverse_ref = f32[8224,128]{1,0:T(8,128)S(1)} custom-call(s32[2048]{0:T(1024)S(1)} %copy-done.8, bf16[2048,512]{1,0:T(8,128)(2,1)S(1)} %copy-done), custom_call_target="tpu_custom_call" | custom-call | tf_op jit(solution)/shard_map/reverse_local/pallas_call | solution.py:537
  28.4 1.9 %prepare.1 = (bf16[512,128]{1,0:T(8,128)(2,1)S(1)}, bf16[512,128]{1,0:T(8,128)(2,1)S(1)}, bf16[2,4096,256]{2,1,0:T(8,128)(2,1)S(1)}, bf16[2,64,512]{2,1,0:T(8,12...) custom-call(f32[32,2048]{1,0:T(8,128)S(1)} %bitcast.6, ...), custom_call_target="tpu_custom_call" | custom-call | tf_op jit(solution)/shard_map/prepare/pallas_call | solution.py:508
  30.3 0.0 collective-permute-done.4.low_ref
  30.4 13.4 %blocks.1 = (f32[2056,128]{1,0:T(8,128)S(1)}, bf16[288,128]{1,0:T(8,128)(2,1)S(1)}, bf16[288,128]{1,0:T(8,128)(2,1)S(1)}, bf16[288,128]{1,0:T(8,128)(2,1)S(1)}) custom-call(s32[27,1,32]{2,1,0:T(1,128)S(1)} %get-tuple-element.32.send_ref, bf16[1152,128]{1,0:T(8,128)(2,1)S(1)} %collective-permute-done.4.low_ref, ...), custom_call_target="tpu_custom_call" | custom-call | tf_op jit(solution)/shard_map/blocks/pallas_call | solution.py:547
  43.8 0.0 collective-permute-start.6
  43.8 5.0 %collective-permute-start.7 = (bf16[288,128]{1,0:T(8,128)(2,1)S(1)}, bf16[288,128]{1,0:T(8,128)(2,1)S(1)}, u32[]{:S(2)}, u32[]{:S(2)}) collective-permute-start(bf16[288,128]{1,0:T(8,128)(2,1)S(1)} %get-tuple-element.51), channel_id=1, source_target_pairs={{0,240},{16,0},{32,16},{48,32},{64,48},{80,64},{96,80},{112,96},{1... | collective-permute-start | bytes 221192 | tf_op jit(solution)/shard_map/ppermute | solution.py:31
  48.8 2.0 %collective-permute-done.6.low_ref = bf16[288,128]{1,0:T(8,128)(2,1)S(1)} collective-permute-done((bf16[288,128]{1,0:T(8,128)(2,1)S(1)}, bf16[288,128]{1,0:T(8,128)(2,1)S(1)}, u32[]{:S(2)}, u32[]{:S(2)}) %collective-permute-start.6) | collective-permute-done | bytes 73760 | tf_op jit(solution)/shard_map/ppermute | solution.py:31
  50.8 1.6 %collective-permute-start.8 = (bf16[288,128]{1,0:T(8,128)(2,1)S(1)}, bf16[288,128]{1,0:T(8,128)(2,1)S(1)}, u32[]{:S(2)}, u32[]{:S(2)}) collective-permute-start(bf16[288,128]{1,0:T(8,128)(2,1)S(1)} %get-tuple-element.52), channel_id=1, source_target_pairs={{0,4},{4,8},{8,12},{12,0},{1,5},{5,9},{9,13},{13,1},{2,6},{6,10},{... | collective-permute-start | bytes 221192 | tf_op jit(solution)/shard_map/ppermute | solution.py:31
  52.4 1.8 %collective-permute-start.9 = (bf16[288,128]{1,0:T(8,128)(2,1)S(1)}, bf16[288,128]{1,0:T(8,128)(2,1)S(1)}, u32[]{:S(2)}, u32[]{:S(2)}) collective-permute-start(bf16[288,128]{1,0:T(8,128)(2,1)S(1)} %get-tuple-element.54), channel_id=1, source_target_pairs={{0,12},{4,0},{8,4},{12,8},{1,13},{5,1},{9,5},{13,9},{2,14},{6,2},{... | collective-permute-start | bytes 221192 | tf_op jit(solution)/shard_map/ppermute | solution.py:31
  54.2 2.3 %collective-permute-done.8.low_ref = bf16[288,128]{1,0:T(8,128)(2,1)S(1)} collective-permute-done((bf16[288,128]{1,0:T(8,128)(2,1)S(1)}, bf16[288,128]{1,0:T(8,128)(2,1)S(1)}, u32[]{:S(2)}, u32[]{:S(2)}) %collective-permute-start.8) | collective-permute-done | bytes 73760 | tf_op jit(solution)/shard_map/ppermute | solution.py:31
  56.5 0.3 collective-permute-done.9.high_ref
  56.8 0.3 collective-permute-start.10
  57.0 1.9 %collective-permute-start.11 = (bf16[288,128]{1,0:T(8,128)(2,1)S(1)}, bf16[288,128]{1,0:T(8,128)(2,1)S(1)}, u32[]{:S(2)}, u32[]{:S(2)}) collective-permute-start(bf16[288,128]{1,0:T(8,128)(2,1)S(1)} %get-tuple-element.57), channel_id=1, source_target_pairs={{0,3},{1,0},{2,1},{3,2},{4,7},{5,4},{6,5},{7,6},{8,11},{9,8},{10,9... | collective-permute-start | bytes 221192 | tf_op jit(solution)/shard_map/ppermute | solution.py:31
  58.9 3.1 %trip_local.1.trip_ref = f32[2056,128]{1,0:T(8,128)S(1)} custom-call(s32[2048]{0:T(1024)S(1)} %copy-done.8, f32[2056,128]{1,0:T(8,128)S(1)} %get-tuple-element.58.trip_ref), custom_call_target="tpu_custom_call" | custom-call | tf_op jit(solution)/shard_map/trip_local/pallas_call | solution.py:578
  62.0 0.8 %collective-permute-done.11.high_ref = bf16[288,128]{1,0:T(8,128)(2,1)S(1)} collective-permute-done((bf16[288,128]{1,0:T(8,128)(2,1)S(1)}, bf16[288,128]{1,0:T(8,128)(2,1)S(1)}, u32[]{:S(2)}, u32[]{:S(2)}) %collective-permute-start.11) | collective-permute-done | bytes 73760 | tf_op jit(solution)/shard_map/ppermute | solution.py:31
  62.7 9.5 %final.1 = bf16[2048,512]{1,0:T(8,128)(2,1)} custom-call(s32[27,1,32]{2,1,0:T(1,128)S(1)} %get-tuple-element.32.send_ref, bf16[288,128]{1,0:T(8,128)(2,1)S(1)} %collective-permute-done.10.low_ref, bf16[288,128]{1,0:T(8,128)(2,1)S(1)} %get-tuple-element.56.middle_ref, bf16[288,128]{1,0:T(8,128)(2,1)S(1)} %collective-permute-done.11.high_ref, ...), custom_call_target="tpu_custom_call" | custom-call | tf_op jit(solution)/shard_map/final/pallas_call | solution.py:588
  (22 shorter events, 0.1 us)
Async XLA Ops:
  0.0 24.1 %copy-start = (bf16[2048,512]{1,0:T(8,128)(2,1)S(1)}, bf16[2048,512]{1,0:T(8,128)(2,1)}, u32[]{:S(2)}) copy-start(bf16[2048,512]{1,0:T(8,128)(2,1)} %rows_ref.3) | copy-start | bytes 6291460
  0.0 24.1 %copy-start.8 = (s32[2048]{0:T(1024)S(1)}, s32[2048]{0:T(1024)}, u32[]{:S(2)}) copy-start(s32[2048]{0:T(1024)} %fetch_ref.3) | copy-start | bytes 24580
  2.9 9.7 %collective-permute-start = (bf16[1152,128]{1,0:T(8,128)(2,1)S(1)}, bf16[1152,128]{1,0:T(8,128)(2,1)S(1)}, u32[]{:S(2)}, u32[]{:S(2)}) collective-permute-start(bf16[1152,128]{1,0:T(8,128)(2,1)S(1)} %get-tuple-element.33), channel_id=1, source_target_pairs={{0,16},{16,32},{32,48},{48,64},{64,80},{80,96},{96,112},{112,128},... | collective-permute-start | bytes 884744 | tf_op jit(solution)/shard_map/ppermute | solution.py:31
  2.9 9.7 %collective-permute-start.1 = (bf16[1152,128]{1,0:T(8,128)(2,1)S(1)}, bf16[1152,128]{1,0:T(8,128)(2,1)S(1)}, u32[]{:S(2)}, u32[]{:S(2)}) collective-permute-start(bf16[1152,128]{1,0:T(8,128)(2,1)S(1)} %get-tuple-element.35), channel_id=1, source_target_pairs={{0,240},{16,0},{32,16},{48,32},{64,48},{80,64},{96,80},{112,96},{1... | collective-permute-start | bytes 884744 | tf_op jit(solution)/shard_map/ppermute | solution.py:31
  12.7 9.0 %collective-permute-start.2 = (bf16[1152,128]{1,0:T(8,128)(2,1)S(1)}, bf16[1152,128]{1,0:T(8,128)(2,1)S(1)}, u32[]{:S(2)}, u32[]{:S(2)}) collective-permute-start(bf16[1152,128]{1,0:T(8,128)(2,1)S(1)} %get-tuple-element.36), channel_id=1, source_target_pairs={{0,4},{4,8},{8,12},{12,0},{1,5},{5,9},{9,13},{13,1},{2,6},{6,10},{... | collective-permute-start | bytes 884744 | tf_op jit(solution)/shard_map/ppermute | solution.py:31
  14.3 7.4 %collective-permute-start.3 = (bf16[1152,128]{1,0:T(8,128)(2,1)S(1)}, bf16[1152,128]{1,0:T(8,128)(2,1)S(1)}, u32[]{:S(2)}, u32[]{:S(2)}) collective-permute-start(bf16[1152,128]{1,0:T(8,128)(2,1)S(1)} %get-tuple-element.38), channel_id=1, source_target_pairs={{0,12},{4,0},{8,4},{12,8},{1,13},{5,1},{9,5},{13,9},{2,14},{6,2},{... | collective-permute-start | bytes 884744 | tf_op jit(solution)/shard_map/ppermute | solution.py:31
  21.7 8.6 %collective-permute-start.4 = (bf16[1152,128]{1,0:T(8,128)(2,1)S(1)}, bf16[1152,128]{1,0:T(8,128)(2,1)S(1)}, u32[]{:S(2)}, u32[]{:S(2)}) collective-permute-start(bf16[1152,128]{1,0:T(8,128)(2,1)S(1)} %get-tuple-element.39), channel_id=1, source_target_pairs={{0,1},{1,2},{2,3},{3,0},{4,5},{5,6},{6,7},{7,4},{8,9},{9,10},{10,1... | collective-permute-start | bytes 884744 | tf_op jit(solution)/shard_map/ppermute | solution.py:31
  22.0 6.3 %copy-start.1 = (bf16[2,512,512]{2,1,0:T(8,128)(2,1)S(1)}, bf16[2,512,512]{2,1,0:T(8,128)(2,1)}, u32[]{:S(2)}) copy-start(bf16[2,512,512]{2,1,0:T(8,128)(2,1)} %first_ref.1) | copy-start | bytes 3145732
  22.0 6.4 %copy-start.2 = (bf16[2,512,512]{2,1,0:T(8,128)(2,1)S(1)}, bf16[2,512,512]{2,1,0:T(8,128)(2,1)}, u32[]{:S(2)}) copy-start(bf16[2,512,512]{2,1,0:T(8,128)(2,1)} %second_ref.1) | copy-start | bytes 3145732
  22.0 6.4 %copy-start.3 = (f32[2048,32]{0,1:T(8,128)S(1)}, f32[2048,32]{0,1:T(8,128)}, u32[]{:S(2)}) copy-start(f32[2048,32]{0,1:T(8,128)} %param.11) | copy-start | bytes 786436
  22.0 6.4 %copy-start.4 = (s32[2048,32]{0,1:T(8,128)S(1)}, s32[2048,32]{0,1:T(8,128)}, u32[]{:S(2)}) copy-start(s32[2048,32]{0,1:T(8,128)} %param.12) | copy-start | bytes 786436
  22.0 6.4 %copy-start.5 = (bf16[2,1024,64]{1,2,0:T(8,128)(2,1)S(1)}, bf16[2,1024,64]{1,2,0:T(8,128)(2,1)}, u32[]{:S(2)}) copy-start(bf16[2,1024,64]{1,2,0:T(8,128)(2,1)} %param.16) | copy-start | bytes 786436
  22.0 6.4 %copy-start.6 = (bf16[2,64,512]{2,1,0:T(8,128)(2,1)S(1)}, bf16[2,64,512]{2,1,0:T(8,128)(2,1)}, u32[]{:S(2)}) copy-start(bf16[2,64,512]{2,1,0:T(8,128)(2,1)} %up_ref.1) | copy-start | bytes 393220
  22.1 6.4 %copy-start.7 = (bf16[2,512,64]{1,2,0:T(8,128)(2,1)S(1)}, bf16[2,512,64]{1,2,0:T(8,128)(2,1)}, u32[]{:S(2)}) copy-start(bf16[2,512,64]{1,2,0:T(8,128)(2,1)} %param.15) | copy-start | bytes 393220
  22.1 6.4 %copy-start.9 = (s32[1,1,1,27,32]{4,2,3,1,0:T(1,128)S(1)}, s32[1,1,1,27,32]{4,2,3,1,0:T(1,128)}, u32[]{:S(2)}) copy-start(s32[1,1,1,27,32]{4,2,3,1,0:T(1,128)} %param.13) | copy-start | bytes 10372
  22.1 8.3 %collective-permute-start.5 = (bf16[1152,128]{1,0:T(8,128)(2,1)S(1)}, bf16[1152,128]{1,0:T(8,128)(2,1)S(1)}, u32[]{:S(2)}, u32[]{:S(2)}) collective-permute-start(bf16[1152,128]{1,0:T(8,128)(2,1)S(1)} %get-tuple-element.41), channel_id=1, source_target_pairs={{0,3},{1,0},{2,1},{3,2},{4,7},{5,4},{6,5},{7,6},{8,11},{9,8},{10,9... | collective-permute-start | bytes 884744 | tf_op jit(solution)/shard_map/ppermute | solution.py:31
  43.8 7.0 %collective-permute-start.6 = (bf16[288,128]{1,0:T(8,128)(2,1)S(1)}, bf16[288,128]{1,0:T(8,128)(2,1)S(1)}, u32[]{:S(2)}, u32[]{:S(2)}) collective-permute-start(bf16[288,128]{1,0:T(8,128)(2,1)S(1)} %get-tuple-element.49), channel_id=1, source_target_pairs={{0,16},{16,32},{32,48},{48,64},{64,80},{80,96},{96,112},{112,128},... | collective-permute-start | bytes 221192 | tf_op jit(solution)/shard_map/ppermute | solution.py:31
  43.8 7.0 %collective-permute-start.7 = (bf16[288,128]{1,0:T(8,128)(2,1)S(1)}, bf16[288,128]{1,0:T(8,128)(2,1)S(1)}, u32[]{:S(2)}, u32[]{:S(2)}) collective-permute-start(bf16[288,128]{1,0:T(8,128)(2,1)S(1)} %get-tuple-element.51), channel_id=1, source_target_pairs={{0,240},{16,0},{32,16},{48,32},{64,48},{80,64},{96,80},{112,96},{1... | collective-permute-start | bytes 221192 | tf_op jit(solution)/shard_map/ppermute | solution.py:31
  50.8 5.6 %collective-permute-start.8 = (bf16[288,128]{1,0:T(8,128)(2,1)S(1)}, bf16[288,128]{1,0:T(8,128)(2,1)S(1)}, u32[]{:S(2)}, u32[]{:S(2)}) collective-permute-start(bf16[288,128]{1,0:T(8,128)(2,1)S(1)} %get-tuple-element.52), channel_id=1, source_target_pairs={{0,4},{4,8},{8,12},{12,0},{1,5},{5,9},{9,13},{13,1},{2,6},{6,10},{... | collective-permute-start | bytes 221192 | tf_op jit(solution)/shard_map/ppermute | solution.py:31
  52.4 4.4 %collective-permute-start.9 = (bf16[288,128]{1,0:T(8,128)(2,1)S(1)}, bf16[288,128]{1,0:T(8,128)(2,1)S(1)}, u32[]{:S(2)}, u32[]{:S(2)}) collective-permute-start(bf16[288,128]{1,0:T(8,128)(2,1)S(1)} %get-tuple-element.54), channel_id=1, source_target_pairs={{0,12},{4,0},{8,4},{12,8},{1,13},{5,1},{9,5},{13,9},{2,14},{6,2},{... | collective-permute-start | bytes 221192 | tf_op jit(solution)/shard_map/ppermute | solution.py:31
  56.8 5.2 %collective-permute-start.10 = (bf16[288,128]{1,0:T(8,128)(2,1)S(1)}, bf16[288,128]{1,0:T(8,128)(2,1)S(1)}, u32[]{:S(2)}, u32[]{:S(2)}) collective-permute-start(bf16[288,128]{1,0:T(8,128)(2,1)S(1)} %get-tuple-element.55), channel_id=1, source_target_pairs={{0,1},{1,2},{2,3},{3,0},{4,5},{5,6},{6,7},{7,4},{8,9},{9,10},{10,1... | collective-permute-start | bytes 221192 | tf_op jit(solution)/shard_map/ppermute | solution.py:31
  57.0 5.7 %collective-permute-start.11 = (bf16[288,128]{1,0:T(8,128)(2,1)S(1)}, bf16[288,128]{1,0:T(8,128)(2,1)S(1)}, u32[]{:S(2)}, u32[]{:S(2)}) collective-permute-start(bf16[288,128]{1,0:T(8,128)(2,1)S(1)} %get-tuple-element.57), channel_id=1, source_target_pairs={{0,3},{1,0},{2,1},{3,2},{4,7},{5,4},{6,5},{7,6},{8,11},{9,8},{10,9... | collective-permute-start | bytes 221192 | tf_op jit(solution)/shard_map/ppermute | solution.py:31

commit v3 on v2

--- a/solution.py
+++ b/solution.py
@@ -102,15 +102,17 @@
     return jnp.minimum(fetch_ref[edge].astype(jnp.uint32), jnp.uint32(spare)).astype(jnp.int32)
 
 
-def for_slots(send_ref, step):
+def for_slots(send_ref, step, thirds=(0, 1, 2)):
     directions, _, each = send_ref.shape
 
-    def body(t, carry):
-        for r in range(each):
-            step(t, r, t * each + r)
+    def body(i, carry):
+        for c in thirds:
+            t = 3 * i + c
+            for r in range(each):
+                step(t, r, t * each + r)
         return carry
 
-    lax.fori_loop(0, directions, body, 0)
+    lax.fori_loop(0, directions // 3, body, 0)
 
 
 def pack_kernel(
@@ -157,7 +159,12 @@
         out_ref[...] = packed_ref[slab * i : slab * (i + 1), :].astype(BF16)
 
 
-def local_kernel(fetch_ref, rows_ref, out_ref, wide_ref):
+def place_wide(send_ref, arrived_ref, rows_ref, t, r, s):
+    target = pl.multiple_of(send_ref[t, 0, r] * 4, 4)
+    rows_ref[pl.ds(target, 4), :] = arrived_ref[pl.ds(pl.multiple_of(s * 4, 4), 4), :]
+
+
+def local_kernel(fetch_ref, send_ref, middle_ref, rows_ref, out_ref, wide_ref, arrived32_ref):
     count = rows_ref.shape[0]
     for start in range(0, count, 256):
         spread_rows(rows_ref, wide_ref, start, 256)
@@ -172,10 +179,12 @@
         return carry
 
     lax.fori_loop(0, count // unroll, body, 0)
+    widen_arrived(((1, middle_ref),), arrived32_ref)
+    for_slots(send_ref, lambda t, r, s: place_wide(send_ref, arrived32_ref, out_ref, t, r, s), (1,))
 
 
 def widen_arrived(pieces, wide_ref):
-    for c, piece in enumerate(pieces):
+    for c, piece in pieces:
         rows = piece.shape[0] // 9
         for i in range(9):
             start = rows * (9 * (i % 3) + 3 * (i // 3) + c)
@@ -183,9 +192,8 @@
 
 
 def blocks_kernel(
-    send_ref,
+    send_hbm_ref,
     low_ref,
-    middle_ref,
     high_ref,
     reverse_ref,
     weight_ref,
@@ -206,18 +214,22 @@
     packed_ref,
     mixed_ref,
     inner_ref,
+    send_ref,
+    listed,
 ):
     count = rows_ref.shape[0]
     groups = summed_ref.shape[0] // 32
     trip = up_ref.shape[1]
     angular = summed_ref.shape[1] // 256
-    widen_arrived((low_ref, middle_ref, high_ref), arrived32_ref)
-
-    def place(t, r, s):
-        target = pl.multiple_of(send_ref[t, 0, r] * 4, 4)
-        reverse_ref[pl.ds(target, 4), :] = arrived32_ref[pl.ds(pl.multiple_of(s * 4, 4), 4), :]
-
-    for_slots(send_ref, place)
+    listing = pltpu.make_async_copy(send_hbm_ref, send_ref, listed)
+    listing.start()
+    widen_arrived(((0, low_ref), (2, high_ref)), arrived32_ref)
+    listing.wait()
+    for_slots(
+        send_ref,
+        lambda t, r, s: place_wide(send_ref, arrived32_ref, reverse_ref, t, r, s),
+        (0, 2),
+    )
     for start in range(0, count, 256):
         for c in range(4):
             rows_ref[start : start + 256, 128 * c : 128 * (c + 1)] = reverse_ref[
@@ -287,23 +299,42 @@
         out_ref[...] = packed_ref[slab * i : slab * (i + 1), :].astype(BF16)
 
 
-def trip_kernel(fetch_ref, trip_ref, out_ref):
-    count = fetch_ref.shape[0]
+def gather_trips(fetch_ref, trip_ref, out_ref, start, count, spare):
     unroll = 32
 
     def body(i, carry):
         for k in range(unroll):
-            edge = i * unroll + k
-            out_ref[pl.ds(edge, 1), :] = trip_ref[pl.ds(local_edge(fetch_ref, edge, count), 1), :]
+            edge = start + i * unroll + k
+            out_ref[pl.ds(edge, 1), :] = trip_ref[pl.ds(local_edge(fetch_ref, edge, spare), 1), :]
         return carry
 
     lax.fori_loop(0, count // unroll, body, 0)
 
 
+def trip_kernel(fetch_ref, trip_ref, out_ref):
+    gather_trips(fetch_ref, trip_ref, out_ref, 0, out_ref.shape[0], fetch_ref.shape[0])
+
+
+def trip_rest_kernel(fetch_ref, trip_ref, begun_ref, out_ref):
+    count = fetch_ref.shape[0]
+    done = begun_ref.shape[0]
+    out_ref[0:done, :] = begun_ref[...]
+    gather_trips(fetch_ref, trip_ref, out_ref, done, count - done, count)
+
+
+def trip_middle_kernel(send_ref, middle_ref, begun_ref, out_ref, arrived32_ref):
+    out_ref[...] = begun_ref[...]
+    widen_arrived(((1, middle_ref),), arrived32_ref)
+
+    def place(t, r, s):
+        out_ref[pl.ds(send_ref[t, 0, r], 1), :] = arrived32_ref[pl.ds(s, 1), :]
+
+    for_slots(send_ref, place, (1,))
+
+
 def final_kernel(
-    send_ref,
+    send_hbm_ref,
     low_ref,
-    middle_ref,
     high_ref,
     trip_ref,
     rows_ref,
@@ -320,15 +351,20 @@
     rows_out_ref,
     mask_ref,
     copied,
+    send_ref,
+    listed,
 ):
     count = rows_ref.shape[0]
     trip = up_ref.shape[1]
-    widen_arrived((low_ref, middle_ref, high_ref), arrived32_ref)
+    listing = pltpu.make_async_copy(send_hbm_ref, send_ref, listed)
+    listing.start()
+    widen_arrived(((0, low_ref), (2, high_ref)), arrived32_ref)
+    listing.wait()
 
     def place(t, r, s):
         trip_ref[pl.ds(send_ref[t, 0, r], 1), :] = arrived32_ref[pl.ds(s, 1), :]
 
-    for_slots(send_ref, place)
+    for_slots(send_ref, place, (0, 2))
     step = 256
 
     def lifted(at, block):
@@ -337,9 +373,8 @@
 
     def lift(i):
         at = span(i, step)
-        for h in range(step // 128):
-            g = i * (step // 128) + h
-            line = live_ref[pl.ds(g, 1), :].astype(F32)
+        for g in range(i * (step // 128), (i + 1) * (step // 128)):
+            line = live_ref[g : g + 1, :].astype(F32)
             mask_ref[span(g, 128), :] = jnp.broadcast_to(line, (128, 128)).T
         rows = rows_ref[at, :].astype(F32)
         mixed_ref[at, :] = ((rows + lifted(at, 0)) * HALF_ROOT).astype(BF16)
@@ -532,17 +567,21 @@
         down_turned,
         senders,
     )
+    hbm_slots = pltpu.with_memory_space_constraint(own_slots, pltpu.HBM)
     arrived = exchange(packed)
 
     reverse = pl.pallas_call(
         local_kernel,
         out_shape=jax.ShapeDtypeStruct((spare * 4, 128), F32),
-        in_specs=[smem, vmem],
+        in_specs=[smem, smem, vmem, vmem],
         out_specs=vmem,
-        scratch_shapes=[pltpu.VMEM((spare * 4, 128), F32)],
-        compiler_params=params(14),
+        scratch_shapes=[
+            pltpu.VMEM((spare * 4, 128), F32),
+            pltpu.VMEM((slots * 4, 128), F32),
+        ],
+        compiler_params=params(16),
         name="reverse_local",
-    )(fetch_index, edge_state)
+    )(fetch_index, own_slots, arrived[1], edge_state)
 
     triplet, *sending = pl.pallas_call(
         blocks_kernel,
@@ -550,7 +589,7 @@
             jax.ShapeDtypeStruct((spare, 2 * trip), F32),
         )
         + (jax.ShapeDtypeStruct((slab, 2 * trip), BF16),) * 3,
-        in_specs=[smem] + [vmem] * 11,
+        in_specs=[outside] + [vmem] * 10,
         out_specs=(vmem,) * 4,
         scratch_shapes=[
             pltpu.VMEM((slots * 4, 128), F32),
@@ -560,12 +599,15 @@
             pltpu.VMEM((slots, 2 * trip), F32),
             pltpu.VMEM((count, width), BF16),
             pltpu.VMEM((count, width), BF16),
+            pltpu.SMEM(senders.shape, jnp.int32),
+            pltpu.SemaphoreType.DMA,
         ],
         compiler_params=params(32),
         name="blocks",
     )(
-        own_slots,
-        *arrived,
+        hbm_slots,
+        arrived[0],
+        arrived[2],
         reverse,
         weights,
         bins,
@@ -575,30 +617,52 @@
         first_half,
         second_half,
     )
+    carried = exchange(sending)
     own_trip = pl.pallas_call(
         trip_kernel,
-        out_shape=jax.ShapeDtypeStruct((spare, 2 * trip), F32),
+        out_shape=jax.ShapeDtypeStruct((count // 2, 2 * trip), F32),
         in_specs=[smem, vmem],
         out_specs=vmem,
         compiler_params=params(5),
         name="trip_local",
     )(fetch_index, triplet)
-    carried = exchange(sending)
+    own_trip = pl.pallas_call(
+        trip_rest_kernel,
+        out_shape=jax.ShapeDtypeStruct((spare, 2 * trip), F32),
+        in_specs=[smem, vmem, vmem],
+        out_specs=vmem,
+        compiler_params=params(5),
+        name="trip_rest",
+    )(fetch_index, triplet, own_trip)
+    own_trip = pl.pallas_call(
+        trip_middle_kernel,
+        out_shape=jax.ShapeDtypeStruct((spare, 2 * trip), F32),
+        in_specs=[smem, vmem, vmem],
+        out_specs=vmem,
+        scratch_shapes=[pltpu.VMEM((slots, 2 * trip), F32)],
+        compiler_params=params(5),
+        name="trip_middle",
+    )(own_slots, carried[1], own_trip)
 
     out = pl.pallas_call(
         final_kernel,
         out_shape=jax.ShapeDtypeStruct((count, width), BF16),
-        in_specs=[smem] + [vmem] * 9,
+        in_specs=[outside] + [vmem] * 8,
         out_specs=outside,
         scratch_shapes=[pltpu.VMEM((slots, 2 * trip), F32)]
         + [pltpu.VMEM((count, width), BF16)] * 5
         + [pltpu.VMEM((count, 128), F32)]
-        + [pltpu.SemaphoreType.DMA((8,))],
+        + [
+            pltpu.SemaphoreType.DMA((8,)),
+            pltpu.SMEM(senders.shape, jnp.int32),
+            pltpu.SemaphoreType.DMA,
+        ],
         compiler_params=params(24),
         name="final",
     )(
-        own_slots,
-        *carried,
+        hbm_slots,
+        carried[0],
+        carried[2],
         own_trip,
         edge_state,
         live_lines,

time: 73.3 us -> 75.1 us (1.025)
  the two profiles are of different devices: /device:TPU:24 before, /device:TPU:6 now
where the time goes in v3:
time: 75.1 us; the launch traced here: 74.8 us
  Pallas kernels  37 us (49%)
  starting transfers between devices  20.1 us (27%)
  waiting for transfers between devices  17.3 us (23%)
    ppermute x12, starting transfers between devices, from_behind(): lax.ppermute(array, axis, [(i, (i + by) % length) for i in range(length)])  20.1 us
    ppermute x12, waiting for transfers between devices, from_behind(): lax.ppermute(array, axis, [(i, (i + by) % length) for i in range(length)])  17.3 us
    pallas_call x1, Pallas kernels, local(): pl.pallas_call(blocks_kernel, out_shape=(jax.ShapeDtypeStruct((spare, 2 *...  13 us
    pallas_call x1, Pallas kernels, local(): pl.pallas_call(final_kernel, out_shape=jax.ShapeDtypeStruct((count, width...  9.4 us
    pallas_call x1, Pallas kernels, local(): pl.pallas_call(local_kernel, out_shape=jax.ShapeDtypeStruct((spare * 4, 1...  4.8 us
    pallas_call x1, Pallas kernels, local(): pl.pallas_call(pack_kernel, out_shape=(jax.ShapeDtypeStruct((slab * 4, 12...  2.83 us
    pallas_call x1, Pallas kernels, local(): pl.pallas_call(trip_rest_kernel, out_shape=jax.ShapeDtypeStruct((spare, 2...  1.9 us
    pallas_call x1, Pallas kernels, local(): pl.pallas_call(prepare_kernel, out_shape=(jax.ShapeDtypeStruct((quarter,...  1.89 us
  transfers between devices with their start and end apart: 12, of which 6 were waited for; matrix products, arithmetic and copies ran while one was open for 0% of the time, Pallas kernels for 15%

profile of v3, /device:TPU:6, one launch (start us, length us, event | category | flops | bytes accessed | tf_op | source)
XLA Modules:
  0.0 74.8 jit_solution(7414877442780706409)
XLA Ops:
  0.1 2.8 %pack.1 = (bf16[1152,128]{1,0:T(8,128)(2,1)S(1)}, bf16[1152,128]{1,0:T(8,128)(2,1)S(1)}, bf16[1152,128]{1,0:T(8,128)(2,1)S(1)}) custom-call(s32[27,1,32]{2,1,0:T(1,128)} %bitcast.12, bf16[2048,512]{1,0:T(8,128)(2,1)} %rows_ref.3), custom_call_target="tpu_custom_call" | custom-call | tf_op jit(solution)/shard_map/pack/pallas_call | solution.py:524
  2.9 0.0 collective-permute-start
  2.9 5.3 %collective-permute-start.1 = (bf16[1152,128]{1,0:T(8,128)(2,1)S(1)}, bf16[1152,128]{1,0:T(8,128)(2,1)S(1)}, u32[]{:S(2)}, u32[]{:S(2)}) collective-permute-start(bf16[1152,128]{1,0:T(8,128)(2,1)S(1)} %get-tuple-element.35), channel_id=1, source_target_pairs={{0,240},{16,0},{32,16},{48,32},{64,48},{80,64},{96,80},{112,96},{1... | collective-permute-start | bytes 884744 | tf_op jit(solution)/shard_map/ppermute | solution.py:31
  8.2 4.4 %collective-permute-done.low_ref = bf16[1152,128]{1,0:T(8,128)(2,1)S(1)} collective-permute-done((bf16[1152,128]{1,0:T(8,128)(2,1)S(1)}, bf16[1152,128]{1,0:T(8,128)(2,1)S(1)}, u32[]{:S(2)}, u32[]{:S(2)}) %collective-permute-start) | collective-permute-done | bytes 294944 | tf_op jit(solution)/shard_map/ppermute | solution.py:31
  12.6 0.0 collective-permute-done.1.high_ref
  12.6 0.1 regroup.4
  12.7 0.0 copy-start
  12.7 0.6 collective-permute-start.2
  13.3 1.5 %collective-permute-start.3 = (bf16[1152,128]{1,0:T(8,128)(2,1)S(1)}, bf16[1152,128]{1,0:T(8,128)(2,1)S(1)}, u32[]{:S(2)}, u32[]{:S(2)}) collective-permute-start(bf16[1152,128]{1,0:T(8,128)(2,1)S(1)} %get-tuple-element.38), channel_id=1, source_target_pairs={{0,12},{4,0},{8,4},{12,8},{1,13},{5,1},{9,5},{13,9},{2,14},{6,2},{... | collective-permute-start | bytes 884744 | tf_op jit(solution)/shard_map/ppermute | solution.py:31
  14.8 5.7 %collective-permute-done.2.low_ref = bf16[1152,128]{1,0:T(8,128)(2,1)S(1)} collective-permute-done((bf16[1152,128]{1,0:T(8,128)(2,1)S(1)}, bf16[1152,128]{1,0:T(8,128)(2,1)S(1)}, u32[]{:S(2)}, u32[]{:S(2)}) %collective-permute-start.2) | collective-permute-done | bytes 294944 | tf_op jit(solution)/shard_map/ppermute | solution.py:31
  20.5 1.4 %collective-permute-done.3.high_ref = bf16[1152,128]{1,0:T(8,128)(2,1)S(1)} collective-permute-done((bf16[1152,128]{1,0:T(8,128)(2,1)S(1)}, bf16[1152,128]{1,0:T(8,128)(2,1)S(1)}, u32[]{:S(2)}, u32[]{:S(2)}) %collective-permute-start.3) | collective-permute-done | bytes 294944 | tf_op jit(solution)/shard_map/ppermute | solution.py:31
  21.9 0.1 regroup.5
  21.9 1.7 %collective-permute-start.4 = (bf16[1152,128]{1,0:T(8,128)(2,1)S(1)}, bf16[1152,128]{1,0:T(8,128)(2,1)S(1)}, u32[]{:S(2)}, u32[]{:S(2)}) collective-permute-start(bf16[1152,128]{1,0:T(8,128)(2,1)S(1)} %get-tuple-element.39), channel_id=1, source_target_pairs={{0,1},{1,2},{2,3},{3,0},{4,5},{5,6},{6,7},{7,4},{8,9},{9,10},{10,1... | collective-permute-start | bytes 884744 | tf_op jit(solution)/shard_map/ppermute | solution.py:31
  23.6 1.7 %collective-permute-start.5 = (bf16[1152,128]{1,0:T(8,128)(2,1)S(1)}, bf16[1152,128]{1,0:T(8,128)(2,1)S(1)}, u32[]{:S(2)}, u32[]{:S(2)}) collective-permute-start(bf16[1152,128]{1,0:T(8,128)(2,1)S(1)} %get-tuple-element.40), channel_id=1, source_target_pairs={{0,3},{1,0},{2,1},{3,2},{4,7},{5,4},{6,5},{7,6},{8,11},{9,8},{10,9... | collective-permute-start | bytes 884744 | tf_op jit(solution)/shard_map/ppermute | solution.py:31
  25.4 1.9 %prepare.1 = (bf16[512,128]{1,0:T(8,128)(2,1)S(1)}, bf16[512,128]{1,0:T(8,128)(2,1)S(1)}, bf16[2,4096,256]{2,1,0:T(8,128)(2,1)S(1)}, bf16[2,64,512]{2,1,0:T(8,12...) custom-call(f32[32,2048]{1,0:T(8,128)S(1)} %bitcast.6, ...), custom_call_target="tpu_custom_call" | custom-call | tf_op jit(solution)/shard_map/prepare/pallas_call | solution.py:543
  27.3 4.8 %reverse_local.1.reverse_ref = f32[8224,128]{1,0:T(8,128)S(1)} custom-call(s32[2048]{0:T(1024)S(1)} %copy-done.8, s32[27,1,32]{2,1,0:T(1,128)S(1)} %get-tuple-element.32.send_ref.send_hbm_ref, bf16[1152,128]{1,0:T(8,128)(2,1)S(1)} %get-tuple-element.41.middle_ref, bf16[2048,512]{1,0:T(8,128)(2,1)S(1)} %copy-done), custom_call_target="tpu_custom_call" | custom-call | tf_op jit(solution)/shard_map/reverse_local/pallas_call | solution.py:573
  32.1 0.0 collective-permute-done.5.high_ref
  32.1 13.0 %blocks.1 = (f32[2056,128]{1,0:T(8,128)S(1)}, bf16[288,128]{1,0:T(8,128)(2,1)S(1)}, bf16[288,128]{1,0:T(8,128)(2,1)S(1)}, bf16[288,128]{1,0:T(8,128)(2,1)S(1)}) custom-call(s32[27,1,32]{2,1,0:T(1,128)} %copy-done.6, bf16[1152,128]{1,0:T(8,128)(2,1)S(1)} %collective-permute-done.4.low_ref, bf16[1152,128]{1,0:T(8,128)(2,1)S(1)} %collective-permute-done.5.high_ref, ...), custom_call_target="tpu_custom_call" | custom-call | tf_op jit(solution)/shard_map/blocks/pallas_call | solution.py:586
  45.1 0.0 collective-permute-start.6
  45.2 3.9 %collective-permute-start.7 = (bf16[288,128]{1,0:T(8,128)(2,1)S(1)}, bf16[288,128]{1,0:T(8,128)(2,1)S(1)}, u32[]{:S(2)}, u32[]{:S(2)}) collective-permute-start(bf16[288,128]{1,0:T(8,128)(2,1)S(1)} %get-tuple-element.51), channel_id=1, source_target_pairs={{0,240},{16,0},{32,16},{48,32},{64,48},{80,64},{96,80},{112,96},{1... | collective-permute-start | bytes 221192 | tf_op jit(solution)/shard_map/ppermute | solution.py:31
  49.0 2.0 %collective-permute-done.6.low_ref = bf16[288,128]{1,0:T(8,128)(2,1)S(1)} collective-permute-done((bf16[288,128]{1,0:T(8,128)(2,1)S(1)}, bf16[288,128]{1,0:T(8,128)(2,1)S(1)}, u32[]{:S(2)}, u32[]{:S(2)}) %collective-permute-start.6) | collective-permute-done | bytes 73760 | tf_op jit(solution)/shard_map/ppermute | solution.py:31
  51.1 0.4 collective-permute-start.8
  51.4 1.7 %collective-permute-start.9 = (bf16[288,128]{1,0:T(8,128)(2,1)S(1)}, bf16[288,128]{1,0:T(8,128)(2,1)S(1)}, u32[]{:S(2)}, u32[]{:S(2)}) collective-permute-start(bf16[288,128]{1,0:T(8,128)(2,1)S(1)} %get-tuple-element.54), channel_id=1, source_target_pairs={{0,12},{4,0},{8,4},{12,8},{1,13},{5,1},{9,5},{13,9},{2,14},{6,2},{... | collective-permute-start | bytes 221192 | tf_op jit(solution)/shard_map/ppermute | solution.py:31
  53.2 2.3 %collective-permute-done.8.low_ref = bf16[288,128]{1,0:T(8,128)(2,1)S(1)} collective-permute-done((bf16[288,128]{1,0:T(8,128)(2,1)S(1)}, bf16[288,128]{1,0:T(8,128)(2,1)S(1)}, u32[]{:S(2)}, u32[]{:S(2)}) %collective-permute-start.8) | collective-permute-done | bytes 73760 | tf_op jit(solution)/shard_map/ppermute | solution.py:31
  55.5 1.5 %collective-permute-done.9.high_ref = bf16[288,128]{1,0:T(8,128)(2,1)S(1)} collective-permute-done((bf16[288,128]{1,0:T(8,128)(2,1)S(1)}, bf16[288,128]{1,0:T(8,128)(2,1)S(1)}, u32[]{:S(2)}, u32[]{:S(2)}) %collective-permute-start.9) | collective-permute-done | bytes 73760 | tf_op jit(solution)/shard_map/ppermute | solution.py:31
  57.0 0.8 %collective-permute-start.10 = (bf16[288,128]{1,0:T(8,128)(2,1)S(1)}, bf16[288,128]{1,0:T(8,128)(2,1)S(1)}, u32[]{:S(2)}, u32[]{:S(2)}) collective-permute-start(bf16[288,128]{1,0:T(8,128)(2,1)S(1)} %get-tuple-element.55), channel_id=1, source_target_pairs={{0,1},{1,2},{2,3},{3,0},{4,5},{5,6},{6,7},{7,4},{8,9},{9,10},{10,1... | collective-permute-start | bytes 221192 | tf_op jit(solution)/shard_map/ppermute | solution.py:31
  57.8 2.5 %collective-permute-start.11 = (bf16[288,128]{1,0:T(8,128)(2,1)S(1)}, bf16[288,128]{1,0:T(8,128)(2,1)S(1)}, u32[]{:S(2)}, u32[]{:S(2)}) collective-permute-start(bf16[288,128]{1,0:T(8,128)(2,1)S(1)} %get-tuple-element.56), channel_id=1, source_target_pairs={{0,3},{1,0},{2,1},{3,2},{4,7},{5,4},{6,5},{7,6},{8,11},{9,8},{10,9... | collective-permute-start | bytes 221192 | tf_op jit(solution)/shard_map/ppermute | solution.py:31
  60.3 1.9 %trip_local.1.begun_ref = f32[1024,128]{1,0:T(8,128)S(1)} custom-call(s32[2048]{0:T(1024)S(1)} %copy-done.8, f32[2056,128]{1,0:T(8,128)S(1)} %get-tuple-element.58.trip_ref), custom_call_target="tpu_custom_call" | custom-call | tf_op jit(solution)/shard_map/trip_local/pallas_call | solution.py:621
  62.2 1.9 %trip_rest.1.begun_ref = f32[2056,128]{1,0:T(8,128)S(1)} custom-call(s32[2048]{0:T(1024)S(1)} %copy-done.8, f32[2056,128]{1,0:T(8,128)S(1)} %get-tuple-element.58.trip_ref, f32[1024,128]{1,0:T(8,128)S(1)} %trip_local.1.begun_ref), custom_call_target="tpu_custom_call" | custom-call | tf_op jit(solution)/shard_map/trip_rest/pallas_call | solution.py:629
  64.1 1.1 %trip_middle.1.trip_ref = f32[2056,128]{1,0:T(8,128)S(1)} custom-call(s32[27,1,32]{2,1,0:T(1,128)S(1)} %copy-done.7, bf16[288,128]{1,0:T(8,128)(2,1)S(1)} %get-tuple-element.57.middle_ref, f32[2056,128]{1,0:T(8,128)S(1)} %trip_rest.1.begun_ref), custom_call_target="tpu_custom_call" | custom-call | tf_op jit(solution)/shard_map/trip_middle/pallas_call | solution.py:637
  65.2 0.0 collective-permute-done.11.high_ref
  65.2 9.4 %final.1 = bf16[2048,512]{1,0:T(8,128)(2,1)} custom-call(s32[27,1,32]{2,1,0:T(1,128)} %copy-done.6, bf16[288,128]{1,0:T(8,128)(2,1)S(1)} %collective-permute-done.10.low_ref, bf16[288,128]{1,0:T(8,128)(2,1)S(1)} %collective-permute-done.11.high_ref, f32[2056,128]{1,0:T(8,128)S(1)} %trip_middle.1.trip_ref, bf16[2048,512]{1,0:T(8,128)(2,1)S(1)} %copy-done, ...), custom_call_target="tpu_custom_call" | custom-call | tf_op jit(solution)/shard_map/final/pallas_call | solution.py:647
  (28 shorter events, 0.1 us)
Async XLA Ops:
  0.0 25.3 %copy-start.11 = (s32[1,1,1,27,32]{4,2,3,1,0:T(1,128)S(1)}, s32[1,1,1,27,32]{4,2,3,1,0:T(1,128)}, u32[]{:S(2)}) copy-start(s32[1,1,1,27,32]{4,2,3,1,0:T(1,128)} %param.13) | copy-start | bytes 10372
  0.0 25.3 %copy-start.8 = (s32[2048]{0:T(1024)S(1)}, s32[2048]{0:T(1024)}, u32[]{:S(2)}) copy-start(s32[2048]{0:T(1024)} %fetch_ref.5) | copy-start | bytes 24580
  0.0 25.3 %copy-start.2 = (bf16[2,512,512]{2,1,0:T(8,128)(2,1)S(1)}, bf16[2,512,512]{2,1,0:T(8,128)(2,1)}, u32[]{:S(2)}) copy-start(bf16[2,512,512]{2,1,0:T(8,128)(2,1)} %second_ref.1) | copy-start | bytes 3145732
  0.0 25.3 %copy-start.1 = (bf16[2,512,512]{2,1,0:T(8,128)(2,1)S(1)}, bf16[2,512,512]{2,1,0:T(8,128)(2,1)}, u32[]{:S(2)}) copy-start(bf16[2,512,512]{2,1,0:T(8,128)(2,1)} %first_ref.1) | copy-start | bytes 3145732
  0.0 25.3 %copy-start.9 = (bf16[2,64,512]{2,1,0:T(8,128)(2,1)S(1)}, bf16[2,64,512]{2,1,0:T(8,128)(2,1)}, u32[]{:S(2)}) copy-start(bf16[2,64,512]{2,1,0:T(8,128)(2,1)} %up_ref.1) | copy-start | bytes 393220
  0.0 25.3 %copy-start.5 = (bf16[2,1024,64]{1,2,0:T(8,128)(2,1)S(1)}, bf16[2,1024,64]{1,2,0:T(8,128)(2,1)}, u32[]{:S(2)}) copy-start(bf16[2,1024,64]{1,2,0:T(8,128)(2,1)} %param.16) | copy-start | bytes 786436
  0.0 25.3 %copy-start.10 = (bf16[2,512,64]{1,2,0:T(8,128)(2,1)S(1)}, bf16[2,512,64]{1,2,0:T(8,128)(2,1)}, u32[]{:S(2)}) copy-start(bf16[2,512,64]{1,2,0:T(8,128)(2,1)} %param.15) | copy-start | bytes 393220
  0.0 25.3 %copy-start.4 = (s32[2048,32]{0,1:T(8,128)S(1)}, s32[2048,32]{0,1:T(8,128)}, u32[]{:S(2)}) copy-start(s32[2048,32]{0,1:T(8,128)} %param.12) | copy-start | bytes 786436
  0.1 25.3 %copy-start.3 = (f32[2048,32]{0,1:T(8,128)S(1)}, f32[2048,32]{0,1:T(8,128)}, u32[]{:S(2)}) copy-start(f32[2048,32]{0,1:T(8,128)} %param.11) | copy-start | bytes 786436
  2.9 9.7 %collective-permute-start = (bf16[1152,128]{1,0:T(8,128)(2,1)S(1)}, bf16[1152,128]{1,0:T(8,128)(2,1)S(1)}, u32[]{:S(2)}, u32[]{:S(2)}) collective-permute-start(bf16[1152,128]{1,0:T(8,128)(2,1)S(1)} %get-tuple-element.33), channel_id=1, source_target_pairs={{0,16},{16,32},{32,48},{48,64},{64,80},{80,96},{96,112},{112,128},... | collective-permute-start | bytes 884744 | tf_op jit(solution)/shard_map/ppermute | solution.py:31
  2.9 9.7 %collective-permute-start.1 = (bf16[1152,128]{1,0:T(8,128)(2,1)S(1)}, bf16[1152,128]{1,0:T(8,128)(2,1)S(1)}, u32[]{:S(2)}, u32[]{:S(2)}) collective-permute-start(bf16[1152,128]{1,0:T(8,128)(2,1)S(1)} %get-tuple-element.35), channel_id=1, source_target_pairs={{0,240},{16,0},{32,16},{48,32},{64,48},{80,64},{96,80},{112,96},{1... | collective-permute-start | bytes 884744 | tf_op jit(solution)/shard_map/ppermute | solution.py:31
  12.7 14.6 %copy-start = (bf16[2048,512]{1,0:T(8,128)(2,1)S(1)}, bf16[2048,512]{1,0:T(8,128)(2,1)}, u32[]{:S(2)}) copy-start(bf16[2048,512]{1,0:T(8,128)(2,1)} %rows_ref.3) | copy-start | bytes 6291460
  12.7 7.8 %collective-permute-start.2 = (bf16[1152,128]{1,0:T(8,128)(2,1)S(1)}, bf16[1152,128]{1,0:T(8,128)(2,1)S(1)}, u32[]{:S(2)}, u32[]{:S(2)}) collective-permute-start(bf16[1152,128]{1,0:T(8,128)(2,1)S(1)} %get-tuple-element.36), channel_id=1, source_target_pairs={{0,4},{4,8},{8,12},{12,0},{1,5},{5,9},{9,13},{13,1},{2,6},{6,10},{... | collective-permute-start | bytes 884744 | tf_op jit(solution)/shard_map/ppermute | solution.py:31
  13.3 8.6 %collective-permute-start.3 = (bf16[1152,128]{1,0:T(8,128)(2,1)S(1)}, bf16[1152,128]{1,0:T(8,128)(2,1)S(1)}, u32[]{:S(2)}, u32[]{:S(2)}) collective-permute-start(bf16[1152,128]{1,0:T(8,128)(2,1)S(1)} %get-tuple-element.38), channel_id=1, source_target_pairs={{0,12},{4,0},{8,4},{12,8},{1,13},{5,1},{9,5},{13,9},{2,14},{6,2},{... | collective-permute-start | bytes 884744 | tf_op jit(solution)/shard_map/ppermute | solution.py:31
  21.9 10.2 %collective-permute-start.4 = (bf16[1152,128]{1,0:T(8,128)(2,1)S(1)}, bf16[1152,128]{1,0:T(8,128)(2,1)S(1)}, u32[]{:S(2)}, u32[]{:S(2)}) collective-permute-start(bf16[1152,128]{1,0:T(8,128)(2,1)S(1)} %get-tuple-element.39), channel_id=1, source_target_pairs={{0,1},{1,2},{2,3},{3,0},{4,5},{5,6},{6,7},{7,4},{8,9},{9,10},{10,1... | collective-permute-start | bytes 884744 | tf_op jit(solution)/shard_map/ppermute | solution.py:31
  23.6 8.5 %collective-permute-start.5 = (bf16[1152,128]{1,0:T(8,128)(2,1)S(1)}, bf16[1152,128]{1,0:T(8,128)(2,1)S(1)}, u32[]{:S(2)}, u32[]{:S(2)}) collective-permute-start(bf16[1152,128]{1,0:T(8,128)(2,1)S(1)} %get-tuple-element.40), channel_id=1, source_target_pairs={{0,3},{1,0},{2,1},{3,2},{4,7},{5,4},{6,5},{7,6},{8,11},{9,8},{10,9... | collective-permute-start | bytes 884744 | tf_op jit(solution)/shard_map/ppermute | solution.py:31
  27.3 4.8 %copy-start.6 = (s32[27,1,32]{2,1,0:T(1,128)}, s32[27,1,32]{2,1,0:T(1,128)S(1)}, u32[]{:S(2)}) copy-start(s32[27,1,32]{2,1,0:T(1,128)S(1)} %get-tuple-element.32.send_ref.send_hbm_ref) | copy-start | bytes 10372
  45.1 5.9 %collective-permute-start.6 = (bf16[288,128]{1,0:T(8,128)(2,1)S(1)}, bf16[288,128]{1,0:T(8,128)(2,1)S(1)}, u32[]{:S(2)}, u32[]{:S(2)}) collective-permute-start(bf16[288,128]{1,0:T(8,128)(2,1)S(1)} %get-tuple-element.49), channel_id=1, source_target_pairs={{0,16},{16,32},{32,48},{48,64},{64,80},{80,96},{96,112},{112,128},... | collective-permute-start | bytes 221192 | tf_op jit(solution)/shard_map/ppermute | solution.py:31
  45.2 5.9 %collective-permute-start.7 = (bf16[288,128]{1,0:T(8,128)(2,1)S(1)}, bf16[288,128]{1,0:T(8,128)(2,1)S(1)}, u32[]{:S(2)}, u32[]{:S(2)}) collective-permute-start(bf16[288,128]{1,0:T(8,128)(2,1)S(1)} %get-tuple-element.51), channel_id=1, source_target_pairs={{0,240},{16,0},{32,16},{48,32},{64,48},{80,64},{96,80},{112,96},{1... | collective-permute-start | bytes 221192 | tf_op jit(solution)/shard_map/ppermute | solution.py:31
  51.1 4.4 %collective-permute-start.8 = (bf16[288,128]{1,0:T(8,128)(2,1)S(1)}, bf16[288,128]{1,0:T(8,128)(2,1)S(1)}, u32[]{:S(2)}, u32[]{:S(2)}) collective-permute-start(bf16[288,128]{1,0:T(8,128)(2,1)S(1)} %get-tuple-element.52), channel_id=1, source_target_pairs={{0,4},{4,8},{8,12},{12,0},{1,5},{5,9},{9,13},{13,1},{2,6},{6,10},{... | collective-permute-start | bytes 221192 | tf_op jit(solution)/shard_map/ppermute | solution.py:31
  51.4 5.6 %collective-permute-start.9 = (bf16[288,128]{1,0:T(8,128)(2,1)S(1)}, bf16[288,128]{1,0:T(8,128)(2,1)S(1)}, u32[]{:S(2)}, u32[]{:S(2)}) collective-permute-start(bf16[288,128]{1,0:T(8,128)(2,1)S(1)} %get-tuple-element.54), channel_id=1, source_target_pairs={{0,12},{4,0},{8,4},{12,8},{1,13},{5,1},{9,5},{13,9},{2,14},{6,2},{... | collective-permute-start | bytes 221192 | tf_op jit(solution)/shard_map/ppermute | solution.py:31
  57.0 8.2 %collective-permute-start.10 = (bf16[288,128]{1,0:T(8,128)(2,1)S(1)}, bf16[288,128]{1,0:T(8,128)(2,1)S(1)}, u32[]{:S(2)}, u32[]{:S(2)}) collective-permute-start(bf16[288,128]{1,0:T(8,128)(2,1)S(1)} %get-tuple-element.55), channel_id=1, source_target_pairs={{0,1},{1,2},{2,3},{3,0},{4,5},{5,6},{6,7},{7,4},{8,9},{9,10},{10,1... | collective-permute-start | bytes 221192 | tf_op jit(solution)/shard_map/ppermute | solution.py:31
  57.8 7.4 %collective-permute-start.11 = (bf16[288,128]{1,0:T(8,128)(2,1)S(1)}, bf16[288,128]{1,0:T(8,128)(2,1)S(1)}, u32[]{:S(2)}, u32[]{:S(2)}) collective-permute-start(bf16[288,128]{1,0:T(8,128)(2,1)S(1)} %get-tuple-element.56), channel_id=1, source_target_pairs={{0,3},{1,0},{2,1},{3,2},{4,7},{5,4},{6,5},{7,6},{8,11},{9,8},{10,9... | collective-permute-start | bytes 221192 | tf_op jit(solution)/shard_map/ppermute | solution.py:31
  60.3 3.8 %copy-start.7 = (s32[27,1,32]{2,1,0:T(1,128)S(1)}, s32[27,1,32]{2,1,0:T(1,128)}, u32[]{:S(2)}) copy-start(s32[27,1,32]{2,1,0:T(1,128)} %copy-done.6) | copy-start | bytes 10372

commit v4 on v3

--- a/solution.py
+++ b/solution.py
@@ -115,21 +115,34 @@
     lax.fori_loop(0, directions // 3, body, 0)
 
 
+def pack_slab(send_ref, wide_ref, packed_ref, out_ref, first):
+    each = send_ref.shape[2]
+
+    def body(i, carry):
+        for r in range(each):
+            source = pl.multiple_of(send_ref[first + i, 0, r] * 4 + 32, 4)
+            target = pl.multiple_of((i * each + r) * 4, 4)
+            packed_ref[pl.ds(target, 4), :] = wide_ref[pl.ds(source, 4), :]
+        return carry
+
+    lax.fori_loop(0, 9, body, 0)
+    out_ref[...] = packed_ref[...].astype(BF16)
+
+
 def pack_kernel(
     send_hbm_ref,
     rows_hbm_ref,
     low_ref,
-    middle_ref,
     high_ref,
+    wide_ref,
     send_ref,
     rows_ref,
-    wide_ref,
-    packed_ref,
+    packed_low_ref,
+    packed_high_ref,
     copied,
     listed,
 ):
     count = rows_ref.shape[0]
-    each = send_ref.shape[2]
     chunk = count // 8
     copies = [
         pltpu.make_async_copy(
@@ -142,21 +155,19 @@
     slots = pltpu.make_async_copy(send_hbm_ref, send_ref, listed)
     slots.start()
     wide_ref[0:32, :] = jnp.zeros((32, 128), F32)
+    wide_ref[4 * count + 32 : 4 * count + 64, :] = jnp.zeros((32, 128), F32)
     for copy in copies:
         copy.start()
     for i, copy in enumerate(copies):
         copy.wait()
         spread_rows(rows_ref, wide_ref, chunk * i, chunk, 8)
     slots.wait()
-
-    def pick(t, r, s):
-        source = pl.multiple_of(send_ref[t, 0, r] * 4 + 32, 4)
-        packed_ref[pl.ds(pl.multiple_of(s * 4, 4), 4), :] = wide_ref[pl.ds(source, 4), :]
-
-    for_slots(send_ref, pick)
-    slab = 9 * 4 * each
-    for i, out_ref in enumerate((low_ref, middle_ref, high_ref)):
-        out_ref[...] = packed_ref[slab * i : slab * (i + 1), :].astype(BF16)
+    pack_slab(send_ref, wide_ref, packed_low_ref, low_ref, 0)
+    pack_slab(send_ref, wide_ref, packed_high_ref, high_ref, 18)
+
+
+def pack_middle_kernel(send_ref, wide_ref, out_ref, packed_ref):
+    pack_slab(send_ref, wide_ref, packed_ref, out_ref, 9)
 
 
 def place_wide(send_ref, arrived_ref, rows_ref, t, r, s):
@@ -164,18 +175,15 @@
     rows_ref[pl.ds(target, 4), :] = arrived_ref[pl.ds(pl.multiple_of(s * 4, 4), 4), :]
 
 
-def local_kernel(fetch_ref, send_ref, middle_ref, rows_ref, out_ref, wide_ref, arrived32_ref):
-    count = rows_ref.shape[0]
-    for start in range(0, count, 256):
-        spread_rows(rows_ref, wide_ref, start, 256)
-    wide_ref[4 * count : 4 * count + 8, :] = jnp.zeros((8, 128), F32)
+def local_kernel(fetch_ref, send_ref, middle_ref, wide_ref, out_ref, arrived32_ref):
+    count = fetch_ref.shape[0]
     unroll = 32
 
     def body(i, carry):
         for k in range(unroll):
-            source = pl.multiple_of(local_edge(fetch_ref, i * unroll + k, count) * 4, 4)
-            target = pl.multiple_of((i * unroll + k) * 4, 4)
-            out_ref[pl.ds(target, 4), :] = wide_ref[pl.ds(source, 4), :]
+            edge = i * unroll + k
+            source = pl.multiple_of(local_edge(fetch_ref, edge, count) * 4 + 32, 4)
+            out_ref[pl.ds(pl.multiple_of(edge * 4, 4), 4), :] = wide_ref[pl.ds(source, 4), :]
         return carry
 
     lax.fori_loop(0, count // unroll, body, 0)
@@ -521,16 +529,20 @@
 
     outside = pl.BlockSpec(memory_space=pltpu.HBM)
     slab = slots // 3
-    packed = pl.pallas_call(
+    low, high, wide = pl.pallas_call(
         pack_kernel,
-        out_shape=(jax.ShapeDtypeStruct((slab * 4, 128), BF16),) * 3,
+        out_shape=(
+            jax.ShapeDtypeStruct((slab * 4, 128), BF16),
+            jax.ShapeDtypeStruct((slab * 4, 128), BF16),
+            jax.ShapeDtypeStruct(((count + 16) * 4, 128), F32),
+        ),
         in_specs=[outside, outside],
         out_specs=(vmem,) * 3,
         scratch_shapes=[
-            pltpu.SMEM((27, 1, each), jnp.int32),
+            pltpu.SMEM(senders.shape, jnp.int32),
             pltpu.VMEM((count, width), BF16),
-            pltpu.VMEM((spare * 4, 128), F32),
-            pltpu.VMEM((slots * 4, 128), F32),
+            pltpu.VMEM((slab * 4, 128), F32),
+            pltpu.VMEM((slab * 4, 128), F32),
             pltpu.SemaphoreType.DMA((8,)),
             pltpu.SemaphoreType.DMA,
         ],
@@ -540,6 +552,15 @@
         pltpu.with_memory_space_constraint(senders, pltpu.HBM),
         pltpu.with_memory_space_constraint(edge_state, pltpu.HBM),
     )
+    middle = pl.pallas_call(
+        pack_middle_kernel,
+        out_shape=jax.ShapeDtypeStruct((slab * 4, 128), BF16),
+        in_specs=[smem, vmem],
+        out_specs=vmem,
+        scratch_shapes=[pltpu.VMEM((slab * 4, 128), F32)],
+        compiler_params=params(8),
+        name="pack_middle",
+    )(senders, wide)
     weights, bins, mixer, up_half, first_half, second_half, down_half, own_slots = pl.pallas_call(
         prepare_kernel,
         out_shape=(
@@ -568,20 +589,17 @@
         senders,
     )
     hbm_slots = pltpu.with_memory_space_constraint(own_slots, pltpu.HBM)
-    arrived = exchange(packed)
+    arrived = exchange((low, middle, high))
 
     reverse = pl.pallas_call(
         local_kernel,
         out_shape=jax.ShapeDtypeStruct((spare * 4, 128), F32),
         in_specs=[smem, smem, vmem, vmem],
         out_specs=vmem,
-        scratch_shapes=[
-            pltpu.VMEM((spare * 4, 128), F32),
-            pltpu.VMEM((slots * 4, 128), F32),
-        ],
+        scratch_shapes=[pltpu.VMEM((slots * 4, 128), F32)],
         compiler_params=params(16),
         name="reverse_local",
-    )(fetch_index, own_slots, arrived[1], edge_state)
+    )(fetch_index, own_slots, arrived[1], wide)
 
     triplet, *sending = pl.pallas_call(
         blocks_kernel,

time: 75.1 us -> 74.3 us (0.989)
  waiting for transfers between devices: 17.3 us -> 16.1 us
    ppermute x12, waiting for transfers between devices: 17.3 us -> 16.1 us  [from_behind(): lax.ppermute(array, axis, [(i, (i + by) % length) for i in range(length)])]
    pallas_call x0 -> x1, Pallas kernels: none -> 1.13 us  [local(): pl.pallas_call(pack_middle_kernel, out_shape=jax.ShapeDtypeStruct((slab *...]
  transfers between devices with their start and end apart: 12 -> 12, of which waited for: 6 -> 6; matrix products, arithmetic and copies ran while one was open for 0% -> 0% of each run, Pallas kernels for 15% -> 16%
where the time goes in v4:
time: 74.3 us; the launch traced here: 74 us
  Pallas kernels  37.1 us (50%)
  starting transfers between devices  20.3 us (27%)
  waiting for transfers between devices  16.1 us (22%)
    ppermute x12, starting transfers between devices, from_behind(): lax.ppermute(array, axis, [(i, (i + by) % length) for i in range(length)])  20.3 us
    ppermute x12, waiting for transfers between devices, from_behind(): lax.ppermute(array, axis, [(i, (i + by) % length) for i in range(length)])  16.1 us
    pallas_call x1, Pallas kernels, local(): pl.pallas_call(blocks_kernel, out_shape=(jax.ShapeDtypeStruct((spare, 2 *...  13 us
    pallas_call x1, Pallas kernels, local(): pl.pallas_call(final_kernel, out_shape=jax.ShapeDtypeStruct((count, width...  9.37 us
    pallas_call x1, Pallas kernels, local(): pl.pallas_call(local_kernel, out_shape=jax.ShapeDtypeStruct((spare * 4, 1...  4.29 us
    pallas_call x1, Pallas kernels, local(): pl.pallas_call(pack_kernel, out_shape=(jax.ShapeDtypeStruct((slab * 4, 12...  2.4 us
    pallas_call x1, Pallas kernels, local(): pl.pallas_call(trip_rest_kernel, out_shape=jax.ShapeDtypeStruct((spare, 2...  1.9 us
    pallas_call x1, Pallas kernels, local(): pl.pallas_call(prepare_kernel, out_shape=(jax.ShapeDtypeStruct((quarter,...  1.89 us
  transfers between devices with their start and end apart: 12, of which 6 were waited for; matrix products, arithmetic and copies ran while one was open for 0% of the time, Pallas kernels for 16%

profile of v4, /device:TPU:6, one launch (start us, length us, event | category | flops | bytes accessed | tf_op | source)
XLA Modules:
  0.0 74.0 jit_solution(9208035615677013503)
XLA Ops:
  0.0 2.4 %pack.1 = (bf16[1152,128]{1,0:T(8,128)(2,1)S(1)}, bf16[1152,128]{1,0:T(8,128)(2,1)S(1)}, f32[8256,128]{1,0:T(8,128)S(1)}) custom-call(s32[27,1,32]{2,1,0:T(1,128)} %bitcast.12, bf16[2048,512]{1,0:T(8,128)(2,1)} %rows_ref.1), custom_call_target="tpu_custom_call" | custom-call | tf_op jit(solution)/shard_map/pack/pallas_call | solution.py:532
  2.4 0.0 collective-permute-start
  2.4 5.3 %collective-permute-start.1 = (bf16[1152,128]{1,0:T(8,128)(2,1)S(1)}, bf16[1152,128]{1,0:T(8,128)(2,1)S(1)}, u32[]{:S(2)}, u32[]{:S(2)}) collective-permute-start(bf16[1152,128]{1,0:T(8,128)(2,1)S(1)} %get-tuple-element.35), channel_id=1, source_target_pairs={{0,240},{16,0},{32,16},{48,32},{64,48},{80,64},{96,80},{112,96},{1... | collective-permute-start | bytes 884744 | tf_op jit(solution)/shard_map/ppermute | solution.py:31
  7.8 0.0 copy-start.4
  7.8 0.0 copy-start.5
  7.8 0.0 copy-start.10
  7.8 1.1 %pack_middle.1.middle_ref = bf16[1152,128]{1,0:T(8,128)(2,1)S(1)} custom-call(s32[27,1,32]{2,1,0:T(1,128)S(1)} %bitcast.13, f32[8256,128]{1,0:T(8,128)S(1)} %get-tuple-element.34.wide_ref), custom_call_target="tpu_custom_call" | custom-call | tf_op jit(solution)/shard_map/pack_middle/pallas_call | solution.py:555
  9.0 3.2 %collective-permute-done.low_ref = bf16[1152,128]{1,0:T(8,128)(2,1)S(1)} collective-permute-done((bf16[1152,128]{1,0:T(8,128)(2,1)S(1)}, bf16[1152,128]{1,0:T(8,128)(2,1)S(1)}, u32[]{:S(2)}, u32[]{:S(2)}) %collective-permute-start) | collective-permute-done | bytes 294944 | tf_op jit(solution)/shard_map/ppermute | solution.py:31
  12.1 0.1 regroup.4
  12.2 0.6 collective-permute-start.2
  12.8 1.5 %collective-permute-start.3 = (bf16[1152,128]{1,0:T(8,128)(2,1)S(1)}, bf16[1152,128]{1,0:T(8,128)(2,1)S(1)}, u32[]{:S(2)}, u32[]{:S(2)}) collective-permute-start(bf16[1152,128]{1,0:T(8,128)(2,1)S(1)} %get-tuple-element.38), channel_id=1, source_target_pairs={{0,12},{4,0},{8,4},{12,8},{1,13},{5,1},{9,5},{13,9},{2,14},{6,2},{... | collective-permute-start | bytes 884744 | tf_op jit(solution)/shard_map/ppermute | solution.py:31
  14.3 5.7 %collective-permute-done.2.low_ref = bf16[1152,128]{1,0:T(8,128)(2,1)S(1)} collective-permute-done((bf16[1152,128]{1,0:T(8,128)(2,1)S(1)}, bf16[1152,128]{1,0:T(8,128)(2,1)S(1)}, u32[]{:S(2)}, u32[]{:S(2)}) %collective-permute-start.2) | collective-permute-done | bytes 294944 | tf_op jit(solution)/shard_map/ppermute | solution.py:31
  20.0 1.4 %collective-permute-done.3.high_ref = bf16[1152,128]{1,0:T(8,128)(2,1)S(1)} collective-permute-done((bf16[1152,128]{1,0:T(8,128)(2,1)S(1)}, bf16[1152,128]{1,0:T(8,128)(2,1)S(1)}, u32[]{:S(2)}, u32[]{:S(2)}) %collective-permute-start.3) | collective-permute-done | bytes 294944 | tf_op jit(solution)/shard_map/ppermute | solution.py:31
  21.4 0.1 regroup.5
  21.4 1.7 %collective-permute-start.4 = (bf16[1152,128]{1,0:T(8,128)(2,1)S(1)}, bf16[1152,128]{1,0:T(8,128)(2,1)S(1)}, u32[]{:S(2)}, u32[]{:S(2)}) collective-permute-start(bf16[1152,128]{1,0:T(8,128)(2,1)S(1)} %get-tuple-element.39), channel_id=1, source_target_pairs={{0,1},{1,2},{2,3},{3,0},{4,5},{5,6},{6,7},{7,4},{8,9},{9,10},{10,1... | collective-permute-start | bytes 884744 | tf_op jit(solution)/shard_map/ppermute | solution.py:31
  23.1 1.7 %collective-permute-start.5 = (bf16[1152,128]{1,0:T(8,128)(2,1)S(1)}, bf16[1152,128]{1,0:T(8,128)(2,1)S(1)}, u32[]{:S(2)}, u32[]{:S(2)}) collective-permute-start(bf16[1152,128]{1,0:T(8,128)(2,1)S(1)} %get-tuple-element.40), channel_id=1, source_target_pairs={{0,3},{1,0},{2,1},{3,2},{4,7},{5,4},{6,5},{7,6},{8,11},{9,8},{10,9... | collective-permute-start | bytes 884744 | tf_op jit(solution)/shard_map/ppermute | solution.py:31
  24.8 1.9 %prepare.1 = (bf16[512,128]{1,0:T(8,128)(2,1)S(1)}, bf16[512,128]{1,0:T(8,128)(2,1)S(1)}, bf16[2,4096,256]{2,1,0:T(8,128)(2,1)S(1)}, bf16[2,64,512]{2,1,0:T(8,12...) custom-call(f32[32,2048]{1,0:T(8,128)S(1)} %bitcast.6, ...), custom_call_target="tpu_custom_call" | custom-call | tf_op jit(solution)/shard_map/prepare/pallas_call | solution.py:564
  26.7 4.3 %reverse_local.1.reverse_ref = f32[8224,128]{1,0:T(8,128)S(1)} custom-call(s32[2048]{0:T(1024)S(1)} %copy-done.8, s32[27,1,32]{2,1,0:T(1,128)S(1)} %get-tuple-element.32.send_ref.send_hbm_ref, bf16[1152,128]{1,0:T(8,128)(2,1)S(1)} %get-tuple-element.41.middle_ref, f32[8256,128]{1,0:T(8,128)S(1)} %get-tuple-element.34.wide_ref), custom_call_target="tpu_custom_call" | custom-call | tf_op jit(solution)/shard_map/reverse_local/pallas_call | solution.py:594
  31.1 13.0 %blocks.1 = (f32[2056,128]{1,0:T(8,128)S(1)}, bf16[288,128]{1,0:T(8,128)(2,1)S(1)}, bf16[288,128]{1,0:T(8,128)(2,1)S(1)}, bf16[288,128]{1,0:T(8,128)(2,1)S(1)}) custom-call(s32[27,1,32]{2,1,0:T(1,128)} %copy-done.6, bf16[1152,128]{1,0:T(8,128)(2,1)S(1)} %collective-permute-done.4.low_ref, bf16[1152,128]{1,0:T(8,128)(2,1)S(1)} %collective-permute-done.5.high_ref, ...), custom_call_target="tpu_custom_call" | custom-call | tf_op jit(solution)/shard_map/blocks/pallas_call | solution.py:604
  44.1 0.0 collective-permute-start.6
  44.1 3.9 %collective-permute-start.7 = (bf16[288,128]{1,0:T(8,128)(2,1)S(1)}, bf16[288,128]{1,0:T(8,128)(2,1)S(1)}, u32[]{:S(2)}, u32[]{:S(2)}) collective-permute-start(bf16[288,128]{1,0:T(8,128)(2,1)S(1)} %get-tuple-element.51), channel_id=1, source_target_pairs={{0,240},{16,0},{32,16},{48,32},{64,48},{80,64},{96,80},{112,96},{1... | collective-permute-start | bytes 221192 | tf_op jit(solution)/shard_map/ppermute | solution.py:31
  48.0 2.0 %collective-permute-done.6.low_ref = bf16[288,128]{1,0:T(8,128)(2,1)S(1)} collective-permute-done((bf16[288,128]{1,0:T(8,128)(2,1)S(1)}, bf16[288,128]{1,0:T(8,128)(2,1)S(1)}, u32[]{:S(2)}, u32[]{:S(2)}) %collective-permute-start.6) | collective-permute-done | bytes 73760 | tf_op jit(solution)/shard_map/ppermute | solution.py:31
  50.0 0.4 collective-permute-start.8
  50.4 1.7 %collective-permute-start.9 = (bf16[288,128]{1,0:T(8,128)(2,1)S(1)}, bf16[288,128]{1,0:T(8,128)(2,1)S(1)}, u32[]{:S(2)}, u32[]{:S(2)}) collective-permute-start(bf16[288,128]{1,0:T(8,128)(2,1)S(1)} %get-tuple-element.54), channel_id=1, source_target_pairs={{0,12},{4,0},{8,4},{12,8},{1,13},{5,1},{9,5},{13,9},{2,14},{6,2},{... | collective-permute-start | bytes 221192 | tf_op jit(solution)/shard_map/ppermute | solution.py:31
  52.2 2.3 %collective-permute-done.8.low_ref = bf16[288,128]{1,0:T(8,128)(2,1)S(1)} collective-permute-done((bf16[288,128]{1,0:T(8,128)(2,1)S(1)}, bf16[288,128]{1,0:T(8,128)(2,1)S(1)}, u32[]{:S(2)}, u32[]{:S(2)}) %collective-permute-start.8) | collective-permute-done | bytes 73760 | tf_op jit(solution)/shard_map/ppermute | solution.py:31
  54.5 1.5 %collective-permute-done.9.high_ref = bf16[288,128]{1,0:T(8,128)(2,1)S(1)} collective-permute-done((bf16[288,128]{1,0:T(8,128)(2,1)S(1)}, bf16[288,128]{1,0:T(8,128)(2,1)S(1)}, u32[]{:S(2)}, u32[]{:S(2)}) %collective-permute-start.9) | collective-permute-done | bytes 73760 | tf_op jit(solution)/shard_map/ppermute | solution.py:31
  56.0 1.3 %collective-permute-start.10 = (bf16[288,128]{1,0:T(8,128)(2,1)S(1)}, bf16[288,128]{1,0:T(8,128)(2,1)S(1)}, u32[]{:S(2)}, u32[]{:S(2)}) collective-permute-start(bf16[288,128]{1,0:T(8,128)(2,1)S(1)} %get-tuple-element.55), channel_id=1, source_target_pairs={{0,1},{1,2},{2,3},{3,0},{4,5},{5,6},{6,7},{7,4},{8,9},{9,10},{10,1... | collective-permute-start | bytes 221192 | tf_op jit(solution)/shard_map/ppermute | solution.py:31
  57.3 2.2 %collective-permute-start.11 = (bf16[288,128]{1,0:T(8,128)(2,1)S(1)}, bf16[288,128]{1,0:T(8,128)(2,1)S(1)}, u32[]{:S(2)}, u32[]{:S(2)}) collective-permute-start(bf16[288,128]{1,0:T(8,128)(2,1)S(1)} %get-tuple-element.56), channel_id=1, source_target_pairs={{0,3},{1,0},{2,1},{3,2},{4,7},{5,4},{6,5},{7,6},{8,11},{9,8},{10,9... | collective-permute-start | bytes 221192 | tf_op jit(solution)/shard_map/ppermute | solution.py:31
  59.5 1.9 %trip_local.1.begun_ref = f32[1024,128]{1,0:T(8,128)S(1)} custom-call(s32[2048]{0:T(1024)S(1)} %copy-done.8, f32[2056,128]{1,0:T(8,128)S(1)} %get-tuple-element.58.trip_ref), custom_call_target="tpu_custom_call" | custom-call | tf_op jit(solution)/shard_map/trip_local/pallas_call | solution.py:639
  61.4 1.9 %trip_rest.1.begun_ref = f32[2056,128]{1,0:T(8,128)S(1)} custom-call(s32[2048]{0:T(1024)S(1)} %copy-done.8, f32[2056,128]{1,0:T(8,128)S(1)} %get-tuple-element.58.trip_ref, f32[1024,128]{1,0:T(8,128)S(1)} %trip_local.1.begun_ref), custom_call_target="tpu_custom_call" | custom-call | tf_op jit(solution)/shard_map/trip_rest/pallas_call | solution.py:647
  63.3 1.1 %trip_middle.1.trip_ref = f32[2056,128]{1,0:T(8,128)S(1)} custom-call(s32[27,1,32]{2,1,0:T(1,128)S(1)} %copy-done.7, bf16[288,128]{1,0:T(8,128)(2,1)S(1)} %get-tuple-element.57.middle_ref, f32[2056,128]{1,0:T(8,128)S(1)} %trip_rest.1.begun_ref), custom_call_target="tpu_custom_call" | custom-call | tf_op jit(solution)/shard_map/trip_middle/pallas_call | solution.py:655
  64.5 9.4 %final.1 = bf16[2048,512]{1,0:T(8,128)(2,1)} custom-call(s32[27,1,32]{2,1,0:T(1,128)} %copy-done.6, bf16[288,128]{1,0:T(8,128)(2,1)S(1)} %collective-permute-done.10.low_ref, bf16[288,128]{1,0:T(8,128)(2,1)S(1)} %collective-permute-done.11.high_ref, f32[2056,128]{1,0:T(8,128)S(1)} %trip_middle.1.trip_ref, bf16[2048,512]{1,0:T(8,128)(2,1)S(1)} %copy-done, ...), custom_call_target="tpu_custom_call" | custom-call | tf_op jit(solution)/shard_map/final/pallas_call | solution.py:665
  (29 shorter events, 0.1 us)
Async XLA Ops:
  0.0 7.7 %copy-start.11 = (s32[1,1,1,27,32]{4,2,3,1,0:T(1,128)S(1)}, s32[1,1,1,27,32]{4,2,3,1,0:T(1,128)}, u32[]{:S(2)}) copy-start(s32[1,1,1,27,32]{4,2,3,1,0:T(1,128)} %param.13) | copy-start | bytes 10372
  2.4 9.7 %collective-permute-start = (bf16[1152,128]{1,0:T(8,128)(2,1)S(1)}, bf16[1152,128]{1,0:T(8,128)(2,1)S(1)}, u32[]{:S(2)}, u32[]{:S(2)}) collective-permute-start(bf16[1152,128]{1,0:T(8,128)(2,1)S(1)} %get-tuple-element.33), channel_id=1, source_target_pairs={{0,16},{16,32},{32,48},{48,64},{64,80},{80,96},{96,112},{112,128},... | collective-permute-start | bytes 884744 | tf_op jit(solution)/shard_map/ppermute | solution.py:31
  2.4 9.7 %collective-permute-start.1 = (bf16[1152,128]{1,0:T(8,128)(2,1)S(1)}, bf16[1152,128]{1,0:T(8,128)(2,1)S(1)}, u32[]{:S(2)}, u32[]{:S(2)}) collective-permute-start(bf16[1152,128]{1,0:T(8,128)(2,1)S(1)} %get-tuple-element.35), channel_id=1, source_target_pairs={{0,240},{16,0},{32,16},{48,32},{64,48},{80,64},{96,80},{112,96},{1... | collective-permute-start | bytes 884744 | tf_op jit(solution)/shard_map/ppermute | solution.py:31
  7.7 17.0 %copy-start.1 = (bf16[2,512,512]{2,1,0:T(8,128)(2,1)S(1)}, bf16[2,512,512]{2,1,0:T(8,128)(2,1)}, u32[]{:S(2)}) copy-start(bf16[2,512,512]{2,1,0:T(8,128)(2,1)} %first_ref.1) | copy-start | bytes 3145732
  7.8 17.0 %copy-start.2 = (bf16[2,512,512]{2,1,0:T(8,128)(2,1)S(1)}, bf16[2,512,512]{2,1,0:T(8,128)(2,1)}, u32[]{:S(2)}) copy-start(bf16[2,512,512]{2,1,0:T(8,128)(2,1)} %second_ref.1) | copy-start | bytes 3145732
  7.8 17.0 %copy-start.3 = (f32[2048,32]{0,1:T(8,128)S(1)}, f32[2048,32]{0,1:T(8,128)}, u32[]{:S(2)}) copy-start(f32[2048,32]{0,1:T(8,128)} %param.11) | copy-start | bytes 786436
  7.8 17.0 %copy-start.4 = (s32[2048,32]{0,1:T(8,128)S(1)}, s32[2048,32]{0,1:T(8,128)}, u32[]{:S(2)}) copy-start(s32[2048,32]{0,1:T(8,128)} %param.12) | copy-start | bytes 786436
  7.8 17.0 %copy-start.5 = (bf16[2,1024,64]{1,2,0:T(8,128)(2,1)S(1)}, bf16[2,1024,64]{1,2,0:T(8,128)(2,1)}, u32[]{:S(2)}) copy-start(bf16[2,1024,64]{1,2,0:T(8,128)(2,1)} %param.16) | copy-start | bytes 786436
  7.8 17.0 %copy-start.8 = (s32[2048]{0:T(1024)S(1)}, s32[2048]{0:T(1024)}, u32[]{:S(2)}) copy-start(s32[2048]{0:T(1024)} %fetch_ref.5) | copy-start | bytes 24580
  7.8 17.0 %copy-start.9 = (bf16[2,64,512]{2,1,0:T(8,128)(2,1)S(1)}, bf16[2,64,512]{2,1,0:T(8,128)(2,1)}, u32[]{:S(2)}) copy-start(bf16[2,64,512]{2,1,0:T(8,128)(2,1)} %up_ref.1) | copy-start | bytes 393220
  7.8 17.0 %copy-start.10 = (bf16[2,512,64]{1,2,0:T(8,128)(2,1)S(1)}, bf16[2,512,64]{1,2,0:T(8,128)(2,1)}, u32[]{:S(2)}) copy-start(bf16[2,512,64]{1,2,0:T(8,128)(2,1)} %param.15) | copy-start | bytes 393220
  12.2 7.8 %collective-permute-start.2 = (bf16[1152,128]{1,0:T(8,128)(2,1)S(1)}, bf16[1152,128]{1,0:T(8,128)(2,1)S(1)}, u32[]{:S(2)}, u32[]{:S(2)}) collective-permute-start(bf16[1152,128]{1,0:T(8,128)(2,1)S(1)} %get-tuple-element.36), channel_id=1, source_target_pairs={{0,4},{4,8},{8,12},{12,0},{1,5},{5,9},{9,13},{13,1},{2,6},{6,10},{... | collective-permute-start | bytes 884744 | tf_op jit(solution)/shard_map/ppermute | solution.py:31
  12.8 8.6 %collective-permute-start.3 = (bf16[1152,128]{1,0:T(8,128)(2,1)S(1)}, bf16[1152,128]{1,0:T(8,128)(2,1)S(1)}, u32[]{:S(2)}, u32[]{:S(2)}) collective-permute-start(bf16[1152,128]{1,0:T(8,128)(2,1)S(1)} %get-tuple-element.38), channel_id=1, source_target_pairs={{0,12},{4,0},{8,4},{12,8},{1,13},{5,1},{9,5},{13,9},{2,14},{6,2},{... | collective-permute-start | bytes 884744 | tf_op jit(solution)/shard_map/ppermute | solution.py:31
  21.4 9.6 %collective-permute-start.4 = (bf16[1152,128]{1,0:T(8,128)(2,1)S(1)}, bf16[1152,128]{1,0:T(8,128)(2,1)S(1)}, u32[]{:S(2)}, u32[]{:S(2)}) collective-permute-start(bf16[1152,128]{1,0:T(8,128)(2,1)S(1)} %get-tuple-element.39), channel_id=1, source_target_pairs={{0,1},{1,2},{2,3},{3,0},{4,5},{5,6},{6,7},{7,4},{8,9},{9,10},{10,1... | collective-permute-start | bytes 884744 | tf_op jit(solution)/shard_map/ppermute | solution.py:31
  23.1 8.0 %collective-permute-start.5 = (bf16[1152,128]{1,0:T(8,128)(2,1)S(1)}, bf16[1152,128]{1,0:T(8,128)(2,1)S(1)}, u32[]{:S(2)}, u32[]{:S(2)}) collective-permute-start(bf16[1152,128]{1,0:T(8,128)(2,1)S(1)} %get-tuple-element.40), channel_id=1, source_target_pairs={{0,3},{1,0},{2,1},{3,2},{4,7},{5,4},{6,5},{7,6},{8,11},{9,8},{10,9... | collective-permute-start | bytes 884744 | tf_op jit(solution)/shard_map/ppermute | solution.py:31
  26.7 4.3 %copy-start.6 = (s32[27,1,32]{2,1,0:T(1,128)}, s32[27,1,32]{2,1,0:T(1,128)S(1)}, u32[]{:S(2)}) copy-start(s32[27,1,32]{2,1,0:T(1,128)S(1)} %get-tuple-element.32.send_ref.send_hbm_ref) | copy-start | bytes 10372
  44.1 5.9 %collective-permute-start.6 = (bf16[288,128]{1,0:T(8,128)(2,1)S(1)}, bf16[288,128]{1,0:T(8,128)(2,1)S(1)}, u32[]{:S(2)}, u32[]{:S(2)}) collective-permute-start(bf16[288,128]{1,0:T(8,128)(2,1)S(1)} %get-tuple-element.49), channel_id=1, source_target_pairs={{0,16},{16,32},{32,48},{48,64},{64,80},{80,96},{96,112},{112,128},... | collective-permute-start | bytes 221192 | tf_op jit(solution)/shard_map/ppermute | solution.py:31
  44.1 5.9 %collective-permute-start.7 = (bf16[288,128]{1,0:T(8,128)(2,1)S(1)}, bf16[288,128]{1,0:T(8,128)(2,1)S(1)}, u32[]{:S(2)}, u32[]{:S(2)}) collective-permute-start(bf16[288,128]{1,0:T(8,128)(2,1)S(1)} %get-tuple-element.51), channel_id=1, source_target_pairs={{0,240},{16,0},{32,16},{48,32},{64,48},{80,64},{96,80},{112,96},{1... | collective-permute-start | bytes 221192 | tf_op jit(solution)/shard_map/ppermute | solution.py:31
  50.0 4.4 %collective-permute-start.8 = (bf16[288,128]{1,0:T(8,128)(2,1)S(1)}, bf16[288,128]{1,0:T(8,128)(2,1)S(1)}, u32[]{:S(2)}, u32[]{:S(2)}) collective-permute-start(bf16[288,128]{1,0:T(8,128)(2,1)S(1)} %get-tuple-element.52), channel_id=1, source_target_pairs={{0,4},{4,8},{8,12},{12,0},{1,5},{5,9},{9,13},{13,1},{2,6},{6,10},{... | collective-permute-start | bytes 221192 | tf_op jit(solution)/shard_map/ppermute | solution.py:31
  50.4 5.6 %collective-permute-start.9 = (bf16[288,128]{1,0:T(8,128)(2,1)S(1)}, bf16[288,128]{1,0:T(8,128)(2,1)S(1)}, u32[]{:S(2)}, u32[]{:S(2)}) collective-permute-start(bf16[288,128]{1,0:T(8,128)(2,1)S(1)} %get-tuple-element.54), channel_id=1, source_target_pairs={{0,12},{4,0},{8,4},{12,8},{1,13},{5,1},{9,5},{13,9},{2,14},{6,2},{... | collective-permute-start | bytes 221192 | tf_op jit(solution)/shard_map/ppermute | solution.py:31
  56.0 8.5 %collective-permute-start.10 = (bf16[288,128]{1,0:T(8,128)(2,1)S(1)}, bf16[288,128]{1,0:T(8,128)(2,1)S(1)}, u32[]{:S(2)}, u32[]{:S(2)}) collective-permute-start(bf16[288,128]{1,0:T(8,128)(2,1)S(1)} %get-tuple-element.55), channel_id=1, source_target_pairs={{0,1},{1,2},{2,3},{3,0},{4,5},{5,6},{6,7},{7,4},{8,9},{9,10},{10,1... | collective-permute-start | bytes 221192 | tf_op jit(solution)/shard_map/ppermute | solution.py:31
  57.3 7.2 %collective-permute-start.11 = (bf16[288,128]{1,0:T(8,128)(2,1)S(1)}, bf16[288,128]{1,0:T(8,128)(2,1)S(1)}, u32[]{:S(2)}, u32[]{:S(2)}) collective-permute-start(bf16[288,128]{1,0:T(8,128)(2,1)S(1)} %get-tuple-element.56), channel_id=1, source_target_pairs={{0,3},{1,0},{2,1},{3,2},{4,7},{5,4},{6,5},{7,6},{8,11},{9,8},{10,9... | collective-permute-start | bytes 221192 | tf_op jit(solution)/shard_map/ppermute | solution.py:31
  59.5 3.8 %copy-start.7 = (s32[27,1,32]{2,1,0:T(1,128)S(1)}, s32[27,1,32]{2,1,0:T(1,128)}, u32[]{:S(2)}) copy-start(s32[27,1,32]{2,1,0:T(1,128)} %copy-done.6) | copy-start | bytes 10372
  61.4 3.1 %copy-start = (bf16[2048,512]{1,0:T(8,128)(2,1)S(1)}, bf16[2048,512]{1,0:T(8,128)(2,1)}, u32[]{:S(2)}) copy-start(bf16[2048,512]{1,0:T(8,128)(2,1)} %rows_ref.1) | copy-start | bytes 6291460

commit v5 on v4

--- a/solution.py
+++ b/solution.py
@@ -199,6 +199,19 @@
             wide_ref[start : start + rows, :] = piece[rows * i : rows * (i + 1), :].astype(F32)
 
 
+def pick_slab(send_ref, trip_ref, packed_ref, out_ref, first):
+    each = send_ref.shape[2]
+
+    def body(i, carry):
+        for r in range(each):
+            source = send_ref[first + i, 0, r]
+            packed_ref[pl.ds(i * each + r, 1), :] = trip_ref[pl.ds(source, 1), :]
+        return carry
+
+    lax.fori_loop(0, 9, body, 0)
+    out_ref[...] = packed_ref[...].astype(BF16)
+
+
 def blocks_kernel(
     send_hbm_ref,
     low_ref,
@@ -213,13 +226,13 @@
     second_ref,
     trip_ref,
     send_low_ref,
-    send_middle_ref,
     send_high_ref,
     arrived32_ref,
     rows_ref,
     wide_ref,
     summed_ref,
-    packed_ref,
+    packed_low_ref,
+    packed_high_ref,
     mixed_ref,
     inner_ref,
     send_ref,
@@ -279,9 +292,11 @@
         zero = jnp.zeros_like(weight)
         chosen = [jnp.where(bins == b, weight, zero) for b in range(angular)]
         own = wide_ref[pl.ds(pl.multiple_of(g * 128, 128), 128), :]
-        sums = dot(jnp.concatenate(chosen, axis=0), own).astype(BF16)
-        for b in range(angular):
-            summed_ref[pl.ds(start, 32), 256 * b : 256 * (b + 1)] = sums[32 * b : 32 * (b + 1), :]
+        for q in range(0, angular, 8):
+            sums = dot(jnp.concatenate(chosen[q : q + 8], axis=0), own).astype(BF16)
+            for b in range(8):
+                at = slice(256 * (q + b), 256 * (q + b + 1))
+                summed_ref[pl.ds(start, 32), at] = sums[32 * b : 32 * (b + 1), :]
         return carry
 
     for i in range(count // step):
@@ -298,13 +313,8 @@
         if block == 0:
             pipelined(count // step, (lift, first, second, lambda i: project(i, 1)), BLOCK_TRIPS)
 
-    def pick(t, r, s):
-        packed_ref[pl.ds(s, 1), :] = trip_ref[pl.ds(send_ref[t, 0, r], 1), :]
-
-    for_slots(send_ref, pick)
-    slab = packed_ref.shape[0] // 3
-    for i, out_ref in enumerate((send_low_ref, send_middle_ref, send_high_ref)):
-        out_ref[...] = packed_ref[slab * i : slab * (i + 1), :].astype(BF16)
+    pick_slab(send_ref, trip_ref, packed_low_ref, send_low_ref, 0)
+    pick_slab(send_ref, trip_ref, packed_high_ref, send_high_ref, 18)
 
 
 def gather_trips(fetch_ref, trip_ref, out_ref, start, count, spare):
@@ -319,19 +329,23 @@
     lax.fori_loop(0, count // unroll, body, 0)
 
 
-def trip_kernel(fetch_ref, trip_ref, out_ref):
+def trip_kernel(fetch_ref, send_ref, trip_ref, out_ref, middle_ref, packed_ref):
+    pick_slab(send_ref, trip_ref, packed_ref, middle_ref, 9)
     gather_trips(fetch_ref, trip_ref, out_ref, 0, out_ref.shape[0], fetch_ref.shape[0])
 
 
 def trip_rest_kernel(fetch_ref, trip_ref, begun_ref, out_ref):
-    count = fetch_ref.shape[0]
-    done = begun_ref.shape[0]
+    done, total = begun_ref.shape[0], out_ref.shape[0]
+    out_ref[0:done, :] = begun_ref[...]
+    gather_trips(fetch_ref, trip_ref, out_ref, done, total - done, fetch_ref.shape[0])
+
+
+def trip_middle_kernel(
+    fetch_ref, send_ref, middle_ref, trip_ref, begun_ref, out_ref, arrived32_ref
+):
+    count, done = fetch_ref.shape[0], begun_ref.shape[0]
     out_ref[0:done, :] = begun_ref[...]
     gather_trips(fetch_ref, trip_ref, out_ref, done, count - done, count)
-
-
-def trip_middle_kernel(send_ref, middle_ref, begun_ref, out_ref, arrived32_ref):
-    out_ref[...] = begun_ref[...]
     widen_arrived(((1, middle_ref),), arrived32_ref)
 
     def place(t, r, s):
@@ -373,7 +387,7 @@
         trip_ref[pl.ds(send_ref[t, 0, r], 1), :] = arrived32_ref[pl.ds(s, 1), :]
 
     for_slots(send_ref, place, (0, 2))
-    step = 256
+    step = 512
 
     def lifted(at, block):
         both = trip_ref[at, :].astype(BF16)
@@ -601,20 +615,21 @@
         name="reverse_local",
     )(fetch_index, own_slots, arrived[1], wide)
 
-    triplet, *sending = pl.pallas_call(
+    triplet, send_low, send_high = pl.pallas_call(
         blocks_kernel,
         out_shape=(
             jax.ShapeDtypeStruct((spare, 2 * trip), F32),
         )
-        + (jax.ShapeDtypeStruct((slab, 2 * trip), BF16),) * 3,
+        + (jax.ShapeDtypeStruct((slab, 2 * trip), BF16),) * 2,
         in_specs=[outside] + [vmem] * 10,
-        out_specs=(vmem,) * 4,
+        out_specs=(vmem,) * 3,
         scratch_shapes=[
             pltpu.VMEM((slots * 4, 128), F32),
             pltpu.VMEM((count, width), BF16),
             pltpu.VMEM((count, 4 * trip), BF16),
             pltpu.VMEM((quarter, angular * 4 * trip), BF16),
-            pltpu.VMEM((slots, 2 * trip), F32),
+            pltpu.VMEM((slab, 2 * trip), F32),
+            pltpu.VMEM((slab, 2 * trip), F32),
             pltpu.VMEM((count, width), BF16),
             pltpu.VMEM((count, width), BF16),
             pltpu.SMEM(senders.shape, jnp.int32),
@@ -635,18 +650,22 @@
         first_half,
         second_half,
     )
-    carried = exchange(sending)
-    own_trip = pl.pallas_call(
+    own_trip, send_middle = pl.pallas_call(
         trip_kernel,
-        out_shape=jax.ShapeDtypeStruct((count // 2, 2 * trip), F32),
-        in_specs=[smem, vmem],
-        out_specs=vmem,
+        out_shape=(
+            jax.ShapeDtypeStruct((quarter, 2 * trip), F32),
+            jax.ShapeDtypeStruct((slab, 2 * trip), BF16),
+        ),
+        in_specs=[smem, smem, vmem],
+        out_specs=(vmem, vmem),
+        scratch_shapes=[pltpu.VMEM((slab, 2 * trip), F32)],
         compiler_params=params(5),
         name="trip_local",
-    )(fetch_index, triplet)
+    )(fetch_index, own_slots, triplet)
+    carried = exchange((send_low, send_middle, send_high))
     own_trip = pl.pallas_call(
         trip_rest_kernel,
-        out_shape=jax.ShapeDtypeStruct((spare, 2 * trip), F32),
+        out_shape=jax.ShapeDtypeStruct((3 * quarter, 2 * trip), F32),
         in_specs=[smem, vmem, vmem],
         out_specs=vmem,
         compiler_params=params(5),
@@ -655,12 +674,12 @@
     own_trip = pl.pallas_call(
         trip_middle_kernel,
         out_shape=jax.ShapeDtypeStruct((spare, 2 * trip), F32),
-        in_specs=[smem, vmem, vmem],
+        in_specs=[smem, smem, vmem, vmem, vmem],
         out_specs=vmem,
         scratch_shapes=[pltpu.VMEM((slots, 2 * trip), F32)],
-        compiler_params=params(5),
+        compiler_params=params(6),
         name="trip_middle",
-    )(own_slots, carried[1], own_trip)
+    )(fetch_index, own_slots, carried[1], triplet, own_trip)
 
     out = pl.pallas_call(
         final_kernel,

time: 74.3 us -> 72.7 us (0.978)
  waiting for transfers between devices: 16.1 us -> 14.3 us
    ppermute x12, waiting for transfers between devices: 16.1 us -> 14.3 us  [from_behind(): lax.ppermute(array, axis, [(i, (i + by) % length) for i in range(length)])]
  transfers between devices with their start and end apart: 12 -> 12, of which waited for: 6 -> 6; matrix products, arithmetic and copies ran while one was open for 0% -> 0% of each run, Pallas kernels for 16% -> 18%
where the time goes in v5:
time: 72.7 us; the launch traced here: 72.4 us
  Pallas kernels  37.3 us (51%)
  starting transfers between devices  20.3 us (28%)
  waiting for transfers between devices  14.3 us (20%)
    ppermute x12, starting transfers between devices, from_behind(): lax.ppermute(array, axis, [(i, (i + by) % length) for i in range(length)])  20.3 us
    ppermute x12, waiting for transfers between devices, from_behind(): lax.ppermute(array, axis, [(i, (i + by) % length) for i in range(length)])  14.3 us
    pallas_call x1, Pallas kernels, local(): pl.pallas_call(blocks_kernel, out_shape=(jax.ShapeDtypeStruct((spare, 2 *...  12.6 us
    pallas_call x1, Pallas kernels, local(): pl.pallas_call(final_kernel, out_shape=jax.ShapeDtypeStruct((count, width...  9.37 us
    pallas_call x1, Pallas kernels, local(): pl.pallas_call(local_kernel, out_shape=jax.ShapeDtypeStruct((spare * 4, 1...  4.29 us
    pallas_call x1, Pallas kernels, local(): pl.pallas_call(pack_kernel, out_shape=(jax.ShapeDtypeStruct((slab * 4, 12...  2.4 us
    pallas_call x1, Pallas kernels, local(): pl.pallas_call(prepare_kernel, out_shape=(jax.ShapeDtypeStruct((quarter,...  1.89 us
    pallas_call x1, Pallas kernels, local(): pl.pallas_call(trip_rest_kernel, out_shape=jax.ShapeDtypeStruct((3 * quar...  1.88 us
  transfers between devices with their start and end apart: 12, of which 6 were waited for; matrix products, arithmetic and copies ran while one was open for 0% of the time, Pallas kernels for 18%

profile of v5, /device:TPU:6, one launch (start us, length us, event | category | flops | bytes accessed | tf_op | source)
XLA Modules:
  0.0 72.4 jit_solution(16414536734469402964)
XLA Ops:
  0.0 2.4 %pack.1 = (bf16[1152,128]{1,0:T(8,128)(2,1)S(1)}, bf16[1152,128]{1,0:T(8,128)(2,1)S(1)}, f32[8256,128]{1,0:T(8,128)S(1)}) custom-call(s32[27,1,32]{2,1,0:T(1,128)} %bitcast.12, bf16[2048,512]{1,0:T(8,128)(2,1)} %rows_ref.1), custom_call_target="tpu_custom_call" | custom-call | tf_op jit(solution)/shard_map/pack/pallas_call | solution.py:546
  2.4 0.0 collective-permute-start
  2.4 5.3 %collective-permute-start.1 = (bf16[1152,128]{1,0:T(8,128)(2,1)S(1)}, bf16[1152,128]{1,0:T(8,128)(2,1)S(1)}, u32[]{:S(2)}, u32[]{:S(2)}) collective-permute-start(bf16[1152,128]{1,0:T(8,128)(2,1)S(1)} %get-tuple-element.36), channel_id=1, source_target_pairs={{0,240},{16,0},{32,16},{48,32},{64,48},{80,64},{96,80},{112,96},{1... | collective-permute-start | bytes 884744 | tf_op jit(solution)/shard_map/ppermute | solution.py:31
  7.8 0.0 copy-start.6
  7.8 0.0 copy-start.7
  7.8 0.0 copy-start.10
  7.8 1.1 %pack_middle.1.middle_ref = bf16[1152,128]{1,0:T(8,128)(2,1)S(1)} custom-call(s32[27,1,32]{2,1,0:T(1,128)S(1)} %bitcast.13, f32[8256,128]{1,0:T(8,128)S(1)} %get-tuple-element.35.wide_ref), custom_call_target="tpu_custom_call" | custom-call | tf_op jit(solution)/shard_map/pack_middle/pallas_call | solution.py:569
  9.0 3.2 %collective-permute-done.low_ref = bf16[1152,128]{1,0:T(8,128)(2,1)S(1)} collective-permute-done((bf16[1152,128]{1,0:T(8,128)(2,1)S(1)}, bf16[1152,128]{1,0:T(8,128)(2,1)S(1)}, u32[]{:S(2)}, u32[]{:S(2)}) %collective-permute-start) | collective-permute-done | bytes 294944 | tf_op jit(solution)/shard_map/ppermute | solution.py:31
  12.1 0.1 regroup.4
  12.2 0.6 collective-permute-start.2
  12.8 1.5 %collective-permute-start.3 = (bf16[1152,128]{1,0:T(8,128)(2,1)S(1)}, bf16[1152,128]{1,0:T(8,128)(2,1)S(1)}, u32[]{:S(2)}, u32[]{:S(2)}) collective-permute-start(bf16[1152,128]{1,0:T(8,128)(2,1)S(1)} %get-tuple-element.39), channel_id=1, source_target_pairs={{0,12},{4,0},{8,4},{12,8},{1,13},{5,1},{9,5},{13,9},{2,14},{6,2},{... | collective-permute-start | bytes 884744 | tf_op jit(solution)/shard_map/ppermute | solution.py:31
  14.3 5.7 %collective-permute-done.2.low_ref = bf16[1152,128]{1,0:T(8,128)(2,1)S(1)} collective-permute-done((bf16[1152,128]{1,0:T(8,128)(2,1)S(1)}, bf16[1152,128]{1,0:T(8,128)(2,1)S(1)}, u32[]{:S(2)}, u32[]{:S(2)}) %collective-permute-start.2) | collective-permute-done | bytes 294944 | tf_op jit(solution)/shard_map/ppermute | solution.py:31
  20.0 1.4 %collective-permute-done.3.high_ref = bf16[1152,128]{1,0:T(8,128)(2,1)S(1)} collective-permute-done((bf16[1152,128]{1,0:T(8,128)(2,1)S(1)}, bf16[1152,128]{1,0:T(8,128)(2,1)S(1)}, u32[]{:S(2)}, u32[]{:S(2)}) %collective-permute-start.3) | collective-permute-done | bytes 294944 | tf_op jit(solution)/shard_map/ppermute | solution.py:31
  21.4 0.1 regroup.5
  21.4 1.7 %collective-permute-start.4 = (bf16[1152,128]{1,0:T(8,128)(2,1)S(1)}, bf16[1152,128]{1,0:T(8,128)(2,1)S(1)}, u32[]{:S(2)}, u32[]{:S(2)}) collective-permute-start(bf16[1152,128]{1,0:T(8,128)(2,1)S(1)} %get-tuple-element.40), channel_id=1, source_target_pairs={{0,1},{1,2},{2,3},{3,0},{4,5},{5,6},{6,7},{7,4},{8,9},{9,10},{10,1... | collective-permute-start | bytes 884744 | tf_op jit(solution)/shard_map/ppermute | solution.py:31
  23.1 1.7 %collective-permute-start.5 = (bf16[1152,128]{1,0:T(8,128)(2,1)S(1)}, bf16[1152,128]{1,0:T(8,128)(2,1)S(1)}, u32[]{:S(2)}, u32[]{:S(2)}) collective-permute-start(bf16[1152,128]{1,0:T(8,128)(2,1)S(1)} %get-tuple-element.41), channel_id=1, source_target_pairs={{0,3},{1,0},{2,1},{3,2},{4,7},{5,4},{6,5},{7,6},{8,11},{9,8},{10,9... | collective-permute-start | bytes 884744 | tf_op jit(solution)/shard_map/ppermute | solution.py:31
  24.8 1.9 %prepare.1 = (bf16[512,128]{1,0:T(8,128)(2,1)S(1)}, bf16[512,128]{1,0:T(8,128)(2,1)S(1)}, bf16[2,4096,256]{2,1,0:T(8,128)(2,1)S(1)}, bf16[2,64,512]{2,1,0:T(8,12...) custom-call(f32[32,2048]{1,0:T(8,128)S(1)} %bitcast.8, ...), custom_call_target="tpu_custom_call" | custom-call | tf_op jit(solution)/shard_map/prepare/pallas_call | solution.py:578
  26.7 4.3 %reverse_local.1.reverse_ref = f32[8224,128]{1,0:T(8,128)S(1)} custom-call(s32[2048]{0:T(1024)S(1)} %copy-done.5, s32[27,1,32]{2,1,0:T(1,128)S(1)} %get-tuple-element.33.send_ref.send_hbm_ref, bf16[1152,128]{1,0:T(8,128)(2,1)S(1)} %get-tuple-element.42.middle_ref, f32[8256,128]{1,0:T(8,128)S(1)} %get-tuple-element.35.wide_ref), custom_call_target="tpu_custom_call" | custom-call | tf_op jit(solution)/shard_map/reverse_local/pallas_call | solution.py:608
  31.1 12.6 %blocks.1 = (f32[2056,128]{1,0:T(8,128)S(1)}, bf16[288,128]{1,0:T(8,128)(2,1)S(1)}, bf16[288,128]{1,0:T(8,128)(2,1)S(1)}) custom-call(s32[27,1,32]{2,1,0:T(1,128)} %copy-done.3, bf16[1152,128]{1,0:T(8,128)(2,1)S(1)} %collective-permute-done.4.low_ref, bf16[1152,128]{1,0:T(8,128)(2,1)S(1)} %collective-permute-done.5.high_ref, ...), custom_call_target="tpu_custom_call" | custom-call | tf_op jit(solution)/shard_map/blocks/pallas_call | solution.py:618
  43.7 0.0 collective-permute-start.6
  43.7 3.9 %collective-permute-start.7 = (bf16[288,128]{1,0:T(8,128)(2,1)S(1)}, bf16[288,128]{1,0:T(8,128)(2,1)S(1)}, u32[]{:S(2)}, u32[]{:S(2)}) collective-permute-start(bf16[288,128]{1,0:T(8,128)(2,1)S(1)} %get-tuple-element.53), channel_id=1, source_target_pairs={{0,240},{16,0},{32,16},{48,32},{64,48},{80,64},{96,80},{112,96},{1... | collective-permute-start | bytes 221192 | tf_op jit(solution)/shard_map/ppermute | solution.py:31
  47.6 1.8 %trip_local.1 = (f32[512,128]{1,0:T(8,128)S(1)}, bf16[288,128]{1,0:T(8,128)(2,1)S(1)}) custom-call(s32[2048]{0:T(1024)S(1)} %copy-done.5, s32[27,1,32]{2,1,0:T(1,128)S(1)} %copy-done.4, f32[2056,128]{1,0:T(8,128)S(1)} %get-tuple-element.51.trip_ref), custom_call_target="tpu_custom_call" | custom-call | tf_op jit(solution)/shard_map/trip_local/pallas_call | solution.py:653
  49.4 0.2 collective-permute-done.6.low_ref
  49.6 0.4 collective-permute-start.8
  50.0 1.8 %collective-permute-start.9 = (bf16[288,128]{1,0:T(8,128)(2,1)S(1)}, bf16[288,128]{1,0:T(8,128)(2,1)S(1)}, u32[]{:S(2)}, u32[]{:S(2)}) collective-permute-start(bf16[288,128]{1,0:T(8,128)(2,1)S(1)} %get-tuple-element.56), channel_id=1, source_target_pairs={{0,12},{4,0},{8,4},{12,8},{1,13},{5,1},{9,5},{13,9},{2,14},{6,2},{... | collective-permute-start | bytes 221192 | tf_op jit(solution)/shard_map/ppermute | solution.py:31
  51.7 2.3 %collective-permute-done.8.low_ref = bf16[288,128]{1,0:T(8,128)(2,1)S(1)} collective-permute-done((bf16[288,128]{1,0:T(8,128)(2,1)S(1)}, bf16[288,128]{1,0:T(8,128)(2,1)S(1)}, u32[]{:S(2)}, u32[]{:S(2)}) %collective-permute-start.8) | collective-permute-done | bytes 73760 | tf_op jit(solution)/shard_map/ppermute | solution.py:31
  54.1 1.5 %collective-permute-done.9.high_ref = bf16[288,128]{1,0:T(8,128)(2,1)S(1)} collective-permute-done((bf16[288,128]{1,0:T(8,128)(2,1)S(1)}, bf16[288,128]{1,0:T(8,128)(2,1)S(1)}, u32[]{:S(2)}, u32[]{:S(2)}) %collective-permute-start.9) | collective-permute-done | bytes 73760 | tf_op jit(solution)/shard_map/ppermute | solution.py:31
  55.6 1.3 %collective-permute-start.10 = (bf16[288,128]{1,0:T(8,128)(2,1)S(1)}, bf16[288,128]{1,0:T(8,128)(2,1)S(1)}, u32[]{:S(2)}, u32[]{:S(2)}) collective-permute-start(bf16[288,128]{1,0:T(8,128)(2,1)S(1)} %get-tuple-element.57), channel_id=1, source_target_pairs={{0,1},{1,2},{2,3},{3,0},{4,5},{5,6},{6,7},{7,4},{8,9},{9,10},{10,1... | collective-permute-start | bytes 221192 | tf_op jit(solution)/shard_map/ppermute | solution.py:31
  56.9 2.2 %collective-permute-start.11 = (bf16[288,128]{1,0:T(8,128)(2,1)S(1)}, bf16[288,128]{1,0:T(8,128)(2,1)S(1)}, u32[]{:S(2)}, u32[]{:S(2)}) collective-permute-start(bf16[288,128]{1,0:T(8,128)(2,1)S(1)} %get-tuple-element.58), channel_id=1, source_target_pairs={{0,3},{1,0},{2,1},{3,2},{4,7},{5,4},{6,5},{7,6},{8,11},{9,8},{10,9... | collective-permute-start | bytes 221192 | tf_op jit(solution)/shard_map/ppermute | solution.py:31
  59.1 1.9 %trip_rest.1.begun_ref = f32[1536,128]{1,0:T(8,128)S(1)} custom-call(s32[2048]{0:T(1024)S(1)} %copy-done.5, f32[2056,128]{1,0:T(8,128)S(1)} %get-tuple-element.51.trip_ref, f32[512,128]{1,0:T(8,128)S(1)} %get-tuple-element.60.begun_ref), custom_call_target="tpu_custom_call" | custom-call | tf_op jit(solution)/shard_map/trip_rest/pallas_call | solution.py:666
  61.0 1.8 %trip_middle.1.trip_ref = f32[2056,128]{1,0:T(8,128)S(1)} custom-call(s32[2048]{0:T(1024)S(1)} %copy-done.5, s32[27,1,32]{2,1,0:T(1,128)S(1)} %copy-done.4, bf16[288,128]{1,0:T(8,128)(2,1)S(1)} %get-tuple-element.59.middle_ref, f32[2056,128]{1,0:T(8,128)S(1)} %get-tuple-element.51.trip_ref, f32[1536,128]{1,0:T(8,128)S(1)} %trip_rest.1.begun_ref), custom_call_target="tpu_custom_call" | custom-call | tf_op jit(solution)/shard_map/trip_middle/pallas_call | solution.py:674
  62.9 9.4 %final.1 = bf16[2048,512]{1,0:T(8,128)(2,1)} custom-call(s32[27,1,32]{2,1,0:T(1,128)} %copy-done.3, bf16[288,128]{1,0:T(8,128)(2,1)S(1)} %collective-permute-done.10.low_ref, bf16[288,128]{1,0:T(8,128)(2,1)S(1)} %collective-permute-done.11.high_ref, f32[2056,128]{1,0:T(8,128)S(1)} %trip_middle.1.trip_ref, bf16[2048,512]{1,0:T(8,128)(2,1)S(1)} %copy-done, ...), custom_call_target="tpu_custom_call" | custom-call | tf_op jit(solution)/shard_map/final/pallas_call | solution.py:684
  (29 shorter events, 0.1 us)
Async XLA Ops:
  0.0 7.7 %copy-start.11 = (s32[1,1,1,27,32]{4,2,3,1,0:T(1,128)S(1)}, s32[1,1,1,27,32]{4,2,3,1,0:T(1,128)}, u32[]{:S(2)}) copy-start(s32[1,1,1,27,32]{4,2,3,1,0:T(1,128)} %param.13) | copy-start | bytes 10372
  2.4 9.7 %collective-permute-start = (bf16[1152,128]{1,0:T(8,128)(2,1)S(1)}, bf16[1152,128]{1,0:T(8,128)(2,1)S(1)}, u32[]{:S(2)}, u32[]{:S(2)}) collective-permute-start(bf16[1152,128]{1,0:T(8,128)(2,1)S(1)} %get-tuple-element.34), channel_id=1, source_target_pairs={{0,16},{16,32},{32,48},{48,64},{64,80},{80,96},{96,112},{112,128},... | collective-permute-start | bytes 884744 | tf_op jit(solution)/shard_map/ppermute | solution.py:31
  2.4 9.7 %collective-permute-start.1 = (bf16[1152,128]{1,0:T(8,128)(2,1)S(1)}, bf16[1152,128]{1,0:T(8,128)(2,1)S(1)}, u32[]{:S(2)}, u32[]{:S(2)}) collective-permute-start(bf16[1152,128]{1,0:T(8,128)(2,1)S(1)} %get-tuple-element.36), channel_id=1, source_target_pairs={{0,240},{16,0},{32,16},{48,32},{64,48},{80,64},{96,80},{112,96},{1... | collective-permute-start | bytes 884744 | tf_op jit(solution)/shard_map/ppermute | solution.py:31
  7.7 17.0 %copy-start.1 = (bf16[2,512,512]{2,1,0:T(8,128)(2,1)S(1)}, bf16[2,512,512]{2,1,0:T(8,128)(2,1)}, u32[]{:S(2)}) copy-start(bf16[2,512,512]{2,1,0:T(8,128)(2,1)} %first_ref.1) | copy-start | bytes 3145732
  7.8 17.0 %copy-start.2 = (bf16[2,512,512]{2,1,0:T(8,128)(2,1)S(1)}, bf16[2,512,512]{2,1,0:T(8,128)(2,1)}, u32[]{:S(2)}) copy-start(bf16[2,512,512]{2,1,0:T(8,128)(2,1)} %second_ref.1) | copy-start | bytes 3145732
  7.8 17.0 %copy-start.5 = (s32[2048]{0:T(1024)S(1)}, s32[2048]{0:T(1024)}, u32[]{:S(2)}) copy-start(s32[2048]{0:T(1024)} %fetch_ref.7) | copy-start | bytes 24580
  7.8 17.0 %copy-start.6 = (f32[2048,32]{0,1:T(8,128)S(1)}, f32[2048,32]{0,1:T(8,128)}, u32[]{:S(2)}) copy-start(f32[2048,32]{0,1:T(8,128)} %param.11) | copy-start | bytes 786436
  7.8 17.0 %copy-start.7 = (s32[2048,32]{0,1:T(8,128)S(1)}, s32[2048,32]{0,1:T(8,128)}, u32[]{:S(2)}) copy-start(s32[2048,32]{0,1:T(8,128)} %param.12) | copy-start | bytes 786436
  7.8 17.0 %copy-start.8 = (bf16[2,1024,64]{1,2,0:T(8,128)(2,1)S(1)}, bf16[2,1024,64]{1,2,0:T(8,128)(2,1)}, u32[]{:S(2)}) copy-start(bf16[2,1024,64]{1,2,0:T(8,128)(2,1)} %param.16) | copy-start | bytes 786436
  7.8 17.0 %copy-start.9 = (bf16[2,64,512]{2,1,0:T(8,128)(2,1)S(1)}, bf16[2,64,512]{2,1,0:T(8,128)(2,1)}, u32[]{:S(2)}) copy-start(bf16[2,64,512]{2,1,0:T(8,128)(2,1)} %up_ref.1) | copy-start | bytes 393220
  7.8 17.0 %copy-start.10 = (bf16[2,512,64]{1,2,0:T(8,128)(2,1)S(1)}, bf16[2,512,64]{1,2,0:T(8,128)(2,1)}, u32[]{:S(2)}) copy-start(bf16[2,512,64]{1,2,0:T(8,128)(2,1)} %param.15) | copy-start | bytes 393220
  12.2 7.8 %collective-permute-start.2 = (bf16[1152,128]{1,0:T(8,128)(2,1)S(1)}, bf16[1152,128]{1,0:T(8,128)(2,1)S(1)}, u32[]{:S(2)}, u32[]{:S(2)}) collective-permute-start(bf16[1152,128]{1,0:T(8,128)(2,1)S(1)} %get-tuple-element.37), channel_id=1, source_target_pairs={{0,4},{4,8},{8,12},{12,0},{1,5},{5,9},{9,13},{13,1},{2,6},{6,10},{... | collective-permute-start | bytes 884744 | tf_op jit(solution)/shard_map/ppermute | solution.py:31
  12.8 8.6 %collective-permute-start.3 = (bf16[1152,128]{1,0:T(8,128)(2,1)S(1)}, bf16[1152,128]{1,0:T(8,128)(2,1)S(1)}, u32[]{:S(2)}, u32[]{:S(2)}) collective-permute-start(bf16[1152,128]{1,0:T(8,128)(2,1)S(1)} %get-tuple-element.39), channel_id=1, source_target_pairs={{0,12},{4,0},{8,4},{12,8},{1,13},{5,1},{9,5},{13,9},{2,14},{6,2},{... | collective-permute-start | bytes 884744 | tf_op jit(solution)/shard_map/ppermute | solution.py:31
  21.4 9.6 %collective-permute-start.4 = (bf16[1152,128]{1,0:T(8,128)(2,1)S(1)}, bf16[1152,128]{1,0:T(8,128)(2,1)S(1)}, u32[]{:S(2)}, u32[]{:S(2)}) collective-permute-start(bf16[1152,128]{1,0:T(8,128)(2,1)S(1)} %get-tuple-element.40), channel_id=1, source_target_pairs={{0,1},{1,2},{2,3},{3,0},{4,5},{5,6},{6,7},{7,4},{8,9},{9,10},{10,1... | collective-permute-start | bytes 884744 | tf_op jit(solution)/shard_map/ppermute | solution.py:31
  23.1 8.0 %collective-permute-start.5 = (bf16[1152,128]{1,0:T(8,128)(2,1)S(1)}, bf16[1152,128]{1,0:T(8,128)(2,1)S(1)}, u32[]{:S(2)}, u32[]{:S(2)}) collective-permute-start(bf16[1152,128]{1,0:T(8,128)(2,1)S(1)} %get-tuple-element.41), channel_id=1, source_target_pairs={{0,3},{1,0},{2,1},{3,2},{4,7},{5,4},{6,5},{7,6},{8,11},{9,8},{10,9... | collective-permute-start | bytes 884744 | tf_op jit(solution)/shard_map/ppermute | solution.py:31
  26.7 4.3 %copy-start.3 = (s32[27,1,32]{2,1,0:T(1,128)}, s32[27,1,32]{2,1,0:T(1,128)S(1)}, u32[]{:S(2)}) copy-start(s32[27,1,32]{2,1,0:T(1,128)S(1)} %get-tuple-element.33.send_ref.send_hbm_ref) | copy-start | bytes 10372
  31.1 16.5 %copy-start.4 = (s32[27,1,32]{2,1,0:T(1,128)S(1)}, s32[27,1,32]{2,1,0:T(1,128)}, u32[]{:S(2)}) copy-start(s32[27,1,32]{2,1,0:T(1,128)} %copy-done.3) | copy-start | bytes 10372
  43.7 5.9 %collective-permute-start.6 = (bf16[288,128]{1,0:T(8,128)(2,1)S(1)}, bf16[288,128]{1,0:T(8,128)(2,1)S(1)}, u32[]{:S(2)}, u32[]{:S(2)}) collective-permute-start(bf16[288,128]{1,0:T(8,128)(2,1)S(1)} %get-tuple-element.50), channel_id=1, source_target_pairs={{0,16},{16,32},{32,48},{48,64},{64,80},{80,96},{96,112},{112,128},... | collective-permute-start | bytes 221192 | tf_op jit(solution)/shard_map/ppermute | solution.py:31
  43.7 5.9 %collective-permute-start.7 = (bf16[288,128]{1,0:T(8,128)(2,1)S(1)}, bf16[288,128]{1,0:T(8,128)(2,1)S(1)}, u32[]{:S(2)}, u32[]{:S(2)}) collective-permute-start(bf16[288,128]{1,0:T(8,128)(2,1)S(1)} %get-tuple-element.53), channel_id=1, source_target_pairs={{0,240},{16,0},{32,16},{48,32},{64,48},{80,64},{96,80},{112,96},{1... | collective-permute-start | bytes 221192 | tf_op jit(solution)/shard_map/ppermute | solution.py:31
  49.6 4.4 %collective-permute-start.8 = (bf16[288,128]{1,0:T(8,128)(2,1)S(1)}, bf16[288,128]{1,0:T(8,128)(2,1)S(1)}, u32[]{:S(2)}, u32[]{:S(2)}) collective-permute-start(bf16[288,128]{1,0:T(8,128)(2,1)S(1)} %get-tuple-element.54), channel_id=1, source_target_pairs={{0,4},{4,8},{8,12},{12,0},{1,5},{5,9},{9,13},{13,1},{2,6},{6,10},{... | collective-permute-start | bytes 221192 | tf_op jit(solution)/shard_map/ppermute | solution.py:31
  50.0 5.6 %collective-permute-start.9 = (bf16[288,128]{1,0:T(8,128)(2,1)S(1)}, bf16[288,128]{1,0:T(8,128)(2,1)S(1)}, u32[]{:S(2)}, u32[]{:S(2)}) collective-permute-start(bf16[288,128]{1,0:T(8,128)(2,1)S(1)} %get-tuple-element.56), channel_id=1, source_target_pairs={{0,12},{4,0},{8,4},{12,8},{1,13},{5,1},{9,5},{13,9},{2,14},{6,2},{... | collective-permute-start | bytes 221192 | tf_op jit(solution)/shard_map/ppermute | solution.py:31
  55.6 7.3 %collective-permute-start.10 = (bf16[288,128]{1,0:T(8,128)(2,1)S(1)}, bf16[288,128]{1,0:T(8,128)(2,1)S(1)}, u32[]{:S(2)}, u32[]{:S(2)}) collective-permute-start(bf16[288,128]{1,0:T(8,128)(2,1)S(1)} %get-tuple-element.57), channel_id=1, source_target_pairs={{0,1},{1,2},{2,3},{3,0},{4,5},{5,6},{6,7},{7,4},{8,9},{9,10},{10,1... | collective-permute-start | bytes 221192 | tf_op jit(solution)/shard_map/ppermute | solution.py:31
  56.9 5.9 %collective-permute-start.11 = (bf16[288,128]{1,0:T(8,128)(2,1)S(1)}, bf16[288,128]{1,0:T(8,128)(2,1)S(1)}, u32[]{:S(2)}, u32[]{:S(2)}) collective-permute-start(bf16[288,128]{1,0:T(8,128)(2,1)S(1)} %get-tuple-element.58), channel_id=1, source_target_pairs={{0,3},{1,0},{2,1},{3,2},{4,7},{5,4},{6,5},{7,6},{8,11},{9,8},{10,9... | collective-permute-start | bytes 221192 | tf_op jit(solution)/shard_map/ppermute | solution.py:31
  59.1 3.7 %copy-start = (bf16[2048,512]{1,0:T(8,128)(2,1)S(1)}, bf16[2048,512]{1,0:T(8,128)(2,1)}, u32[]{:S(2)}) copy-start(bf16[2048,512]{1,0:T(8,128)(2,1)} %rows_ref.1) | copy-start | bytes 6291460

commit v6 on v5

--- a/solution.py
+++ b/solution.py
@@ -47,26 +47,81 @@
                 out_ref[target : target + rows, :] = slab_ref[source : source + rows, :]
 
 
-def exchange(slabs):
+def second_split_kernel(low_ref, middle_ref, high_ref, *out_refs):
+    outer_low_ref, outer_high_ref, own_ref, inner_low_ref, inner_high_ref = out_refs
+    rows = low_ref.shape[0] // 9
+
+    def copy(out_ref, i, slab_ref, j):
+        out_ref[rows * i : rows * (i + 1), :] = slab_ref[rows * j : rows * (j + 1), :]
+
+    for a, slab_ref in enumerate((low_ref, middle_ref, high_ref)):
+        for c in range(3):
+            copy(own_ref, 3 * a + c, slab_ref, 3 + c)
+        for b, outer_ref, inner_ref in (
+            (0, outer_low_ref, inner_low_ref),
+            (2, outer_high_ref, inner_high_ref),
+        ):
+            copy(outer_ref, 2 * a, slab_ref, 3 * b)
+            copy(outer_ref, 2 * a + 1, slab_ref, 3 * b + 2)
+            copy(inner_ref, a, slab_ref, 3 * b + 1)
+
+
+def third_split_kernel(low_ref, own_ref, high_ref, low_out_ref, high_out_ref):
+    rows = own_ref.shape[0] // 9
+
+    def copy(out_ref, i, slab_ref, j):
+        out_ref[rows * i : rows * (i + 1), :] = slab_ref[rows * j : rows * (j + 1), :]
+
+    for a in range(3):
+        for c, out_ref in ((0, low_out_ref), (2, high_out_ref)):
+            copy(out_ref, a, low_ref, 2 * a + c // 2)
+            copy(out_ref, 3 + a, own_ref, 3 * a + c)
+            copy(out_ref, 6 + a, high_ref, 2 * a + c // 2)
+
+
+def middle_kernel(low_ref, own_ref, high_ref, out_ref):
+    rows = own_ref.shape[0] // 9
+    out_ref[0 : 3 * rows, :] = low_ref[...]
+    out_ref[6 * rows : 9 * rows, :] = high_ref[...]
+    for a in range(3):
+        out_ref[rows * (3 + a) : rows * (4 + a), :] = own_ref[
+            rows * (3 * a + 1) : rows * (3 * a + 2), :
+        ]
+
+
+def exchange(slabs, split=False):
     vmem = pl.BlockSpec(memory_space=pltpu.VMEM)
-
-    def regroup(kernel, pieces):
+    rows, lanes = slabs[0].shape
+    kind = slabs[0].dtype
+
+    def regroup(kernel, pieces, counts):
         return pl.pallas_call(
             kernel,
-            out_shape=[jax.ShapeDtypeStruct(piece.shape, piece.dtype) for piece in pieces],
+            out_shape=[jax.ShapeDtypeStruct((rows * n // 9, lanes), kind) for n in counts],
             in_specs=[vmem] * 3,
-            out_specs=[vmem] * 3,
+            out_specs=[vmem] * len(counts),
             compiler_params=pltpu.CompilerParams(vmem_limit_bytes=4 * MIB),
             name="regroup",
         )(*pieces)
 
-    def hop(sent, axis):
-        low, middle, high = sent
-        return [from_behind(high, axis, 1), middle, from_behind(low, axis, -1)]
-
-    slabs = hop(slabs, "gx")
-    slabs = hop(regroup(second_kernel, slabs), "gy")
-    return hop(regroup(third_kernel, slabs), "gz")
+    def hop(low, high, axis):
+        return from_behind(high, axis, 1), from_behind(low, axis, -1)
+
+    from_low, from_high = hop(slabs[0], slabs[2], "gx")
+    slabs = (from_low, slabs[1], from_high)
+    if not split:
+        low, own, high = regroup(second_kernel, slabs, (9, 9, 9))
+        from_low, from_high = hop(low, high, "gy")
+        low, middle, high = regroup(third_kernel, (from_low, own, from_high), (9, 9, 9))
+        from_low, from_high = hop(low, high, "gz")
+        return from_low, middle, from_high
+    low, high, own, inner_low, inner_high = regroup(second_split_kernel, slabs, (6, 6, 9, 3, 3))
+    from_low, from_high = hop(low, high, "gy")
+    inner_low, inner_high = hop(inner_low, inner_high, "gy")
+    low, high = regroup(third_split_kernel, (from_low, own, from_high), (9, 9))
+    from_low, from_high = hop(low, high, "gz")
+    middle = regroup(middle_kernel, (inner_low, own, inner_high), (9,))[0]
+    return from_low, middle, from_high
 
 
 def pipelined(blocks, stages, trips):
@@ -603,7 +658,7 @@
         senders,
     )
     hbm_slots = pltpu.with_memory_space_constraint(own_slots, pltpu.HBM)
-    arrived = exchange((low, middle, high))
+    arrived = exchange((low, middle, high), True)
 
     reverse = pl.pallas_call(
         local_kernel,

time: 72.7 us -> 74.1 us (1.019)
  the two profiles are of different devices: /device:TPU:6 before, /device:TPU:103 now
where the time goes in v6:
time: 74.1 us; the launch traced here: 73.7 us
  Pallas kernels  37.3 us (50%)
  waiting for transfers between devices  18.1 us (24%)
  starting transfers between devices  17.9 us (24%)
    ppermute x14, waiting for transfers between devices, from_behind(): lax.ppermute(array, axis, [(i, (i + by) % length) for i in range(length)])  18.1 us
    ppermute x14, starting transfers between devices, from_behind(): lax.ppermute(array, axis, [(i, (i + by) % length) for i in range(length)])  17.9 us
    pallas_call x1, Pallas kernels, local(): pl.pallas_call(blocks_kernel, out_shape=(jax.ShapeDtypeStruct((spare, 2 *...  12.6 us
    pallas_call x1, Pallas kernels, local(): pl.pallas_call(final_kernel, out_shape=jax.ShapeDtypeStruct((count, width...  9.35 us
    pallas_call x1, Pallas kernels, local(): pl.pallas_call(local_kernel, out_shape=jax.ShapeDtypeStruct((spare * 4, 1...  4.29 us
    pallas_call x1, Pallas kernels, local(): pl.pallas_call(pack_kernel, out_shape=(jax.ShapeDtypeStruct((slab * 4, 12...  2.4 us
    pallas_call x1, Pallas kernels, local(): pl.pallas_call(prepare_kernel, out_shape=(jax.ShapeDtypeStruct((quarter,...  1.89 us
    pallas_call x1, Pallas kernels, local(): pl.pallas_call(trip_rest_kernel, out_shape=jax.ShapeDtypeStruct((3 * quar...  1.88 us
  transfers between devices with their start and end apart: 14, of which 9 were waited for; matrix products, arithmetic and copies ran while one was open for 0% of the time, Pallas kernels for 17%

profile of v6, /device:TPU:103, one launch (start us, length us, event | category | flops | bytes accessed | tf_op | source)
XLA Modules:
  0.0 73.7 jit_solution(2429455616524356789)
XLA Ops:
  0.0 2.4 %pack.1 = (bf16[1152,128]{1,0:T(8,128)(2,1)S(1)}, bf16[1152,128]{1,0:T(8,128)(2,1)S(1)}, f32[8256,128]{1,0:T(8,128)S(1)}) custom-call(s32[27,1,32]{2,1,0:T(1,128)} %bitcast.12, bf16[2048,512]{1,0:T(8,128)(2,1)} %rows_ref.1), custom_call_target="tpu_custom_call" | custom-call | tf_op jit(solution)/shard_map/pack/pallas_call | solution.py:601
  2.4 3.4 %collective-permute-start = (bf16[1152,128]{1,0:T(8,128)(2,1)S(1)}, bf16[1152,128]{1,0:T(8,128)(2,1)S(1)}, u32[]{:S(2)}, u32[]{:S(2)}) collective-permute-start(bf16[1152,128]{1,0:T(8,128)(2,1)S(1)} %get-tuple-element.35), channel_id=1, source_target_pairs={{0,16},{16,32},{32,48},{48,64},{64,80},{80,96},{96,112},{112,128},... | collective-permute-start | bytes 884744 | tf_op jit(solution)/shard_map/ppermute | solution.py:31
  5.8 0.0 copy-start.5
  5.9 0.0 copy-start.8
  5.9 1.1 %pack_middle.1.middle_ref = bf16[1152,128]{1,0:T(8,128)(2,1)S(1)} custom-call(s32[27,1,32]{2,1,0:T(1,128)S(1)} %bitcast.13, f32[8256,128]{1,0:T(8,128)S(1)} %get-tuple-element.36.wide_ref), custom_call_target="tpu_custom_call" | custom-call | tf_op jit(solution)/shard_map/pack_middle/pallas_call | solution.py:624
  7.1 2.4 %collective-permute-done.low_ref = bf16[1152,128]{1,0:T(8,128)(2,1)S(1)} collective-permute-done((bf16[1152,128]{1,0:T(8,128)(2,1)S(1)}, bf16[1152,128]{1,0:T(8,128)(2,1)S(1)}, u32[]{:S(2)}, u32[]{:S(2)}) %collective-permute-start) | collective-permute-done | bytes 294944 | tf_op jit(solution)/shard_map/ppermute | solution.py:31
  9.5 3.7 %collective-permute-done.1.high_ref = bf16[1152,128]{1,0:T(8,128)(2,1)S(1)} collective-permute-done((bf16[1152,128]{1,0:T(8,128)(2,1)S(1)}, bf16[1152,128]{1,0:T(8,128)(2,1)S(1)}, u32[]{:S(2)}, u32[]{:S(2)}) %collective-permute-start.1) | collective-permute-done | bytes 294944 | tf_op jit(solution)/shard_map/ppermute | solution.py:31
  13.2 0.1 regroup.5
  13.3 0.3 collective-permute-start.2
  13.5 1.3 %collective-permute-start.3 = (bf16[768,128]{1,0:T(8,128)(2,1)S(1)}, bf16[768,128]{1,0:T(8,128)(2,1)S(1)}, u32[]{:S(2)}, u32[]{:S(2)}) collective-permute-start(bf16[768,128]{1,0:T(8,128)(2,1)S(1)} %get-tuple-element.40), channel_id=1, source_target_pairs={{0,12},{4,0},{8,4},{12,8},{1,13},{5,1},{9,5},{13,9},{2,14},{6,2},{... | collective-permute-start | bytes 589832 | tf_op jit(solution)/shard_map/ppermute | solution.py:31
  14.8 3.1 %collective-permute-done.2.low_ref = bf16[768,128]{1,0:T(8,128)(2,1)S(1)} collective-permute-done((bf16[768,128]{1,0:T(8,128)(2,1)S(1)}, bf16[768,128]{1,0:T(8,128)(2,1)S(1)}, u32[]{:S(2)}, u32[]{:S(2)}) %collective-permute-start.2) | collective-permute-done | bytes 196640 | tf_op jit(solution)/shard_map/ppermute | solution.py:31
  17.9 1.4 %collective-permute-done.3.high_ref = bf16[768,128]{1,0:T(8,128)(2,1)S(1)} collective-permute-done((bf16[768,128]{1,0:T(8,128)(2,1)S(1)}, bf16[768,128]{1,0:T(8,128)(2,1)S(1)}, u32[]{:S(2)}, u32[]{:S(2)}) %collective-permute-start.3) | collective-permute-done | bytes 196640 | tf_op jit(solution)/shard_map/ppermute | solution.py:31
  19.3 1.4 %collective-permute-start.4 = (bf16[1152,128]{1,0:T(8,128)(2,1)S(1)}, bf16[1152,128]{1,0:T(8,128)(2,1)S(1)}, u32[]{:S(2)}, u32[]{:S(2)}) collective-permute-start(bf16[1152,128]{1,0:T(8,128)(2,1)S(1)} %get-tuple-element.41), channel_id=1, source_target_pairs={{0,1},{1,2},{2,3},{3,0},{4,5},{5,6},{6,7},{7,4},{8,9},{9,10},{10,1... | collective-permute-start | bytes 884744 | tf_op jit(solution)/shard_map/ppermute | solution.py:31
  20.7 1.5 %collective-permute-start.5 = (bf16[1152,128]{1,0:T(8,128)(2,1)S(1)}, bf16[1152,128]{1,0:T(8,128)(2,1)S(1)}, u32[]{:S(2)}, u32[]{:S(2)}) collective-permute-start(bf16[1152,128]{1,0:T(8,128)(2,1)S(1)} %get-tuple-element.42), channel_id=1, source_target_pairs={{0,3},{1,0},{2,1},{3,2},{4,7},{5,4},{6,5},{7,6},{8,11},{9,8},{10,9... | collective-permute-start | bytes 884744 | tf_op jit(solution)/shard_map/ppermute | solution.py:31
  22.2 1.5 %collective-permute-start.7 = (bf16[384,128]{1,0:T(8,128)(2,1)S(1)}, bf16[384,128]{1,0:T(8,128)(2,1)S(1)}, u32[]{:S(2)}, u32[]{:S(2)}) collective-permute-start(bf16[384,128]{1,0:T(8,128)(2,1)S(1)} %get-tuple-element.44), channel_id=1, source_target_pairs={{0,12},{4,0},{8,4},{12,8},{1,13},{5,1},{9,5},{13,9},{2,14},{6,2},{... | collective-permute-start | bytes 294920 | tf_op jit(solution)/shard_map/ppermute | solution.py:31
  23.7 1.9 %prepare.1 = (bf16[512,128]{1,0:T(8,128)(2,1)S(1)}, bf16[512,128]{1,0:T(8,128)(2,1)S(1)}, bf16[2,4096,256]{2,1,0:T(8,128)(2,1)S(1)}, bf16[2,64,512]{2,1,0:T(8,12...) custom-call(f32[32,2048]{1,0:T(8,128)S(1)} %bitcast.8, ...), custom_call_target="tpu_custom_call" | custom-call | tf_op jit(solution)/shard_map/prepare/pallas_call | solution.py:633
  25.6 0.3 collective-permute-done.6.low_ref
  26.0 0.9 %collective-permute-done.7.high_ref = bf16[384,128]{1,0:T(8,128)(2,1)S(1)} collective-permute-done((bf16[384,128]{1,0:T(8,128)(2,1)S(1)}, bf16[384,128]{1,0:T(8,128)(2,1)S(1)}, u32[]{:S(2)}, u32[]{:S(2)}) %collective-permute-start.7) | collective-permute-done | bytes 98336 | tf_op jit(solution)/shard_map/ppermute | solution.py:31
  26.9 4.3 %reverse_local.1.reverse_ref = f32[8224,128]{1,0:T(8,128)S(1)} custom-call(s32[2048]{0:T(1024)S(1)} %copy-done.5, s32[27,1,32]{2,1,0:T(1,128)S(1)} %get-tuple-element.34.send_ref.send_hbm_ref, bf16[1152,128]{1,0:T(8,128)(2,1)S(1)} %regroup.7.middle_ref, f32[8256,128]{1,0:T(8,128)S(1)} %get-tuple-element.36.wide_ref), custom_call_target="tpu_custom_call" | custom-call | tf_op jit(solution)/shard_map/reverse_local/pallas_call | solution.py:663
  31.3 12.6 %blocks.1 = (f32[2056,128]{1,0:T(8,128)S(1)}, bf16[288,128]{1,0:T(8,128)(2,1)S(1)}, bf16[288,128]{1,0:T(8,128)(2,1)S(1)}) custom-call(s32[27,1,32]{2,1,0:T(1,128)} %copy-done.3, bf16[1152,128]{1,0:T(8,128)(2,1)S(1)} %collective-permute-done.4.low_ref, bf16[1152,128]{1,0:T(8,128)(2,1)S(1)} %collective-permute-done.5.high_ref, ...), custom_call_target="tpu_custom_call" | custom-call | tf_op jit(solution)/shard_map/blocks/pallas_call | solution.py:673
  43.8 4.3 %collective-permute-start.8 = (bf16[288,128]{1,0:T(8,128)(2,1)S(1)}, bf16[288,128]{1,0:T(8,128)(2,1)S(1)}, u32[]{:S(2)}, u32[]{:S(2)}) collective-permute-start(bf16[288,128]{1,0:T(8,128)(2,1)S(1)} %get-tuple-element.52), channel_id=1, source_target_pairs={{0,16},{16,32},{32,48},{48,64},{64,80},{80,96},{96,112},{112,128},... | collective-permute-start | bytes 221192 | tf_op jit(solution)/shard_map/ppermute | solution.py:31
  48.1 1.8 %trip_local.1 = (f32[512,128]{1,0:T(8,128)S(1)}, bf16[288,128]{1,0:T(8,128)(2,1)S(1)}) custom-call(s32[2048]{0:T(1024)S(1)} %copy-done.5, s32[27,1,32]{2,1,0:T(1,128)S(1)} %copy-done.4, f32[2056,128]{1,0:T(8,128)S(1)} %get-tuple-element.53.trip_ref), custom_call_target="tpu_custom_call" | custom-call | tf_op jit(solution)/shard_map/trip_local/pallas_call | solution.py:708
  49.9 3.2 %collective-permute-done.9.high_ref = bf16[288,128]{1,0:T(8,128)(2,1)S(1)} collective-permute-done((bf16[288,128]{1,0:T(8,128)(2,1)S(1)}, bf16[288,128]{1,0:T(8,128)(2,1)S(1)}, u32[]{:S(2)}, u32[]{:S(2)}) %collective-permute-start.9) | collective-permute-done | bytes 73760 | tf_op jit(solution)/shard_map/ppermute | solution.py:31
  53.1 0.1 collective-permute-start.10
  53.2 1.5 %collective-permute-start.11 = (bf16[288,128]{1,0:T(8,128)(2,1)S(1)}, bf16[288,128]{1,0:T(8,128)(2,1)S(1)}, u32[]{:S(2)}, u32[]{:S(2)}) collective-permute-start(bf16[288,128]{1,0:T(8,128)(2,1)S(1)} %get-tuple-element.58), channel_id=1, source_target_pairs={{0,12},{4,0},{8,4},{12,8},{1,13},{5,1},{9,5},{13,9},{2,14},{6,2},{... | collective-permute-start | bytes 221192 | tf_op jit(solution)/shard_map/ppermute | solution.py:31
  54.7 1.7 %collective-permute-done.10.low_ref = bf16[288,128]{1,0:T(8,128)(2,1)S(1)} collective-permute-done((bf16[288,128]{1,0:T(8,128)(2,1)S(1)}, bf16[288,128]{1,0:T(8,128)(2,1)S(1)}, u32[]{:S(2)}, u32[]{:S(2)}) %collective-permute-start.10) | collective-permute-done | bytes 73760 | tf_op jit(solution)/shard_map/ppermute | solution.py:31
  56.4 1.3 %collective-permute-done.11.high_ref = bf16[288,128]{1,0:T(8,128)(2,1)S(1)} collective-permute-done((bf16[288,128]{1,0:T(8,128)(2,1)S(1)}, bf16[288,128]{1,0:T(8,128)(2,1)S(1)}, u32[]{:S(2)}, u32[]{:S(2)}) %collective-permute-start.11) | collective-permute-done | bytes 73760 | tf_op jit(solution)/shard_map/ppermute | solution.py:31
  57.7 0.2 collective-permute-start.12
  57.9 2.6 %collective-permute-start.13 = (bf16[288,128]{1,0:T(8,128)(2,1)S(1)}, bf16[288,128]{1,0:T(8,128)(2,1)S(1)}, u32[]{:S(2)}, u32[]{:S(2)}) collective-permute-start(bf16[288,128]{1,0:T(8,128)(2,1)S(1)} %get-tuple-element.60), channel_id=1, source_target_pairs={{0,3},{1,0},{2,1},{3,2},{4,7},{5,4},{6,5},{7,6},{8,11},{9,8},{10,9... | collective-permute-start | bytes 221192 | tf_op jit(solution)/shard_map/ppermute | solution.py:31
  60.5 1.9 %trip_rest.1.begun_ref = f32[1536,128]{1,0:T(8,128)S(1)} custom-call(s32[2048]{0:T(1024)S(1)} %copy-done.5, f32[2056,128]{1,0:T(8,128)S(1)} %get-tuple-element.53.trip_ref, f32[512,128]{1,0:T(8,128)S(1)} %get-tuple-element.62.begun_ref), custom_call_target="tpu_custom_call" | custom-call | tf_op jit(solution)/shard_map/trip_rest/pallas_call | solution.py:721
  62.4 1.8 %trip_middle.1.trip_ref = f32[2056,128]{1,0:T(8,128)S(1)} custom-call(s32[2048]{0:T(1024)S(1)} %copy-done.5, s32[27,1,32]{2,1,0:T(1,128)S(1)} %copy-done.4, bf16[288,128]{1,0:T(8,128)(2,1)S(1)} %get-tuple-element.61.middle_ref, f32[2056,128]{1,0:T(8,128)S(1)} %get-tuple-element.53.trip_ref, f32[1536,128]{1,0:T(8,128)S(1)} %trip_rest.1.begun_ref), custom_call_target="tpu_custom_call" | custom-call | tf_op jit(solution)/shard_map/trip_middle/pallas_call | solution.py:729
  64.2 9.4 %final.1 = bf16[2048,512]{1,0:T(8,128)(2,1)} custom-call(s32[27,1,32]{2,1,0:T(1,128)} %copy-done.3, bf16[288,128]{1,0:T(8,128)(2,1)S(1)} %collective-permute-done.12.low_ref, bf16[288,128]{1,0:T(8,128)(2,1)S(1)} %collective-permute-done.13.high_ref, f32[2056,128]{1,0:T(8,128)S(1)} %trip_middle.1.trip_ref, bf16[2048,512]{1,0:T(8,128)(2,1)S(1)} %copy-done, ...), custom_call_target="tpu_custom_call" | custom-call | tf_op jit(solution)/shard_map/final/pallas_call | solution.py:739
  (34 shorter events, 0.2 us)
Async XLA Ops:
  0.0 5.8 %copy-start.11 = (s32[1,1,1,27,32]{4,2,3,1,0:T(1,128)S(1)}, s32[1,1,1,27,32]{4,2,3,1,0:T(1,128)}, u32[]{:S(2)}) copy-start(s32[1,1,1,27,32]{4,2,3,1,0:T(1,128)} %param.13) | copy-start | bytes 10372
  2.4 7.1 %collective-permute-start = (bf16[1152,128]{1,0:T(8,128)(2,1)S(1)}, bf16[1152,128]{1,0:T(8,128)(2,1)S(1)}, u32[]{:S(2)}, u32[]{:S(2)}) collective-permute-start(bf16[1152,128]{1,0:T(8,128)(2,1)S(1)} %get-tuple-element.35), channel_id=1, source_target_pairs={{0,16},{16,32},{32,48},{48,64},{64,80},{80,96},{96,112},{112,128},... | collective-permute-start | bytes 884744 | tf_op jit(solution)/shard_map/ppermute | solution.py:31
  5.8 7.4 %collective-permute-start.1 = (bf16[1152,128]{1,0:T(8,128)(2,1)S(1)}, bf16[1152,128]{1,0:T(8,128)(2,1)S(1)}, u32[]{:S(2)}, u32[]{:S(2)}) collective-permute-start(bf16[1152,128]{1,0:T(8,128)(2,1)S(1)} %get-tuple-element.37), channel_id=1, source_target_pairs={{0,240},{16,0},{32,16},{48,32},{64,48},{80,64},{96,80},{112,96},{1... | collective-permute-start | bytes 884744 | tf_op jit(solution)/shard_map/ppermute | solution.py:31
  5.8 17.8 %copy-start.1 = (bf16[2,512,512]{2,1,0:T(8,128)(2,1)S(1)}, bf16[2,512,512]{2,1,0:T(8,128)(2,1)}, u32[]{:S(2)}) copy-start(bf16[2,512,512]{2,1,0:T(8,128)(2,1)} %first_ref.1) | copy-start | bytes 3145732
  5.8 17.8 %copy-start.2 = (bf16[2,512,512]{2,1,0:T(8,128)(2,1)S(1)}, bf16[2,512,512]{2,1,0:T(8,128)(2,1)}, u32[]{:S(2)}) copy-start(bf16[2,512,512]{2,1,0:T(8,128)(2,1)} %second_ref.1) | copy-start | bytes 3145732
  5.8 17.8 %copy-start.5 = (s32[2048]{0:T(1024)S(1)}, s32[2048]{0:T(1024)}, u32[]{:S(2)}) copy-start(s32[2048]{0:T(1024)} %fetch_ref.7) | copy-start | bytes 24580
  5.9 17.8 %copy-start.6 = (f32[2048,32]{0,1:T(8,128)S(1)}, f32[2048,32]{0,1:T(8,128)}, u32[]{:S(2)}) copy-start(f32[2048,32]{0,1:T(8,128)} %param.11) | copy-start | bytes 786436
  5.9 17.8 %copy-start.7 = (s32[2048,32]{0,1:T(8,128)S(1)}, s32[2048,32]{0,1:T(8,128)}, u32[]{:S(2)}) copy-start(s32[2048,32]{0,1:T(8,128)} %param.12) | copy-start | bytes 786436
  5.9 17.8 %copy-start.8 = (bf16[2,1024,64]{1,2,0:T(8,128)(2,1)S(1)}, bf16[2,1024,64]{1,2,0:T(8,128)(2,1)}, u32[]{:S(2)}) copy-start(bf16[2,1024,64]{1,2,0:T(8,128)(2,1)} %param.16) | copy-start | bytes 786436
  5.9 17.8 %copy-start.9 = (bf16[2,64,512]{2,1,0:T(8,128)(2,1)S(1)}, bf16[2,64,512]{2,1,0:T(8,128)(2,1)}, u32[]{:S(2)}) copy-start(bf16[2,64,512]{2,1,0:T(8,128)(2,1)} %up_ref.1) | copy-start | bytes 393220
  5.9 17.8 %copy-start.10 = (bf16[2,512,64]{1,2,0:T(8,128)(2,1)S(1)}, bf16[2,512,64]{1,2,0:T(8,128)(2,1)}, u32[]{:S(2)}) copy-start(bf16[2,512,64]{1,2,0:T(8,128)(2,1)} %param.15) | copy-start | bytes 393220
  13.3 4.6 %collective-permute-start.2 = (bf16[768,128]{1,0:T(8,128)(2,1)S(1)}, bf16[768,128]{1,0:T(8,128)(2,1)S(1)}, u32[]{:S(2)}, u32[]{:S(2)}) collective-permute-start(bf16[768,128]{1,0:T(8,128)(2,1)S(1)} %get-tuple-element.38), channel_id=1, source_target_pairs={{0,4},{4,8},{8,12},{12,0},{1,5},{5,9},{9,13},{13,1},{2,6},{6,10},{... | collective-permute-start | bytes 589832 | tf_op jit(solution)/shard_map/ppermute | solution.py:31
  13.5 5.7 %collective-permute-start.3 = (bf16[768,128]{1,0:T(8,128)(2,1)S(1)}, bf16[768,128]{1,0:T(8,128)(2,1)S(1)}, u32[]{:S(2)}, u32[]{:S(2)}) collective-permute-start(bf16[768,128]{1,0:T(8,128)(2,1)S(1)} %get-tuple-element.40), channel_id=1, source_target_pairs={{0,12},{4,0},{8,4},{12,8},{1,13},{5,1},{9,5},{13,9},{2,14},{6,2},{... | collective-permute-start | bytes 589832 | tf_op jit(solution)/shard_map/ppermute | solution.py:31
  19.3 11.9 %collective-permute-start.4 = (bf16[1152,128]{1,0:T(8,128)(2,1)S(1)}, bf16[1152,128]{1,0:T(8,128)(2,1)S(1)}, u32[]{:S(2)}, u32[]{:S(2)}) collective-permute-start(bf16[1152,128]{1,0:T(8,128)(2,1)S(1)} %get-tuple-element.41), channel_id=1, source_target_pairs={{0,1},{1,2},{2,3},{3,0},{4,5},{5,6},{6,7},{7,4},{8,9},{9,10},{10,1... | collective-permute-start | bytes 884744 | tf_op jit(solution)/shard_map/ppermute | solution.py:31
  20.7 10.6 %collective-permute-start.5 = (bf16[1152,128]{1,0:T(8,128)(2,1)S(1)}, bf16[1152,128]{1,0:T(8,128)(2,1)S(1)}, u32[]{:S(2)}, u32[]{:S(2)}) collective-permute-start(bf16[1152,128]{1,0:T(8,128)(2,1)S(1)} %get-tuple-element.42), channel_id=1, source_target_pairs={{0,3},{1,0},{2,1},{3,2},{4,7},{5,4},{6,5},{7,6},{8,11},{9,8},{10,9... | collective-permute-start | bytes 884744 | tf_op jit(solution)/shard_map/ppermute | solution.py:31
  22.2 3.8 %collective-permute-start.6 = (bf16[384,128]{1,0:T(8,128)(2,1)S(1)}, bf16[384,128]{1,0:T(8,128)(2,1)S(1)}, u32[]{:S(2)}, u32[]{:S(2)}) collective-permute-start(bf16[384,128]{1,0:T(8,128)(2,1)S(1)} %get-tuple-element.43), channel_id=1, source_target_pairs={{0,4},{4,8},{8,12},{12,0},{1,5},{5,9},{9,13},{13,1},{2,6},{6,10},{... | collective-permute-start | bytes 294920 | tf_op jit(solution)/shard_map/ppermute | solution.py:31
  22.2 4.7 %collective-permute-start.7 = (bf16[384,128]{1,0:T(8,128)(2,1)S(1)}, bf16[384,128]{1,0:T(8,128)(2,1)S(1)}, u32[]{:S(2)}, u32[]{:S(2)}) collective-permute-start(bf16[384,128]{1,0:T(8,128)(2,1)S(1)} %get-tuple-element.44), channel_id=1, source_target_pairs={{0,12},{4,0},{8,4},{12,8},{1,13},{5,1},{9,5},{13,9},{2,14},{6,2},{... | collective-permute-start | bytes 294920 | tf_op jit(solution)/shard_map/ppermute | solution.py:31
  25.6 5.6 %copy-start.3 = (s32[27,1,32]{2,1,0:T(1,128)}, s32[27,1,32]{2,1,0:T(1,128)S(1)}, u32[]{:S(2)}) copy-start(s32[27,1,32]{2,1,0:T(1,128)S(1)} %get-tuple-element.34.send_ref.send_hbm_ref) | copy-start | bytes 10372
  31.2 16.9 %copy-start.4 = (s32[27,1,32]{2,1,0:T(1,128)S(1)}, s32[27,1,32]{2,1,0:T(1,128)}, u32[]{:S(2)}) copy-start(s32[27,1,32]{2,1,0:T(1,128)} %copy-done.3) | copy-start | bytes 10372
  43.8 6.0 %collective-permute-start.8 = (bf16[288,128]{1,0:T(8,128)(2,1)S(1)}, bf16[288,128]{1,0:T(8,128)(2,1)S(1)}, u32[]{:S(2)}, u32[]{:S(2)}) collective-permute-start(bf16[288,128]{1,0:T(8,128)(2,1)S(1)} %get-tuple-element.52), channel_id=1, source_target_pairs={{0,16},{16,32},{32,48},{48,64},{64,80},{80,96},{96,112},{112,128},... | collective-permute-start | bytes 221192 | tf_op jit(solution)/shard_map/ppermute | solution.py:31
  48.1 5.0 %collective-permute-start.9 = (bf16[288,128]{1,0:T(8,128)(2,1)S(1)}, bf16[288,128]{1,0:T(8,128)(2,1)S(1)}, u32[]{:S(2)}, u32[]{:S(2)}) collective-permute-start(bf16[288,128]{1,0:T(8,128)(2,1)S(1)} %get-tuple-element.55), channel_id=1, source_target_pairs={{0,240},{16,0},{32,16},{48,32},{64,48},{80,64},{96,80},{112,96},{1... | collective-permute-start | bytes 221192 | tf_op jit(solution)/shard_map/ppermute | solution.py:31
  53.1 3.3 %collective-permute-start.10 = (bf16[288,128]{1,0:T(8,128)(2,1)S(1)}, bf16[288,128]{1,0:T(8,128)(2,1)S(1)}, u32[]{:S(2)}, u32[]{:S(2)}) collective-permute-start(bf16[288,128]{1,0:T(8,128)(2,1)S(1)} %get-tuple-element.56), channel_id=1, source_target_pairs={{0,4},{4,8},{8,12},{12,0},{1,5},{5,9},{9,13},{13,1},{2,6},{6,10},{... | collective-permute-start | bytes 221192 | tf_op jit(solution)/shard_map/ppermute | solution.py:31
  53.2 4.5 %collective-permute-start.11 = (bf16[288,128]{1,0:T(8,128)(2,1)S(1)}, bf16[288,128]{1,0:T(8,128)(2,1)S(1)}, u32[]{:S(2)}, u32[]{:S(2)}) collective-permute-start(bf16[288,128]{1,0:T(8,128)(2,1)S(1)} %get-tuple-element.58), channel_id=1, source_target_pairs={{0,12},{4,0},{8,4},{12,8},{1,13},{5,1},{9,5},{13,9},{2,14},{6,2},{... | collective-permute-start | bytes 221192 | tf_op jit(solution)/shard_map/ppermute | solution.py:31
  57.7 6.5 %collective-permute-start.12 = (bf16[288,128]{1,0:T(8,128)(2,1)S(1)}, bf16[288,128]{1,0:T(8,128)(2,1)S(1)}, u32[]{:S(2)}, u32[]{:S(2)}) collective-permute-start(bf16[288,128]{1,0:T(8,128)(2,1)S(1)} %get-tuple-element.59), channel_id=1, source_target_pairs={{0,1},{1,2},{2,3},{3,0},{4,5},{5,6},{6,7},{7,4},{8,9},{9,10},{10,1... | collective-permute-start | bytes 221192 | tf_op jit(solution)/shard_map/ppermute | solution.py:31
  57.9 6.3 %collective-permute-start.13 = (bf16[288,128]{1,0:T(8,128)(2,1)S(1)}, bf16[288,128]{1,0:T(8,128)(2,1)S(1)}, u32[]{:S(2)}, u32[]{:S(2)}) collective-permute-start(bf16[288,128]{1,0:T(8,128)(2,1)S(1)} %get-tuple-element.60), channel_id=1, source_target_pairs={{0,3},{1,0},{2,1},{3,2},{4,7},{5,4},{6,5},{7,6},{8,11},{9,8},{10,9... | collective-permute-start | bytes 221192 | tf_op jit(solution)/shard_map/ppermute | solution.py:31
  60.5 3.7 %copy-start = (bf16[2048,512]{1,0:T(8,128)(2,1)S(1)}, bf16[2048,512]{1,0:T(8,128)(2,1)}, u32[]{:S(2)}) copy-start(bf16[2048,512]{1,0:T(8,128)(2,1)} %rows_ref.1) | copy-start | bytes 6291460
